TPU v7x, 32 devices: a whole 2x2x4 slice. The times are simulated.
32 devices in a mesh: seq: 16 (over z, y, core), head: 2 (over x).
Axes of the slice: x: 2, y: 2, z: 4, core: 2. Of those that a mesh axis runs over, the one named last changes fastest.
Arguments:
- queries: bfloat16 [2048, 2048], P('seq', 'head'), may hold values from -190 to 190
- key_vectors: bfloat16 [2048, 256], P('seq', 'head'), may hold values from -6.1 to 6.1
- value_vectors: bfloat16 [2048, 256], P('seq', 'head'), may hold values from -54 to 54
- log_gate: float32 [16, 2048], P('head', 'seq'), may hold values from -1 to 0, as said below
- query_map: float32 [16, 128, 128], P('head'), may hold values from -0.5 to 0.5
- key_map: float32 [16, 128, 128], P('head'), may hold values from -0.5 to 0.5
- level_weight: float32 [16, 12], P('head'), may hold values from 0.25 to 2
- norm_gain: float32 [2048], P('head'), may hold values from 0.5 to 1.5
Outputs:
- grad_query_map: float32 [16, 128, 128], P('head')
- grad_key_map: float32 [16, 128, 128], P('head')
- grad_level_weight: float32 [16, 12], P('head')
- grad_norm_gain: float32 [2048], P('head')
Inputs may be any that keep to these rules, and one draw needn't show every extreme that they name: `log_gate`: every entry is negative.
All inputs are finite; a program needn't handle non-finite values.
Results may differ from a plain program's by a relative error of at most 0.0015.
Values may be sent and summed in bfloat16 or wider, within the bound.
No kernel may reach another device: no remote copies, remote signals or barrier semaphores. Data moves between devices by JAX's collectives and lax.ppermute only.
A program may use at most 128 MiB of HBM per device.

v0:
```python
import functools

import jax
import jax.numpy as jnp
from jax import lax
from jax.experimental import pallas as pl
from jax.experimental.pallas import tpu as pltpu
from jax.sharding import PartitionSpec as P


HIGHEST = lax.Precision.HIGHEST
NEGATIVE = -1e30
EPSILON = 1e-05
F32 = jnp.float32
BF16 = jnp.bfloat16
NN = (((1,), (0,)), ((), ()))
NT = (((1,), (1,)), ((), ()))
TN = (((0,), (0,)), ((), ()))
GATE_ROWS = 32
PARTS = 2


def dot(a, b, dims=NN):
    return lax.dot_general(a, b, dims, preferred_element_type=F32)


def exact_dot(a, b, dims=NN):
    return lax.dot_general(a, b, dims, precision=HIGHEST, preferred_element_type=F32)


def halves(x):
    high = x.astype(BF16)
    return high, (x - high.astype(F32)).astype(BF16)


def dot_f32(a, b, dims=NN):
    lhs = jnp.concatenate([a[0], a[0], a[1]], axis=dims[0][0][0])
    rhs = jnp.concatenate([b[0], b[1], b[0]], axis=dims[0][1][0])
    return dot(lhs, rhs, dims)


def dot_left(a, b, dims=NN):
    lhs = jnp.concatenate([a[0], a[1]], axis=dims[0][0][0])
    rhs = jnp.concatenate([b, b], axis=dims[0][1][0])
    return dot(lhs, rhs, dims)


def dot_right(a, b, dims=NN):
    lhs = jnp.concatenate([a, a], axis=dims[0][0][0])
    rhs = jnp.concatenate([b[0], b[1]], axis=dims[0][1][0])
    return dot(lhs, rhs, dims)


def iota2(shape, axis):
    return lax.broadcasted_iota(jnp.int32, shape, axis)


def upper_ones(size):
    return (iota2((size, size), 0) <= iota2((size, size), 1)).astype(F32)


def fetch(sems, *pairs):
    copies = [pltpu.make_async_copy(src, dst, sems.at[i]) for i, (src, dst) in enumerate(pairs)]
    for copy in copies:
        copy.start()
    for copy in copies:
        copy.wait()


def pack_kernel(k_hbm, v_hbm, gate_hbm, out_ref, k_ref, v_ref, gate_ref, sems):
    fetch(sems, (k_hbm, k_ref), (v_hbm, v_ref), (gate_hbm, gate_ref))
    rows = k_ref.shape[0]
    heads = gate_ref.shape[0]
    out_ref[0:rows, :] = k_ref[...].astype(F32).T.astype(BF16)
    out_ref[rows : 2 * rows, :] = v_ref[...]
    gate = gate_ref[...]
    high = gate.astype(BF16).astype(F32)
    middle = (gate - high).astype(BF16).astype(F32)
    low = gate - high - middle
    blank = jnp.zeros((GATE_ROWS - 3 * heads, gate.shape[1]), F32)
    out_ref[2 * rows :, :] = jnp.concatenate([high, middle, low, blank], axis=0).astype(BF16)


def local_kernel(
    packed_ref, level_hbm, q_hbm, qmap_hbm, kmap_hbm, qp_ref, qt_ref, sd_ref, mix_ref, loc_ref,
    q_ref, qmap_ref, kmap_ref, level_ref, sems,
):
    fetch(sems, (q_hbm, q_ref), (qmap_hbm, qmap_ref), (kmap_hbm, kmap_ref), (level_hbm, level_ref))
    heads, dim, _ = qmap_ref.shape
    width, rows = packed_ref.shape
    low_bits = rows.bit_length() - 1
    piece = packed_ref[width - GATE_ROWS :, :].astype(F32)
    gate = piece[0:heads] + piece[heads : 2 * heads] + piece[2 * heads : 3 * heads]
    cum = exact_dot(gate, upper_ones(rows))
    cum_t = cum.T
    kt = packed_ref[0:rows, :]
    v = packed_ref[rows : 2 * rows, :]
    row, col = iota2((rows, rows), 0), iota2((rows, rows), 1)
    causal = col <= row
    differ = row ^ col
    highs, lows = [], []
    for h in range(heads):
        qp = dot_right(q_ref[:, h * dim : (h + 1) * dim], halves(qmap_ref[h]))
        qp_ref[h] = qp
        qt = dot_f32(halves(qp), halves(kmap_ref[h]), NT)
        qt_ref[h] = qt
        high, low = halves(qt)
        highs.append(high)
        lows.append(low)
    score = dot_left((jnp.concatenate(highs, axis=0), jnp.concatenate(lows, axis=0)), kt)
    highs, lows = [], []
    for h in range(heads):
        decay = jnp.exp(jnp.where(causal, cum_t[:, h : h + 1] - cum[h : h + 1, :], NEGATIVE))
        weight = jnp.full((rows, rows), level_ref[h, 0], F32)
        for level in range(1, low_bits + 1):
            weight = jnp.where(differ >= (1 << (level - 1)), level_ref[h, level], weight)
        decayed = score[h * rows : (h + 1) * rows] * decay
        mix_ref[h] = decay * weight
        sd_ref[h] = decayed
        high, low = halves(decayed * weight)
        highs.append(high)
        lows.append(low)
    loc = dot_left((jnp.concatenate(highs, axis=0), jnp.concatenate(lows, axis=0)), v)
    for h in range(heads):
        loc_ref[h] = loc[h * rows : (h + 1) * rows]


def stacked_queries(q_ref, dim):
    return jnp.concatenate([q_ref[:, at : at + dim] for at in range(0, q_ref.shape[1], dim)], axis=0)


def pair_decay(span, even_ref, odd_ref, heads):
    pairs, width, rows = even_ref.shape
    gates = []
    for ref in (even_ref, odd_ref):
        for p in range(pairs):
            piece = ref[p, width - GATE_ROWS :, :].astype(F32)
            gates.append(piece[0:heads] + piece[heads : 2 * heads] + piece[2 * heads : 3 * heads])
    cum = exact_dot(jnp.concatenate(gates, axis=0), upper_ones(rows))
    cum_e, cum_o = cum[: pairs * heads], cum[pairs * heads :]
    end_e = jnp.broadcast_to(cum_e[:, rows - 1 : rows], cum_e.shape)
    end_o = jnp.broadcast_to(cum_o[:, rows - 1 : rows], cum_o.shape)
    odd_span = (span & 1) == 1
    decay_e = jnp.exp(end_e - cum_e + jnp.where(odd_span, 0.0, end_o))
    decay_o = jnp.exp(end_o - cum_o + jnp.where(odd_span, end_e, 0.0))
    return cum_e, cum_o, end_e, end_o, decay_e, decay_o


def pair_blocks(even_ref, odd_ref, p, rows):
    kt = jnp.concatenate([even_ref[p, 0:rows, :], odd_ref[p, 0:rows, :]], axis=1)
    v = jnp.concatenate([even_ref[p, rows : 2 * rows, :], odd_ref[p, rows : 2 * rows, :]], axis=0)
    return kt, v


def pair_state(kt, v, weight, state_ref, p):
    heads = weight.shape[0]
    dim = kt.shape[0]
    kt32 = kt.astype(F32)
    highs, lows = [], []
    for h in range(heads):
        high, low = halves(kt32 * weight[h : h + 1, :])
        highs.append(high)
        lows.append(low)
    state = dot_left((jnp.concatenate(highs, axis=0), jnp.concatenate(lows, axis=0)), v)
    for h in range(heads):
        state_ref[p, h] = state[h * dim : (h + 1) * dim]


def early_kernel(
    span_ref, q_ref, even_ref, odd_ref, score_ref, peak_ref, state_ref, ends_ref, before_ref, decay_scr, *, offsets,
):
    pairs, heads, dim, _ = state_ref.shape
    rows = even_ref.shape[2]
    span = span_ref[0]
    _, cum_o, end_e, end_o, decay_e, decay_o = pair_decay(span, even_ref, odd_ref, heads)
    ends_ref[...] = end_e + end_o
    before_ref[...] = end_o[0:heads]
    for p in range(pairs):
        at = slice(p * heads, (p + 1) * heads)
        if p == 0:
            first = jnp.concatenate([jnp.zeros_like(decay_e[at]), jnp.exp(end_o[at] - cum_o[at])], axis=1)
            decay_scr[p] = first
        else:
            decay_scr[p] = jnp.concatenate([decay_e[at], decay_o[at]], axis=1)
    q_all = stacked_queries(q_ref, dim)
    scale = dim ** (-0.5)
    row, col = iota2((rows, 2 * rows), 0), iota2((rows, 2 * rows), 1)
    odd_span = (span & 1) == 1
    seen = (col <= row) | ((col >= rows) & odd_span)
    kt, v = pair_blocks(even_ref, odd_ref, 0, rows)
    score = dot(q_all, kt) * scale
    score = jnp.where(jnp.concatenate([seen] * heads, axis=0), score, NEGATIVE)
    score_ref[0] = score
    peak_ref[...] = jnp.maximum(score[:, :rows], score[:, rows:])

    @pl.when(odd_span)
    def _():
        pair_state(kt, v, decay_scr[0], state_ref, 0)

    for p in range(1, pairs):

        @pl.when((span ^ offsets[p]) < span)
        def _(p=p):
            kt, v = pair_blocks(even_ref, odd_ref, p, rows)
            score = dot(q_all, kt) * scale
            score_ref[p] = score
            peak_ref[...] = jnp.maximum(peak_ref[...], jnp.maximum(score[:, :rows], score[:, rows:]))
            pair_state(kt, v, decay_scr[p], state_ref, p)


def forward_kernel(
    span_ref, level_ref, q_ref, even_a_ref, odd_a_ref, even_b_ref, odd_b_ref, score_a_ref, peak_a_ref, state_a_ref,
    ends_a_ref, before_ref, qt_ref, loc_ref, gain_ref, gate_ref,
    raw_ref, target_ref, level_state_ref, comb_ref, sums_ref,
    score_scr, peak_scr, state_scr, total_scr, acc_scr, *, offsets,
):
    heads, rows, dim = qt_ref.shape
    early, late = even_a_ref.shape[0], even_b_ref.shape[0]
    pairs = early + late
    span_bits = level_state_ref.shape[0]
    low_bits = rows.bit_length() - 1
    span = span_ref[0]
    odd_span = (span & 1) == 1
    scale = dim ** (-0.5)
    q_all = stacked_queries(q_ref, dim)
    _, _, end_e, end_o, decay_e, decay_o = pair_decay(span, even_b_ref, odd_b_ref, heads)
    peak_scr[...] = peak_a_ref[...]
    for p in range(late):

        @pl.when((span ^ offsets[early + p]) < span)
        def _(p=p):
            at = slice(p * heads, (p + 1) * heads)
            kt, v = pair_blocks(even_b_ref, odd_b_ref, p, rows)
            score = dot(q_all, kt) * scale
            score_scr[p] = score
            peak_scr[...] = jnp.maximum(peak_scr[...], jnp.maximum(score[:, :rows], score[:, rows:]))
            pair_state(kt, v, jnp.concatenate([decay_e[at], decay_o[at]], axis=1), state_scr, p)

    ends = jnp.concatenate([ends_a_ref[...], end_e + end_o], axis=0)
    size = pairs * heads

    def pair_of(index):
        position = index // heads
        offset = position * 0
        for p in range(pairs):
            offset = jnp.where(position == p, offsets[p], offset)
        return (span ^ offset) >> 1, index % heads

    mine, my_head = pair_of(iota2((size, size), 0))
    other, other_head = pair_of(iota2((size, size), 1))
    between = (other > mine) & (other < (span >> 1)) & (my_head == other_head)
    carried = exact_dot(between.astype(F32), ends)
    before = jnp.where(odd_span, before_ref[...], 0.0)
    factor = jnp.exp(carried + jnp.concatenate([before] * pairs, axis=0))

    peak = jnp.max(peak_scr[...], axis=1, keepdims=True)
    peak_scr[...] = jnp.broadcast_to(peak, peak_scr.shape)

    def weigh(score, v):
        top = peak_scr[...]
        left = jnp.exp(score[:, :rows] - top)
        right = jnp.exp(score[:, rows:] - top)
        total = left + right
        return total, dot(jnp.concatenate([left.astype(BF16), right.astype(BF16)], axis=1), v)

    total_scr[...], acc_scr[...] = weigh(score_a_ref[0], pair_blocks(even_a_ref, odd_a_ref, 0, rows)[1])
    for p in range(1, pairs):

        @pl.when((span ^ offsets[p]) < span)
        def _(p=p):
            if p < early:
                total, acc = weigh(score_a_ref[p], pair_blocks(even_a_ref, odd_a_ref, p, rows)[1])
            else:
                q = p - early
                total, acc = weigh(score_scr[q], pair_blocks(even_b_ref, odd_b_ref, q, rows)[1])
            total_scr[...] += total
            acc_scr[...] += acc

    for level in range(span_bits):
        members = [p for p in range(pairs) if max(offsets[p], 1).bit_length() - 1 == level]
        used = ((span >> level) & 1) == 1

        @pl.when(used)
        def _(members=members, level=level):
            for h in range(heads):
                value = None
                for p in members:
                    state = state_a_ref[p, h] if p < early else state_scr[p - early, h]
                    if p > 0:
                        state = state * factor[p * heads + h : p * heads + h + 1, :]
                    value = state if value is None else value + state
                level_state_ref[level, h] = value

        @pl.when(jnp.logical_not(used))
        def _(level=level):
            level_state_ref[level] = jnp.zeros_like(level_state_ref[level])

    total = jnp.sum(total_scr[...], axis=1, keepdims=True)
    target_all = acc_scr[...] / total
    entry = jnp.exp(exact_dot(gate_ref[...], upper_ones(rows)).T)
    squares = jnp.zeros((rows, dim), F32)
    gained = jnp.zeros((rows, dim), F32)
    crossed = jnp.zeros((rows, dim), F32)
    for h in range(heads):
        combined = jnp.zeros((dim, dim), F32)
        for level in range(span_bits):
            combined = combined + level_ref[h, low_bits + 1 + level] * level_state_ref[level, h]
        comb_ref[h] = combined
        far = entry[:, h : h + 1] * dot_f32(halves(qt_ref[h]), halves(combined))
        raw = loc_ref[h] + far
        target = target_all[h * rows : (h + 1) * rows]
        raw_ref[h] = raw
        target_ref[h] = target
        gain = gain_ref[h : h + 1, :]
        square = raw * raw
        squares = squares + square
        gained = gained + square * (gain * gain)
        crossed = crossed + target * raw * gain
    lanes = iota2((rows, rows), 1)
    columns = jnp.where(
        lanes == 0,
        jnp.sum(squares, axis=1, keepdims=True),
        jnp.where(
            lanes == 1,
            jnp.sum(gained, axis=1, keepdims=True),
            jnp.where(lanes == 2, jnp.sum(crossed, axis=1, keepdims=True), 0.0),
        ),
    )
    sums_ref[...] = columns.T[0:8]


def chunk_of(head, heads, span, splits):
    group = heads >> len(splits)
    chunk = 0
    for place, stride in enumerate(splits):
        shift = len(splits) - 1 - place
        bit = (head // group >> shift) & 1
        chunk = chunk + ((bit ^ ((span // stride) & 1)) << shift)
    return chunk * group + head % group


def backward_kernel(
    span_ref, sums_a_ref, sums_b_ref, gate_ref, q_ref, k_ref, v_ref, kmap_ref, gain_ref,
    qp_ref, qt_ref, sd_ref, mix_ref, raw_ref, target_ref, state_ref, comb_ref,
    keep_ref, send_ref, *, norm_width, total_tokens, splits, heads,
):
    _, rows, dim = qt_ref.shape
    share = len(heads)
    span_bits = state_ref.shape[0]
    low_bits = rows.bit_length() - 1
    span = span_ref[0]
    first = (span & 1) == 0
    sums = (sums_a_ref[...] + sums_b_ref[...]).T
    squares, gained, crossed = sums[:, 0:1], sums[:, 1:2], sums[:, 2:3]
    inverse = lax.rsqrt(squares / norm_width + EPSILON)
    inner = (inverse * gained - crossed) / total_tokens
    shrink = inverse * inverse * inverse * inner / norm_width
    entry = jnp.exp(exact_dot(gate_ref[...], upper_ones(rows)).T)
    k = k_ref[...]
    v = v_ref[...]
    row, col = iota2((rows, rows), 0), iota2((rows, rows), 1)
    differ = row ^ col
    levels = low_bits + 1 + span_bits
    pad = 16
    gain_rows, residuals, highs, lows = [], [], [], []
    for h in heads:
        gain = gain_ref[h : h + 1, :]
        raw = raw_ref[h]
        normed = raw * inverse
        mismatch = (normed * gain - target_ref[h]) / total_tokens
        gain_rows.append(jnp.sum(mismatch * normed, axis=0, keepdims=True))
        residual = inverse * (mismatch * gain) - raw * shrink
        residuals.append(residual)
        high, low = halves(residual)
        highs.append(high)
        lows.append(low)
    d_mix = dot_left((jnp.concatenate(highs, axis=0), jnp.concatenate(lows, axis=0)), v, NT)
    level_rows, highs, lows = [], [], []
    for i, h in enumerate(heads):
        d_mix_h = d_mix[i * rows : (i + 1) * rows]
        high, low = halves(d_mix_h * mix_ref[h])
        highs.append(high)
        lows.append(low)
        through = d_mix_h * sd_ref[h]
        mine = []
        for level in range(low_bits + 1):
            least = 0 if level == 0 else 1 << (level - 1)
            here = (differ >= least) & (differ < (1 << level))
            mine.append(jnp.sum(jnp.where(here, through, 0.0), axis=0, keepdims=True))
        level_rows.append(mine)
    d_local = dot_left((jnp.concatenate(highs, axis=0), jnp.concatenate(lows, axis=0)), k)
    for i, h in enumerate(heads):
        lead = halves(entry[:, h : h + 1] * residuals[i])
        d_qt = halves(d_local[i * rows : (i + 1) * rows] + dot_f32(lead, halves(comb_ref[h]), NT))
        grad_k = dot_f32(d_qt, halves(qp_ref[h]), TN)
        d_qp = dot_f32(d_qt, halves(kmap_ref[h]))
        grad_q = dot_right(q_ref[:, h * dim : (h + 1) * dim], halves(d_qp), TN)
        d_comb = dot_f32(halves(qt_ref[h]), lead, TN)
        for level in range(span_bits):
            level_rows[i].append(jnp.sum(state_ref[level, h] * d_comb, axis=0, keepdims=True))
        level_rows[i].append(jnp.zeros((pad - levels, rows), F32))
        at = pl.ds(pl.multiple_of(chunk_of(i, share, span, splits) * dim, dim), dim)
        keep_ref[at, :] = jnp.where(first, grad_q, grad_k)
        send_ref[at, :] = jnp.where(first, grad_k, grad_q)
    table = jnp.sum(jnp.concatenate([r for mine in level_rows for r in mine], axis=0), axis=1, keepdims=True)
    spread = iota2((share * pad, rows), 0) % pad == iota2((share * pad, rows), 1)
    pick = iota2((share, share * pad), 1) // pad == iota2((share, share * pad), 0)
    level_sums = exact_dot(pick.astype(F32), jnp.where(spread, table, 0.0))
    small = jnp.concatenate(gain_rows + [level_sums], axis=0)
    tail = pl.ds(share * dim, 2 * share)
    keep_ref[tail, :] = small
    send_ref[tail, :] = small


def place_kernel(span_ref, *refs, splits):
    q_ref, k_ref = refs[-2:]
    heads, dim, _ = q_ref.shape
    parts = (len(refs) - 2) // 2
    share = heads // parts
    span = span_ref[0]
    first = (span & 1) == 0
    for h in range(heads):
        mine_ref, other_ref = refs[2 * (h // share) : 2 * (h // share) + 2]
        at = pl.ds(pl.multiple_of(chunk_of(h % share, share, span, splits) * dim, dim), dim)
        mine, other = mine_ref[at, :], other_ref[at, :]
        q_ref[h] = jnp.where(first, mine, other)
        k_ref[h] = jnp.where(first, other, mine)


def vmem(count):
    return [pl.BlockSpec(memory_space=pltpu.VMEM)] * count


def hbm(count):
    return [pl.BlockSpec(memory_space=pltpu.HBM)] * count


def smem(count):
    return [pl.BlockSpec(memory_space=pltpu.SMEM)] * count


def shape(*dims, dtype=F32):
    return jax.ShapeDtypeStruct(dims, dtype)


def call(kernel, ins, outs, limit, flops, scratch=(), **static):
    body = functools.partial(kernel, **static) if static else kernel
    single = not isinstance(outs, (list, tuple))
    return pl.pallas_call(
        body,
        out_shape=outs,
        in_specs=ins,
        out_specs=pl.BlockSpec(memory_space=pltpu.VMEM) if single else vmem(len(outs)),
        scratch_shapes=list(scratch),
        compiler_params=pltpu.CompilerParams(vmem_limit_bytes=limit << 20),
        cost_estimate=pl.CostEstimate(flops=flops, bytes_accessed=1 << 20, transcendentals=0),
    )


def in_hbm(*values):
    return [pltpu.with_memory_space_constraint(value, pltpu.HBM) for value in values]


def swap(value, axis, stride):
    count = lax.axis_size(axis)
    return lax.ppermute(value, axis, [(i, i ^ stride) for i in range(count)])


def on_device(queries, key_vectors, value_vectors, log_gate, query_map, key_map, level_weight, norm_gain):
    rows, dim = key_vectors.shape
    heads = queries.shape[1] // dim
    count = lax.axis_size("seq")
    groups = lax.axis_size("head")
    span_bits = count.bit_length() - 1
    span = lax.axis_index("seq").astype(jnp.int32).reshape(1)
    total_tokens = rows * count
    norm_width = heads * dim * groups
    gain = norm_gain.reshape(heads, dim)
    strides = [1 << bit for bit in reversed(range(1, span_bits))]
    splits = (2, 4)
    cube = (heads, dim, dim)
    packed_rows = 2 * rows + GATE_ROWS

    offsets = [0]
    for stride in strides:
        offsets += [offset + stride for offset in offsets]
    early = len(offsets) // 2

    packed = call(pack_kernel, hbm(3), shape(packed_rows, rows, dtype=BF16), 8, 1 << 20, scratch=[
        pltpu.VMEM((rows, dim), BF16),
        pltpu.VMEM((rows, dim), BF16),
        pltpu.VMEM((heads, rows), F32),
        pltpu.SemaphoreType.DMA((3,)),
    ])(*in_hbm(key_vectors, value_vectors, log_gate))
    qp, qt, score_decay, mix, local = call(
        local_kernel, vmem(1) + hbm(4), [shape(*cube)] * 5, 24, 1 << 29,
        scratch=[
            pltpu.VMEM(queries.shape, BF16),
            pltpu.VMEM(cube, F32),
            pltpu.VMEM(cube, F32),
            pltpu.SMEM(level_weight.shape, F32),
            pltpu.SemaphoreType.DMA((4,)),
        ],
    )(packed, *in_hbm(level_weight, queries, query_map, key_map))

    even_a = packed[None]
    for stride in strides[:-1]:
        received = swap(even_a, "seq", stride)
        even_a = jnp.concatenate([even_a, received], axis=0)
    even_b = swap(even_a, "seq", strides[-1])
    odd_a = swap(even_a, "seq", 1)
    odd_b = swap(even_b, "seq", 1)

    scores, peaks, states, ends, before = call(
        early_kernel,
        smem(1) + vmem(3),
        [
            shape(early, heads * rows, 2 * rows),
            shape(heads * rows, rows),
            shape(early, *cube),
            shape(early * heads, rows),
            shape(heads, rows),
        ],
        24,
        1 << 30,
        scratch=[pltpu.VMEM((early, heads, 2 * rows), F32)],
        offsets=tuple(offsets),
    )(span, queries, even_a, odd_a)
    raw, target, level_states, combined, sums = call(
        forward_kernel,
        smem(2) + vmem(14),
        [shape(*cube), shape(*cube), shape(span_bits, *cube), shape(*cube), shape(8, rows)],
        32,
        1 << 31,
        scratch=[
            pltpu.VMEM((early, heads * rows, 2 * rows), F32),
            pltpu.VMEM((heads * rows, rows), F32),
            pltpu.VMEM((early, *cube), F32),
            pltpu.VMEM((heads * rows, rows), F32),
            pltpu.VMEM((heads * rows, dim), F32),
        ],
        offsets=tuple(offsets),
    )(
        span, level_weight, queries, even_a, odd_a, even_b, odd_b, scores, peaks, states, ends, before,
        qt, local, gain, log_gate,
    )

    stride = 1
    while stride < groups:
        received = swap(sums, "head", stride)
        if 2 * stride < groups:
            sums = sums + received
        stride *= 2

    share = heads // PARTS
    size = share * dim
    held = []
    for part in range(PARTS):
        keep, send = call(
            backward_kernel,
            smem(1) + vmem(16),
            [shape(share * (dim + 2), dim)] * 2,
            24,
            1 << 29,
            norm_width=float(norm_width),
            total_tokens=float(total_tokens),
            splits=splits,
            heads=range(part * share, (part + 1) * share),
        )(
            span, sums, received, log_gate, queries, key_vectors, value_vectors, key_map, gain,
            qp, qt, score_decay, mix, raw, target, level_states, combined,
        )
        held.append(keep + swap(send, "seq", 1))
    for split in splits:
        size //= 2
        for part in range(PARTS):
            here = held[part]
            got = swap(here[size:], "seq", split)
            held[part] = jnp.concatenate([here[:size] + got[:size], here[2 * size :] + got[size:]])
    for stride in strides:
        if stride not in splits:
            for part in range(PARTS):
                held[part] = held[part] + swap(held[part], "seq", stride)
    small = [here[size:] for here in held]
    mine = [here[:size] for here in held]
    for split in reversed(splits):
        for part in range(PARTS):
            mine[part] = jnp.concatenate([mine[part], swap(mine[part], "seq", split)])
    pieces = []
    for part in range(PARTS):
        pieces += [mine[part], swap(mine[part], "seq", 1)]
    grad_query, grad_key = call(
        place_kernel, smem(1) + vmem(2 * PARTS), [shape(*cube)] * 2, 16, 1 << 20, splits=splits
    )(span, *pieces)
    grad_gain = jnp.concatenate([piece[:share] for piece in small]).reshape(-1)
    grad_levels = jnp.concatenate([piece[share:, : level_weight.shape[1]] for piece in small])
    return grad_query, grad_key, grad_levels, grad_gain


def solution(mesh):
    placed = (
        P("seq", "head"),
        P("seq", "head"),
        P("seq", "head"),
        P("head", "seq"),
        P("head", None, None),
        P("head", None, None),
        P("head", None),
        P("head"),
    )

    return jax.shard_map(
        on_device,
        mesh=mesh,
        in_specs=placed,
        out_specs=(P("head", None, None), P("head", None, None), P("head", None), P("head")),
        check_vma=False,
    )
```

profile of v0, /device:TPU:0, one launch (start us, length us, event | category | flops | bytes accessed | tf_op | source)
XLA Modules:
  0.0 76.9 jit_solution(8201246266463196075)
XLA Ops:
  0.6 0.0 copy-start
  0.6 0.9 %shard_map.111.packed_ref = bf16[288,128]{1,0:T(8,128)(2,1)S(1)} custom-call(bf16[128,128]{1,0:T(8,128)(2,1)} %k_ref.3, bf16[128,128]{1,0:T(8,128)(2,1)} %v_ref.3, f32[8,128]{1,0:T(8,128)} %gate_ref.5), custom_call_target="tpu_custom_call" | custom-call | flops 1048576 | bytes 1048576 | tf_op jit(solution)/shard_map/pallas_call | solution.py:489
  1.6 4.1 %collective-permute-start = (bf16[1,288,128]{2,1,0:T(8,128)(2,1)S(1)}, bf16[1,288,128]{2,1,0:T(8,128)(2,1)S(1)}, u32[]{:S(2)}, u32[]{:S(2)}) collective-permute-start(bf16[1,288,128]{2,1,0:T(8,128)(2,1)S(1)} %bitcast.5), channel_id=1, source_target_pairs={{0,16},{2,18},{4,20},{6,22},{8,24},{10,26},{12,28},{14,30},{16,0},... | collective-permute-start | bytes 221192 | tf_op jit(solution)/shard_map/ppermute | solution.py:466
  5.7 3.9 %collective-permute-done = bf16[1,288,128]{2,1,0:T(8,128)(2,1)S(1)} collective-permute-done((bf16[1,288,128]{2,1,0:T(8,128)(2,1)S(1)}, bf16[1,288,128]{2,1,0:T(8,128)(2,1)S(1)}, u32[]{:S(2)}, u32[]{:S(2)}) %collective-permute-start) | collective-permute-done | bytes 73760 | tf_op jit(solution)/shard_map/ppermute | solution.py:466
  9.7 0.7 collective-permute-start.1
  10.4 4.5 %collective-permute-done.1 = bf16[2,288,128]{2,1,0:T(8,128)(2,1)S(1)} collective-permute-done((bf16[2,288,128]{2,1,0:T(8,128)(2,1)S(1)}, bf16[2,288,128]{2,1,0:T(8,128)(2,1)S(1)}, u32[]{:S(2)}, u32[]{:S(2)}) %collective-permute-start.1) | collective-permute-done | bytes 147488 | tf_op jit(solution)/shard_map/ppermute | solution.py:466
  14.9 1.8 %collective-permute-start.3 = (bf16[4,288,128]{2,1,0:T(8,128)(2,1)S(1)}, bf16[4,288,128]{2,1,0:T(8,128)(2,1)S(1)}, u32[]{:S(2)}, u32[]{:S(2)}) collective-permute-start(bf16[4,288,128]{2,1,0:T(8,128)(2,1)S(1)} %pad_maximum_fusion.even_ref.even_a_ref), channel_id=1, source_target_pairs={{0,4},{2,6},{4,0},{6,2},{8,12},{10,14},{12,8},{14,10},{16,20},{18,... | collective-permute-start | bytes 884744 | tf_op jit(solution)/shard_map/ppermute | solution.py:466
  16.7 0.0 collective-permute-start.2
  16.7 5.0 %collective-permute-done.3.even_b_ref = bf16[4,288,128]{2,1,0:T(8,128)(2,1)S(1)} collective-permute-done((bf16[4,288,128]{2,1,0:T(8,128)(2,1)S(1)}, bf16[4,288,128]{2,1,0:T(8,128)(2,1)S(1)}, u32[]{:S(2)}, u32[]{:S(2)}) %collective-permute-start.3) | collective-permute-done | bytes 294944 | tf_op jit(solution)/shard_map/ppermute | solution.py:466
  21.7 0.0 collective-permute-start.4
  21.7 3.3 %shard_map.113 = (f32[8,128,128]{2,1,0:T(8,128)S(1)}, f32[8,128,128]{2,1,0:T(8,128)S(1)}, f32[8,128,128]{2,1,0:T(8,128)S(1)}, f32[8,128,128]{2,1,0:T(8,128)S(1)}, f32[8,128,128]{2,1,0:T(8,128)S(1)}) custom-call(bf16[288,128]{1,0:T(8,128)(2,1)S(1)} %shard_map.111.packed_ref, f32[8,12]{1,0:T(8,128)} %level_ref.1, bf16[128,1024]{1,0:T(8,128)(2,1)} %q_ref.7, ...), custom_call_target="tpu_custom_call" | custom-call | flops 536870912 | bytes 1048576 | tf_op jit(solution)/shard_map/pallas_call | solution.py:495
  25.0 0.0 copy-start.4
  25.0 0.0 copy-start.5
  25.0 0.0 copy-start.6
  25.0 0.0 collective-permute-done.2.odd_ref.odd_a_ref
  25.0 0.0 copy-done
  25.0 0.4 shard_map.112
  25.4 0.0 collective-permute-done.4.odd_b_ref
  25.4 0.3 copy-done.4
  25.7 0.0 copy-done.5
  25.7 0.0 copy-done.6
  25.7 0.0 copy-start.1
  25.7 0.0 copy-start.2
  25.7 0.0 copy-start.3
  25.7 2.5 %shard_map.114 = (f32[8,128,128]{2,1,0:T(8,128)S(1)}, f32[8,128,128]{2,1,0:T(8,128)S(1)}, f32[4,8,128,128]{3,2,1,0:T(8,128)S(1)}, f32[8,128,128]{2,1,0:T(8,128)S(1)}, f32[8,128]{1,0:T(8,128)S(1)}) custom-call(s32[1]{0:T(128)} %bitcast.span_ref, f32[8,12]{1,0:T(8,128)S(1)} %copy-done.6, bf16[128,1024]{1,0:T(8,128)(2,1)S(1)} %copy-done, ...), custom_call_target="tpu_custom_call" | custom-call | flops 2147483648 | bytes 1048576 | tf_op jit(solution)/shard_map/pallas_call | solution.py:529
  28.2 1.7 %collective-permute-start.5 = (f32[8,128]{1,0:T(8,128)S(1)}, f32[8,128]{1,0:T(8,128)S(1)}, u32[]{:S(2)}, u32[]{:S(2)}) collective-permute-start(f32[8,128]{1,0:T(8,128)S(1)} %get-tuple-element.32.sums_a_ref), channel_id=1, source_target_pairs={{0,1},{1,0},{2,3},{3,2},{4,5},{5,4},{6,7},{7,6},{8,9},{9,8},{10,11... | collective-permute-start | bytes 12296 | tf_op jit(solution)/shard_map/ppermute | solution.py:466
  29.9 1.9 %collective-permute-done.5.sums_b_ref = f32[8,128]{1,0:T(8,128)S(1)} collective-permute-done((f32[8,128]{1,0:T(8,128)S(1)}, f32[8,128]{1,0:T(8,128)S(1)}, u32[]{:S(2)}, u32[]{:S(2)}) %collective-permute-start.5) | collective-permute-done | bytes 4128 | tf_op jit(solution)/shard_map/ppermute | solution.py:466
  31.8 0.0 copy-done.1
  31.8 0.0 copy-done.2
  31.9 0.0 copy-done.3
  31.9 2.7 %shard_map.116 = (f32[520,128]{1,0:T(8,128)S(1)}, f32[520,128]{1,0:T(8,128)S(1)}) custom-call(s32[1]{0:T(128)} %bitcast.span_ref, f32[8,128]{1,0:T(8,128)S(1)} %get-tuple-element.32.sums_a_ref, f32[8,128]{1,0:T(8,128)S(1)} %collective-permute-done.5.sums_b_ref, f32[8,128]{1,0:T(8,128)S(1)} %copy-done.4, bf16[128,1024]{1,0:T(8,128)(2,1)S(1)} %copy-done, ...), custom_call_target="tpu_custom_call" | custom-call | flops 536870912 | bytes 1048576 | tf_op jit(solution)/shard_map/pallas_call | solution.py:559
  34.6 0.0 collective-permute-start.13
  34.6 2.7 %shard_map.115 = (f32[520,128]{1,0:T(8,128)S(1)}, f32[520,128]{1,0:T(8,128)S(1)}) custom-call(s32[1]{0:T(128)} %bitcast.span_ref, f32[8,128]{1,0:T(8,128)S(1)} %get-tuple-element.32.sums_a_ref, f32[8,128]{1,0:T(8,128)S(1)} %collective-permute-done.5.sums_b_ref, f32[8,128]{1,0:T(8,128)S(1)} %copy-done.4, bf16[128,1024]{1,0:T(8,128)(2,1)S(1)} %copy-done, ...), custom_call_target="tpu_custom_call" | custom-call | flops 536870912 | bytes 1048576 | tf_op jit(solution)/shard_map/pallas_call | solution.py:559
  37.3 0.5 collective-permute-start.6
  37.8 0.0 collective-permute-done.13
  37.9 2.7 %collective-permute-start.14 = (f32[264,128]{1,0:T(8,128)S(1)}, f32[264,128]{1,0:T(8,128)S(1)}, u32[]{:S(2)}, u32[]{:S(2)}) collective-permute-start(f32[264,128]{1,0:T(8,128)S(1)} %slice.112), channel_id=1, source_target_pairs={{0,4},{2,6},{4,0},{6,2},{8,12},{10,14},{12,8},{14,10},{16,20},{18,... | collective-permute-start | bytes 405512 | tf_op jit(solution)/shard_map/ppermute | solution.py:466
  40.6 0.0 collective-permute-done.6
  40.6 1.1 %collective-permute-start.7 = (f32[264,128]{1,0:T(8,128)S(1)}, f32[264,128]{1,0:T(8,128)S(1)}, u32[]{:S(2)}, u32[]{:S(2)}) collective-permute-start(f32[264,128]{1,0:T(8,128)S(1)} %slice.103), channel_id=1, source_target_pairs={{0,4},{2,6},{4,0},{6,2},{8,12},{10,14},{12,8},{14,10},{16,20},{18,... | collective-permute-start | bytes 405512 | tf_op jit(solution)/shard_map/ppermute | solution.py:466
  41.7 3.3 %collective-permute-done.14 = f32[264,128]{1,0:T(8,128)S(1)} collective-permute-done((f32[264,128]{1,0:T(8,128)S(1)}, f32[264,128]{1,0:T(8,128)S(1)}, u32[]{:S(2)}, u32[]{:S(2)}) %collective-permute-start.14) | collective-permute-done | bytes 135200 | tf_op jit(solution)/shard_map/ppermute | solution.py:466
  45.0 3.6 %collective-permute-start.15 = (f32[136,128]{1,0:T(8,128)S(1)}, f32[136,128]{1,0:T(8,128)S(1)}, u32[]{:S(2)}, u32[]{:S(2)}) collective-permute-start(f32[136,128]{1,0:T(8,128)S(1)} %pad_maximum_fusion.6), channel_id=1, source_target_pairs={{0,8},{2,10},{4,12},{6,14},{8,0},{10,2},{12,4},{14,6},{16,24},{18,... | collective-permute-start | bytes 208904 | tf_op jit(solution)/shard_map/ppermute | solution.py:466
  48.7 0.0 collective-permute-done.7
  48.7 2.3 %collective-permute-start.8 = (f32[136,128]{1,0:T(8,128)S(1)}, f32[136,128]{1,0:T(8,128)S(1)}, u32[]{:S(2)}, u32[]{:S(2)}) collective-permute-start(f32[136,128]{1,0:T(8,128)S(1)} %pad_maximum_fusion.7), channel_id=1, source_target_pairs={{0,8},{2,10},{4,12},{6,14},{8,0},{10,2},{12,4},{14,6},{16,24},{18,... | collective-permute-start | bytes 208904 | tf_op jit(solution)/shard_map/ppermute | solution.py:466
  51.0 0.0 collective-permute-done.15
  51.0 7.1 %collective-permute-start.16 = (f32[136,128]{1,0:T(8,128)S(1)}, f32[136,128]{1,0:T(8,128)S(1)}, u32[]{:S(2)}, u32[]{:S(2)}) collective-permute-start(f32[136,128]{1,0:T(8,128)S(1)} %pad_maximum_fusion.9), channel_id=1, source_target_pairs={{0,16},{2,18},{4,20},{6,22},{8,24},{10,26},{12,28},{14,30},{16,0},... | collective-permute-start | bytes 208904 | tf_op jit(solution)/shard_map/ppermute | solution.py:466
  58.1 0.0 collective-permute-done.8
  58.2 2.6 %collective-permute-start.9 = (f32[136,128]{1,0:T(8,128)S(1)}, f32[136,128]{1,0:T(8,128)S(1)}, u32[]{:S(2)}, u32[]{:S(2)}) collective-permute-start(f32[136,128]{1,0:T(8,128)S(1)} %pad_maximum_fusion.8), channel_id=1, source_target_pairs={{0,16},{2,18},{4,20},{6,22},{8,24},{10,26},{12,28},{14,30},{16,0},... | collective-permute-start | bytes 208904 | tf_op jit(solution)/shard_map/ppermute | solution.py:466
  60.7 0.0 collective-permute-done.16
  60.8 3.8 %collective-permute-start.17 = (f32[128,128]{1,0:T(8,128)S(1)}, f32[128,128]{1,0:T(8,128)S(1)}, u32[]{:S(2)}, u32[]{:S(2)}) collective-permute-start(f32[128,128]{1,0:T(8,128)S(1)} %slice.119), channel_id=1, source_target_pairs={{0,8},{2,10},{4,12},{6,14},{8,0},{10,2},{12,4},{14,6},{16,24},{18,... | collective-permute-start | bytes 196616 | tf_op jit(solution)/shard_map/ppermute | solution.py:466
  64.5 0.0 collective-permute-done.9
  64.6 1.1 %collective-permute-start.10 = (f32[128,128]{1,0:T(8,128)S(1)}, f32[128,128]{1,0:T(8,128)S(1)}, u32[]{:S(2)}, u32[]{:S(2)}) collective-permute-start(f32[128,128]{1,0:T(8,128)S(1)} %slice.110), channel_id=1, source_target_pairs={{0,8},{2,10},{4,12},{6,14},{8,0},{10,2},{12,4},{14,6},{16,24},{18,... | collective-permute-start | bytes 196616 | tf_op jit(solution)/shard_map/ppermute | solution.py:466
  65.7 1.7 %collective-permute-done.17 = f32[128,128]{1,0:T(8,128)S(1)} collective-permute-done((f32[128,128]{1,0:T(8,128)S(1)}, f32[128,128]{1,0:T(8,128)S(1)}, u32[]{:S(2)}, u32[]{:S(2)}) %collective-permute-start.17) | collective-permute-done | bytes 65568 | tf_op jit(solution)/shard_map/ppermute | solution.py:466
  67.4 1.4 %collective-permute-start.18 = (f32[256,128]{1,0:T(8,128)S(1)}, f32[256,128]{1,0:T(8,128)S(1)}, u32[]{:S(2)}, u32[]{:S(2)}) collective-permute-start(f32[256,128]{1,0:T(8,128)S(1)} %pad_maximum_fusion.5), channel_id=1, source_target_pairs={{0,4},{2,6},{4,0},{6,2},{8,12},{10,14},{12,8},{14,10},{16,20},{18,... | collective-permute-start | bytes 393224 | tf_op jit(solution)/shard_map/ppermute | solution.py:466
  68.8 0.1 collective-permute-done.10
  68.9 1.7 %collective-permute-start.11 = (f32[256,128]{1,0:T(8,128)S(1)}, f32[256,128]{1,0:T(8,128)S(1)}, u32[]{:S(2)}, u32[]{:S(2)}) collective-permute-start(f32[256,128]{1,0:T(8,128)S(1)} %pad_maximum_fusion.4), channel_id=1, source_target_pairs={{0,4},{2,6},{4,0},{6,2},{8,12},{10,14},{12,8},{14,10},{16,20},{18,... | collective-permute-start | bytes 393224 | tf_op jit(solution)/shard_map/ppermute | solution.py:466
  70.6 2.2 %collective-permute-done.18 = f32[256,128]{1,0:T(8,128)S(1)} collective-permute-done((f32[256,128]{1,0:T(8,128)S(1)}, f32[256,128]{1,0:T(8,128)S(1)}, u32[]{:S(2)}, u32[]{:S(2)}) %collective-permute-start.18) | collective-permute-done | bytes 131104 | tf_op jit(solution)/shard_map/ppermute | solution.py:466
  72.9 0.1 collective-permute-start.19
  72.9 1.3 %collective-permute-done.11 = f32[256,128]{1,0:T(8,128)S(1)} collective-permute-done((f32[256,128]{1,0:T(8,128)S(1)}, f32[256,128]{1,0:T(8,128)S(1)}, u32[]{:S(2)}, u32[]{:S(2)}) %collective-permute-start.11) | collective-permute-done | bytes 131104 | tf_op jit(solution)/shard_map/ppermute | solution.py:466
  74.3 0.1 collective-permute-start.12
  74.4 0.6 maximum_bitcast_fusion
  75.0 0.6 pad_maximum_fusion.10
  75.6 0.0 collective-permute-done.19.refs_3_
  75.6 0.3 collective-permute-done.12.refs_1_
  75.9 1.0 %shard_map.117 = (f32[8,128,128]{2,1,0:T(8,128)}, f32[8,128,128]{2,1,0:T(8,128)}) custom-call(s32[1]{0:T(128)} %bitcast.span_ref, f32[512,128]{1,0:T(8,128)S(1)} %pad_maximum_fusion.1.refs_0_, f32[512,128]{1,0:T(8,128)S(1)} %collective-permute-done.12.refs_1_, f32[512,128]{1,0:T(8,128)S(1)} %pad_maximum_fusion.2.refs_2_, ...), custom_call_target="tpu_custom_call" | custom-call | flops 1048576 | bytes 1048576 | tf_op jit(solution)/shard_map/pallas_call | solution.py:592
  (30 shorter events, 0.3 us)
Async XLA Ops:
  0.6 24.4 %copy-start = (bf16[128,1024]{1,0:T(8,128)(2,1)S(1)}, bf16[128,1024]{1,0:T(8,128)(2,1)}, u32[]{:S(2)}) copy-start(bf16[128,1024]{1,0:T(8,128)(2,1)} %q_ref.7) | copy-start | bytes 786436
  1.6 8.0 %collective-permute-start = (bf16[1,288,128]{2,1,0:T(8,128)(2,1)S(1)}, bf16[1,288,128]{2,1,0:T(8,128)(2,1)S(1)}, u32[]{:S(2)}, u32[]{:S(2)}) collective-permute-start(bf16[1,288,128]{2,1,0:T(8,128)(2,1)S(1)} %bitcast.5), channel_id=1, source_target_pairs={{0,16},{2,18},{4,20},{6,22},{8,24},{10,26},{12,28},{14,30},{16,0},... | collective-permute-start | bytes 221192 | tf_op jit(solution)/shard_map/ppermute | solution.py:466
  9.7 5.2 %collective-permute-start.1 = (bf16[2,288,128]{2,1,0:T(8,128)(2,1)S(1)}, bf16[2,288,128]{2,1,0:T(8,128)(2,1)S(1)}, u32[]{:S(2)}, u32[]{:S(2)}) collective-permute-start(bf16[2,288,128]{2,1,0:T(8,128)(2,1)S(1)} %pad_maximum_fusion.3), channel_id=1, source_target_pairs={{0,8},{2,10},{4,12},{6,14},{8,0},{10,2},{12,4},{14,6},{16,24},{18,... | collective-permute-start | bytes 442376 | tf_op jit(solution)/shard_map/ppermute | solution.py:466
  14.9 6.8 %collective-permute-start.3 = (bf16[4,288,128]{2,1,0:T(8,128)(2,1)S(1)}, bf16[4,288,128]{2,1,0:T(8,128)(2,1)S(1)}, u32[]{:S(2)}, u32[]{:S(2)}) collective-permute-start(bf16[4,288,128]{2,1,0:T(8,128)(2,1)S(1)} %pad_maximum_fusion.even_ref.even_a_ref), channel_id=1, source_target_pairs={{0,4},{2,6},{4,0},{6,2},{8,12},{10,14},{12,8},{14,10},{16,20},{18,... | collective-permute-start | bytes 884744 | tf_op jit(solution)/shard_map/ppermute | solution.py:466
  16.7 8.3 %collective-permute-start.2 = (bf16[4,288,128]{2,1,0:T(8,128)(2,1)S(1)}, bf16[4,288,128]{2,1,0:T(8,128)(2,1)S(1)}, u32[]{:S(2)}, u32[]{:S(2)}) collective-permute-start(bf16[4,288,128]{2,1,0:T(8,128)(2,1)S(1)} %pad_maximum_fusion.even_ref.even_a_ref), channel_id=1, source_target_pairs={{0,2},{2,0},{4,6},{6,4},{8,10},{10,8},{12,14},{14,12},{16,18},{18,... | collective-permute-start | bytes 884744 | tf_op jit(solution)/shard_map/ppermute | solution.py:466
  21.7 3.7 %collective-permute-start.4 = (bf16[4,288,128]{2,1,0:T(8,128)(2,1)S(1)}, bf16[4,288,128]{2,1,0:T(8,128)(2,1)S(1)}, u32[]{:S(2)}, u32[]{:S(2)}) collective-permute-start(bf16[4,288,128]{2,1,0:T(8,128)(2,1)S(1)} %collective-permute-done.3.even_b_ref), channel_id=1, source_target_pairs={{0,2},{2,0},{4,6},{6,4},{8,10},{10,8},{12,14},{14,12},{16,18},{18,... | collective-permute-start | bytes 884744 | tf_op jit(solution)/shard_map/ppermute | solution.py:466
  25.0 0.7 copy-start.4
  25.0 0.7 copy-start.5
  25.0 0.7 copy-start.6
  25.7 6.2 %copy-start.1 = (f32[8,128,128]{2,1,0:T(8,128)S(1)}, f32[8,128,128]{2,1,0:T(8,128)}, u32[]{:S(2)}) copy-start(f32[8,128,128]{2,1,0:T(8,128)} %kmap_ref.3) | copy-start | bytes 1572868
  25.7 6.2 %copy-start.2 = (bf16[128,128]{1,0:T(8,128)(2,1)S(1)}, bf16[128,128]{1,0:T(8,128)(2,1)}, u32[]{:S(2)}) copy-start(bf16[128,128]{1,0:T(8,128)(2,1)} %k_ref.3) | copy-start | bytes 98308
  25.7 6.2 %copy-start.3 = (bf16[128,128]{1,0:T(8,128)(2,1)S(1)}, bf16[128,128]{1,0:T(8,128)(2,1)}, u32[]{:S(2)}) copy-start(bf16[128,128]{1,0:T(8,128)(2,1)} %v_ref.3) | copy-start | bytes 98308
  28.2 3.6 %collective-permute-start.5 = (f32[8,128]{1,0:T(8,128)S(1)}, f32[8,128]{1,0:T(8,128)S(1)}, u32[]{:S(2)}, u32[]{:S(2)}) collective-permute-start(f32[8,128]{1,0:T(8,128)S(1)} %get-tuple-element.32.sums_a_ref), channel_id=1, source_target_pairs={{0,1},{1,0},{2,3},{3,2},{4,5},{5,4},{6,7},{7,6},{8,9},{9,8},{10,11... | collective-permute-start | bytes 12296 | tf_op jit(solution)/shard_map/ppermute | solution.py:466
  34.6 3.2 %collective-permute-start.13 = (f32[520,128]{1,0:T(8,128)S(1)}, f32[520,128]{1,0:T(8,128)S(1)}, u32[]{:S(2)}, u32[]{:S(2)}) collective-permute-start(f32[520,128]{1,0:T(8,128)S(1)} %get-tuple-element.43), channel_id=1, source_target_pairs={{0,2},{2,0},{4,6},{6,4},{8,10},{10,8},{12,14},{14,12},{16,18},{18,... | collective-permute-start | bytes 798728 | tf_op jit(solution)/shard_map/ppermute | solution.py:466
  37.3 3.2 %collective-permute-start.6 = (f32[520,128]{1,0:T(8,128)S(1)}, f32[520,128]{1,0:T(8,128)S(1)}, u32[]{:S(2)}, u32[]{:S(2)}) collective-permute-start(f32[520,128]{1,0:T(8,128)S(1)} %get-tuple-element.41), channel_id=1, source_target_pairs={{0,2},{2,0},{4,6},{6,4},{8,10},{10,8},{12,14},{14,12},{16,18},{18,... | collective-permute-start | bytes 798728 | tf_op jit(solution)/shard_map/ppermute | solution.py:466
  37.9 7.1 %collective-permute-start.14 = (f32[264,128]{1,0:T(8,128)S(1)}, f32[264,128]{1,0:T(8,128)S(1)}, u32[]{:S(2)}, u32[]{:S(2)}) collective-permute-start(f32[264,128]{1,0:T(8,128)S(1)} %slice.112), channel_id=1, source_target_pairs={{0,4},{2,6},{4,0},{6,2},{8,12},{10,14},{12,8},{14,10},{16,20},{18,... | collective-permute-start | bytes 405512 | tf_op jit(solution)/shard_map/ppermute | solution.py:466
  40.6 8.0 %collective-permute-start.7 = (f32[264,128]{1,0:T(8,128)S(1)}, f32[264,128]{1,0:T(8,128)S(1)}, u32[]{:S(2)}, u32[]{:S(2)}) collective-permute-start(f32[264,128]{1,0:T(8,128)S(1)} %slice.103), channel_id=1, source_target_pairs={{0,4},{2,6},{4,0},{6,2},{8,12},{10,14},{12,8},{14,10},{16,20},{18,... | collective-permute-start | bytes 405512 | tf_op jit(solution)/shard_map/ppermute | solution.py:466
  45.0 5.9 %collective-permute-start.15 = (f32[136,128]{1,0:T(8,128)S(1)}, f32[136,128]{1,0:T(8,128)S(1)}, u32[]{:S(2)}, u32[]{:S(2)}) collective-permute-start(f32[136,128]{1,0:T(8,128)S(1)} %pad_maximum_fusion.6), channel_id=1, source_target_pairs={{0,8},{2,10},{4,12},{6,14},{8,0},{10,2},{12,4},{14,6},{16,24},{18,... | collective-permute-start | bytes 208904 | tf_op jit(solution)/shard_map/ppermute | solution.py:466
  48.7 9.4 %collective-permute-start.8 = (f32[136,128]{1,0:T(8,128)S(1)}, f32[136,128]{1,0:T(8,128)S(1)}, u32[]{:S(2)}, u32[]{:S(2)}) collective-permute-start(f32[136,128]{1,0:T(8,128)S(1)} %pad_maximum_fusion.7), channel_id=1, source_target_pairs={{0,8},{2,10},{4,12},{6,14},{8,0},{10,2},{12,4},{14,6},{16,24},{18,... | collective-permute-start | bytes 208904 | tf_op jit(solution)/shard_map/ppermute | solution.py:466
  51.0 9.7 %collective-permute-start.16 = (f32[136,128]{1,0:T(8,128)S(1)}, f32[136,128]{1,0:T(8,128)S(1)}, u32[]{:S(2)}, u32[]{:S(2)}) collective-permute-start(f32[136,128]{1,0:T(8,128)S(1)} %pad_maximum_fusion.9), channel_id=1, source_target_pairs={{0,16},{2,18},{4,20},{6,22},{8,24},{10,26},{12,28},{14,30},{16,0},... | collective-permute-start | bytes 208904 | tf_op jit(solution)/shard_map/ppermute | solution.py:466
  58.2 6.4 %collective-permute-start.9 = (f32[136,128]{1,0:T(8,128)S(1)}, f32[136,128]{1,0:T(8,128)S(1)}, u32[]{:S(2)}, u32[]{:S(2)}) collective-permute-start(f32[136,128]{1,0:T(8,128)S(1)} %pad_maximum_fusion.8), channel_id=1, source_target_pairs={{0,16},{2,18},{4,20},{6,22},{8,24},{10,26},{12,28},{14,30},{16,0},... | collective-permute-start | bytes 208904 | tf_op jit(solution)/shard_map/ppermute | solution.py:466
  60.8 6.6 %collective-permute-start.17 = (f32[128,128]{1,0:T(8,128)S(1)}, f32[128,128]{1,0:T(8,128)S(1)}, u32[]{:S(2)}, u32[]{:S(2)}) collective-permute-start(f32[128,128]{1,0:T(8,128)S(1)} %slice.119), channel_id=1, source_target_pairs={{0,8},{2,10},{4,12},{6,14},{8,0},{10,2},{12,4},{14,6},{16,24},{18,... | collective-permute-start | bytes 196616 | tf_op jit(solution)/shard_map/ppermute | solution.py:466
  64.6 4.3 %collective-permute-start.10 = (f32[128,128]{1,0:T(8,128)S(1)}, f32[128,128]{1,0:T(8,128)S(1)}, u32[]{:S(2)}, u32[]{:S(2)}) collective-permute-start(f32[128,128]{1,0:T(8,128)S(1)} %slice.110), channel_id=1, source_target_pairs={{0,8},{2,10},{4,12},{6,14},{8,0},{10,2},{12,4},{14,6},{16,24},{18,... | collective-permute-start | bytes 196616 | tf_op jit(solution)/shard_map/ppermute | solution.py:466
  67.4 5.5 %collective-permute-start.18 = (f32[256,128]{1,0:T(8,128)S(1)}, f32[256,128]{1,0:T(8,128)S(1)}, u32[]{:S(2)}, u32[]{:S(2)}) collective-permute-start(f32[256,128]{1,0:T(8,128)S(1)} %pad_maximum_fusion.5), channel_id=1, source_target_pairs={{0,4},{2,6},{4,0},{6,2},{8,12},{10,14},{12,8},{14,10},{16,20},{18,... | collective-permute-start | bytes 393224 | tf_op jit(solution)/shard_map/ppermute | solution.py:466
  68.9 5.3 %collective-permute-start.11 = (f32[256,128]{1,0:T(8,128)S(1)}, f32[256,128]{1,0:T(8,128)S(1)}, u32[]{:S(2)}, u32[]{:S(2)}) collective-permute-start(f32[256,128]{1,0:T(8,128)S(1)} %pad_maximum_fusion.4), channel_id=1, source_target_pairs={{0,4},{2,6},{4,0},{6,2},{8,12},{10,14},{12,8},{14,10},{16,20},{18,... | collective-permute-start | bytes 393224 | tf_op jit(solution)/shard_map/ppermute | solution.py:466
  72.9 2.7 %collective-permute-start.19 = (f32[512,128]{1,0:T(8,128)S(1)}, f32[512,128]{1,0:T(8,128)S(1)}, u32[]{:S(2)}, u32[]{:S(2)}) collective-permute-start(f32[512,128]{1,0:T(8,128)S(1)} %pad_maximum_fusion.2.refs_2_), channel_id=1, source_target_pairs={{0,2},{2,0},{4,6},{6,4},{8,10},{10,8},{12,14},{14,12},{16,18},{18,... | collective-permute-start | bytes 786440 | tf_op jit(solution)/shard_map/ppermute | solution.py:466
  74.3 1.6 %collective-permute-start.12 = (f32[512,128]{1,0:T(8,128)S(1)}, f32[512,128]{1,0:T(8,128)S(1)}, u32[]{:S(2)}, u32[]{:S(2)}) collective-permute-start(f32[512,128]{1,0:T(8,128)S(1)} %pad_maximum_fusion.1.refs_0_), channel_id=1, source_target_pairs={{0,2},{2,0},{4,6},{6,4},{8,10},{10,8},{12,14},{14,12},{16,18},{18,... | collective-permute-start | bytes 786440 | tf_op jit(solution)/shard_map/ppermute | solution.py:466
where the time goes:
time: 77.2 us; the launch traced here: 76.9 us
  starting transfers between devices  36.4 us (47%)
  waiting for transfers between devices  24.1 us (31%)
  Pallas kernels  13.6 us (18%)
  other arithmetic  1.49 us (2%)
  between operations  0.91 us (1%)
    ppermute x20, starting transfers between devices, swap(): return lax.ppermute(value, axis, [(i, i ^ stride) for i in range(count)])  36.4 us
    ppermute x20, waiting for transfers between devices, swap(): return lax.ppermute(value, axis, [(i, i ^ stride) for i in range(count)])  24.1 us
    pallas_call x2, Pallas kernels, on_device(): call(backward_kernel, smem(1) + vmem(16), [shape(share * (dim + 2), dim)]...  5.45 us
    pallas_call x1, Pallas kernels, on_device(): call(local_kernel, vmem(1) + hbm(4), [shape(*cube)] * 5, 24, 1 << 29, scr...  3.26 us
    pallas_call x1, Pallas kernels, on_device(): call(forward_kernel, smem(2) + vmem(14), [shape(*cube), shape(*cube), sha...  2.5 us
  transfers between devices with their start and end apart: 20, of which 10 were waited for; matrix products, arithmetic and copies ran while one was open for 2% of the time, Pallas kernels for 8%

commit v1 on v0

--- a/solution.py
+++ b/solution.py
@@ -166,6 +166,14 @@
         state_ref[p, h] = state[h * dim : (h + 1) * dim]
 
 
+def by_level(offsets):
+    levels = {}
+    for p, offset in enumerate(offsets):
+        if p > 0:
+            levels.setdefault(offset.bit_length() - 1, []).append(p)
+    return sorted(levels.items())
+
+
 def early_kernel(
     span_ref, q_ref, even_ref, odd_ref, score_ref, peak_ref, state_ref, ends_ref, before_ref, decay_scr, *, offsets,
 ):
@@ -197,15 +205,19 @@
     def _():
         pair_state(kt, v, decay_scr[0], state_ref, 0)
 
-    for p in range(1, pairs):
-
-        @pl.when((span ^ offsets[p]) < span)
-        def _(p=p):
-            kt, v = pair_blocks(even_ref, odd_ref, p, rows)
-            score = dot(q_all, kt) * scale
-            score_ref[p] = score
-            peak_ref[...] = jnp.maximum(peak_ref[...], jnp.maximum(score[:, :rows], score[:, rows:]))
-            pair_state(kt, v, decay_scr[p], state_ref, p)
+    for bit, members in by_level(offsets[:pairs]):
+
+        @pl.when(((span >> bit) & 1) == 1)
+        def _(members=members):
+            top = peak_ref[...]
+            blocks = [pair_blocks(even_ref, odd_ref, p, rows) for p in members]
+            for p, (kt, _) in zip(members, blocks):
+                score = dot(q_all, kt) * scale
+                score_ref[p] = score
+                top = jnp.maximum(top, jnp.maximum(score[:, :rows], score[:, rows:]))
+            peak_ref[...] = top
+            for p, (kt, v) in zip(members, blocks):
+                pair_state(kt, v, decay_scr[p], state_ref, p)
 
 
 def forward_kernel(
@@ -225,16 +237,23 @@
     q_all = stacked_queries(q_ref, dim)
     _, _, end_e, end_o, decay_e, decay_o = pair_decay(span, even_b_ref, odd_b_ref, heads)
     peak_scr[...] = peak_a_ref[...]
-    for p in range(late):
-
-        @pl.when((span ^ offsets[early + p]) < span)
-        def _(p=p):
-            at = slice(p * heads, (p + 1) * heads)
-            kt, v = pair_blocks(even_b_ref, odd_b_ref, p, rows)
-            score = dot(q_all, kt) * scale
-            score_scr[p] = score
-            peak_scr[...] = jnp.maximum(peak_scr[...], jnp.maximum(score[:, :rows], score[:, rows:]))
-            pair_state(kt, v, jnp.concatenate([decay_e[at], decay_o[at]], axis=1), state_scr, p)
+    for bit, members in by_level(offsets):
+        members = [p - early for p in members if p >= early]
+        if not members:
+            continue
+
+        @pl.when(((span >> bit) & 1) == 1)
+        def _(members=members):
+            top = peak_scr[...]
+            blocks = [pair_blocks(even_b_ref, odd_b_ref, p, rows) for p in members]
+            for p, (kt, _) in zip(members, blocks):
+                score = dot(q_all, kt) * scale
+                score_scr[p] = score
+                top = jnp.maximum(top, jnp.maximum(score[:, :rows], score[:, rows:]))
+            peak_scr[...] = top
+            for p, (kt, v) in zip(members, blocks):
+                at = slice(p * heads, (p + 1) * heads)
+                pair_state(kt, v, jnp.concatenate([decay_e[at], decay_o[at]], axis=1), state_scr, p)
 
     ends = jnp.concatenate([ends_a_ref[...], end_e + end_o], axis=0)
     size = pairs * heads
@@ -256,23 +275,27 @@
     peak = jnp.max(peak_scr[...], axis=1, keepdims=True)
     peak_scr[...] = jnp.broadcast_to(peak, peak_scr.shape)
 
-    def weigh(score, v):
+    def weigh(members):
         top = peak_scr[...]
-        left = jnp.exp(score[:, :rows] - top)
-        right = jnp.exp(score[:, rows:] - top)
-        total = left + right
-        return total, dot(jnp.concatenate([left.astype(BF16), right.astype(BF16)], axis=1), v)
-
-    total_scr[...], acc_scr[...] = weigh(score_a_ref[0], pair_blocks(even_a_ref, odd_a_ref, 0, rows)[1])
-    for p in range(1, pairs):
-
-        @pl.when((span ^ offsets[p]) < span)
-        def _(p=p):
+        total, weights, values = None, [], []
+        for p in members:
             if p < early:
-                total, acc = weigh(score_a_ref[p], pair_blocks(even_a_ref, odd_a_ref, p, rows)[1])
+                score, v = score_a_ref[p], pair_blocks(even_a_ref, odd_a_ref, p, rows)[1]
             else:
-                q = p - early
-                total, acc = weigh(score_scr[q], pair_blocks(even_b_ref, odd_b_ref, q, rows)[1])
+                score, v = score_scr[p - early], pair_blocks(even_b_ref, odd_b_ref, p - early, rows)[1]
+            left = jnp.exp(score[:, :rows] - top)
+            right = jnp.exp(score[:, rows:] - top)
+            total = left + right if total is None else total + (left + right)
+            weights += [left.astype(BF16), right.astype(BF16)]
+            values.append(v)
+        return total, dot(jnp.concatenate(weights, axis=1), jnp.concatenate(values, axis=0))
+
+    total_scr[...], acc_scr[...] = weigh([0])
+    for bit, members in by_level(offsets):
+
+        @pl.when(((span >> bit) & 1) == 1)
+        def _(members=members):
+            total, acc = weigh(members)
             total_scr[...] += total
             acc_scr[...] += acc
 
@@ -412,19 +435,25 @@
     send_ref[tail, :] = small
 
 
-def place_kernel(span_ref, *refs, splits):
-    q_ref, k_ref = refs[-2:]
+def place_kernel(span_ref, *refs, orders):
+    q_ref, k_ref, level_ref, gain_ref = refs[-4:]
     heads, dim, _ = q_ref.shape
-    parts = (len(refs) - 2) // 2
+    parts = len(orders)
     share = heads // parts
     span = span_ref[0]
     first = (span & 1) == 0
-    for h in range(heads):
-        mine_ref, other_ref = refs[2 * (h // share) : 2 * (h // share) + 2]
-        at = pl.ds(pl.multiple_of(chunk_of(h % share, share, span, splits) * dim, dim), dim)
-        mine, other = mine_ref[at, :], other_ref[at, :]
-        q_ref[h] = jnp.where(first, mine, other)
-        k_ref[h] = jnp.where(first, other, mine)
+    for part, splits in enumerate(orders):
+        mine_ref, other_ref, small_ref = refs[3 * part : 3 * part + 3]
+        tail = small_ref.shape[0] - 2 * share
+        for i in range(share):
+            h = part * share + i
+            at = pl.ds(pl.multiple_of(chunk_of(i, share, span, splits) * dim, dim), dim)
+            mine, other = mine_ref[at, :], other_ref[at, :]
+            q_ref[h] = jnp.where(first, mine, other)
+            k_ref[h] = jnp.where(first, other, mine)
+        heads_here = pl.ds(part * share, share)
+        gain_ref[heads_here, :] = small_ref[tail : tail + share, :]
+        level_ref[heads_here, :] = small_ref[tail + share :, : level_ref.shape[1]]
 
 
 def vmem(count):
@@ -477,7 +506,7 @@
     norm_width = heads * dim * groups
     gain = norm_gain.reshape(heads, dim)
     strides = [1 << bit for bit in reversed(range(1, span_bits))]
-    splits = (2, 4)
+    orders = [(2, 4), (4, 2)]
     cube = (heads, dim, dim)
     packed_rows = 2 * rows + GATE_ROWS
 
@@ -564,36 +593,41 @@
             1 << 29,
             norm_width=float(norm_width),
             total_tokens=float(total_tokens),
-            splits=splits,
+            splits=orders[part],
             heads=range(part * share, (part + 1) * share),
         )(
             span, sums, received, log_gate, queries, key_vectors, value_vectors, key_map, gain,
             qp, qt, score_decay, mix, raw, target, level_states, combined,
         )
         held.append(keep + swap(send, "seq", 1))
-    for split in splits:
+    for step in range(len(orders[0])):
         size //= 2
         for part in range(PARTS):
+            split = orders[part][step]
             here = held[part]
             got = swap(here[size:], "seq", split)
             held[part] = jnp.concatenate([here[:size] + got[:size], here[2 * size :] + got[size:]])
     for stride in strides:
-        if stride not in splits:
+        if stride not in orders[0]:
             for part in range(PARTS):
                 held[part] = held[part] + swap(held[part], "seq", stride)
-    small = [here[size:] for here in held]
     mine = [here[:size] for here in held]
-    for split in reversed(splits):
+    for step in reversed(range(len(orders[0]))):
         for part in range(PARTS):
+            split = orders[part][step]
             mine[part] = jnp.concatenate([mine[part], swap(mine[part], "seq", split)])
     pieces = []
     for part in range(PARTS):
-        pieces += [mine[part], swap(mine[part], "seq", 1)]
-    grad_query, grad_key = call(
-        place_kernel, smem(1) + vmem(2 * PARTS), [shape(*cube)] * 2, 16, 1 << 20, splits=splits
+        pieces += [mine[part], swap(mine[part], "seq", 1), held[part]]
+    grad_query, grad_key, grad_levels, grad_gain = call(
+        place_kernel,
+        smem(1) + vmem(3 * PARTS),
+        [shape(*cube), shape(*cube), shape(*level_weight.shape), shape(heads, dim)],
+        16,
+        1 << 20,
+        orders=orders,
     )(span, *pieces)
-    grad_gain = jnp.concatenate([piece[:share] for piece in small]).reshape(-1)
-    grad_levels = jnp.concatenate([piece[share:, : level_weight.shape[1]] for piece in small])
+    grad_gain = grad_gain.reshape(-1)
     return grad_query, grad_key, grad_levels, grad_gain
 
 

time: 77.2 us -> 75.5 us (0.978)
  starting transfers between devices: 36.4 us -> 34.7 us
  waiting for transfers between devices: 24.1 us -> 25.5 us
  other arithmetic: 1.49 us -> 0.29 us
    ppermute x20, starting transfers between devices: 36.4 us -> 34.7 us  [swap(): return lax.ppermute(value, axis, [(i, i ^ stride) for i in range(count)])]
    ppermute x20, waiting for transfers between devices: 24.1 us -> 25.5 us  [swap(): return lax.ppermute(value, axis, [(i, i ^ stride) for i in range(count)])]
  transfers between devices with their start and end apart: 20 -> 20, of which waited for: 10 -> 12; matrix products, arithmetic and copies ran while one was open for 2% -> 0% of each run, Pallas kernels for 8% -> 8%
where the time goes in v1:
time: 75.5 us; the launch traced here: 75.3 us
  starting transfers between devices  34.7 us (46%)
  waiting for transfers between devices  25.5 us (34%)
  Pallas kernels  13.5 us (18%)
  between operations  0.89 us (1%)
    ppermute x20, starting transfers between devices, swap(): return lax.ppermute(value, axis, [(i, i ^ stride) for i in range(count)])  34.7 us
    ppermute x20, waiting for transfers between devices, swap(): return lax.ppermute(value, axis, [(i, i ^ stride) for i in range(count)])  25.5 us
    pallas_call x2, Pallas kernels, on_device(): call(backward_kernel, smem(1) + vmem(16), [shape(share * (dim + 2), dim)]...  5.45 us
    pallas_call x1, Pallas kernels, on_device(): call(local_kernel, vmem(1) + hbm(4), [shape(*cube)] * 5, 24, 1 << 29, scr...  3.26 us
    pallas_call x1, Pallas kernels, on_device(): call(forward_kernel, smem(2) + vmem(14), [shape(*cube), shape(*cube), sha...  2.46 us
  transfers between devices with their start and end apart: 20, of which 12 were waited for; matrix products, arithmetic and copies ran while one was open for 0% of the time, Pallas kernels for 8%

profile of v1, /device:TPU:0, one launch (start us, length us, event | category | flops | bytes accessed | tf_op | source)
XLA Modules:
  0.0 75.3 jit_solution(9349676429026156189)
XLA Ops:
  0.6 0.0 copy-start
  0.6 0.9 %shard_map.111.packed_ref = bf16[288,128]{1,0:T(8,128)(2,1)S(1)} custom-call(bf16[128,128]{1,0:T(8,128)(2,1)} %k_ref.3, bf16[128,128]{1,0:T(8,128)(2,1)} %v_ref.3, f32[8,128]{1,0:T(8,128)} %gate_ref.5), custom_call_target="tpu_custom_call" | custom-call | flops 1048576 | bytes 1048576 | tf_op jit(solution)/shard_map/pallas_call | solution.py:518
  1.6 4.1 %collective-permute-start = (bf16[1,288,128]{2,1,0:T(8,128)(2,1)S(1)}, bf16[1,288,128]{2,1,0:T(8,128)(2,1)S(1)}, u32[]{:S(2)}, u32[]{:S(2)}) collective-permute-start(bf16[1,288,128]{2,1,0:T(8,128)(2,1)S(1)} %bitcast.4), channel_id=1, source_target_pairs={{0,16},{2,18},{4,20},{6,22},{8,24},{10,26},{12,28},{14,30},{16,0},... | collective-permute-start | bytes 221192 | tf_op jit(solution)/shard_map/ppermute | solution.py:495
  5.7 3.9 %collective-permute-done = bf16[1,288,128]{2,1,0:T(8,128)(2,1)S(1)} collective-permute-done((bf16[1,288,128]{2,1,0:T(8,128)(2,1)S(1)}, bf16[1,288,128]{2,1,0:T(8,128)(2,1)S(1)}, u32[]{:S(2)}, u32[]{:S(2)}) %collective-permute-start) | collective-permute-done | bytes 73760 | tf_op jit(solution)/shard_map/ppermute | solution.py:495
  9.7 0.7 collective-permute-start.1
  10.4 4.5 %collective-permute-done.1 = bf16[2,288,128]{2,1,0:T(8,128)(2,1)S(1)} collective-permute-done((bf16[2,288,128]{2,1,0:T(8,128)(2,1)S(1)}, bf16[2,288,128]{2,1,0:T(8,128)(2,1)S(1)}, u32[]{:S(2)}, u32[]{:S(2)}) %collective-permute-start.1) | collective-permute-done | bytes 147488 | tf_op jit(solution)/shard_map/ppermute | solution.py:495
  14.9 1.8 %collective-permute-start.3 = (bf16[4,288,128]{2,1,0:T(8,128)(2,1)S(1)}, bf16[4,288,128]{2,1,0:T(8,128)(2,1)S(1)}, u32[]{:S(2)}, u32[]{:S(2)}) collective-permute-start(bf16[4,288,128]{2,1,0:T(8,128)(2,1)S(1)} %pad_maximum_fusion.even_ref.even_a_ref), channel_id=1, source_target_pairs={{0,4},{2,6},{4,0},{6,2},{8,12},{10,14},{12,8},{14,10},{16,20},{18,... | collective-permute-start | bytes 884744 | tf_op jit(solution)/shard_map/ppermute | solution.py:495
  16.7 0.0 collective-permute-start.2
  16.7 5.0 %collective-permute-done.3.even_b_ref = bf16[4,288,128]{2,1,0:T(8,128)(2,1)S(1)} collective-permute-done((bf16[4,288,128]{2,1,0:T(8,128)(2,1)S(1)}, bf16[4,288,128]{2,1,0:T(8,128)(2,1)S(1)}, u32[]{:S(2)}, u32[]{:S(2)}) %collective-permute-start.3) | collective-permute-done | bytes 294944 | tf_op jit(solution)/shard_map/ppermute | solution.py:495
  21.7 0.0 collective-permute-start.4
  21.7 3.3 %shard_map.113 = (f32[8,128,128]{2,1,0:T(8,128)S(1)}, f32[8,128,128]{2,1,0:T(8,128)S(1)}, f32[8,128,128]{2,1,0:T(8,128)S(1)}, f32[8,128,128]{2,1,0:T(8,128)S(1)}, f32[8,128,128]{2,1,0:T(8,128)S(1)}) custom-call(bf16[288,128]{1,0:T(8,128)(2,1)S(1)} %shard_map.111.packed_ref, f32[8,12]{1,0:T(8,128)} %level_ref.1, bf16[128,1024]{1,0:T(8,128)(2,1)} %q_ref.7, ...), custom_call_target="tpu_custom_call" | custom-call | flops 536870912 | bytes 1048576 | tf_op jit(solution)/shard_map/pallas_call | solution.py:524
  25.0 0.0 copy-start.4
  25.0 0.0 copy-start.5
  25.0 0.0 copy-start.6
  25.0 0.0 collective-permute-done.2.odd_ref.odd_a_ref
  25.0 0.0 copy-done
  25.0 0.3 shard_map.112
  25.4 0.0 collective-permute-done.4.odd_b_ref
  25.4 0.3 copy-done.4
  25.7 0.0 copy-done.5
  25.7 0.0 copy-done.6
  25.7 0.0 copy-start.1
  25.7 0.0 copy-start.2
  25.7 0.0 copy-start.3
  25.7 2.5 %shard_map.114 = (f32[8,128,128]{2,1,0:T(8,128)S(1)}, f32[8,128,128]{2,1,0:T(8,128)S(1)}, f32[4,8,128,128]{3,2,1,0:T(8,128)S(1)}, f32[8,128,128]{2,1,0:T(8,128)S(1)}, f32[8,128]{1,0:T(8,128)S(1)}) custom-call(s32[1]{0:T(128)} %bitcast.span_ref, f32[8,12]{1,0:T(8,128)S(1)} %copy-done.6, bf16[128,1024]{1,0:T(8,128)(2,1)S(1)} %copy-done, ...), custom_call_target="tpu_custom_call" | custom-call | flops 2147483648 | bytes 1048576 | tf_op jit(solution)/shard_map/pallas_call | solution.py:558
  28.2 1.7 %collective-permute-start.5 = (f32[8,128]{1,0:T(8,128)S(1)}, f32[8,128]{1,0:T(8,128)S(1)}, u32[]{:S(2)}, u32[]{:S(2)}) collective-permute-start(f32[8,128]{1,0:T(8,128)S(1)} %get-tuple-element.34.sums_a_ref), channel_id=1, source_target_pairs={{0,1},{1,0},{2,3},{3,2},{4,5},{5,4},{6,7},{7,6},{8,9},{9,8},{10,11... | collective-permute-start | bytes 12296 | tf_op jit(solution)/shard_map/ppermute | solution.py:495
  29.9 1.9 %collective-permute-done.5.sums_b_ref = f32[8,128]{1,0:T(8,128)S(1)} collective-permute-done((f32[8,128]{1,0:T(8,128)S(1)}, f32[8,128]{1,0:T(8,128)S(1)}, u32[]{:S(2)}, u32[]{:S(2)}) %collective-permute-start.5) | collective-permute-done | bytes 4128 | tf_op jit(solution)/shard_map/ppermute | solution.py:495
  31.8 0.0 copy-done.1
  31.8 0.0 copy-done.2
  31.8 0.0 copy-done.3
  31.8 2.7 %shard_map.116 = (f32[520,128]{1,0:T(8,128)S(1)}, f32[520,128]{1,0:T(8,128)S(1)}) custom-call(s32[1]{0:T(128)} %bitcast.span_ref, f32[8,128]{1,0:T(8,128)S(1)} %get-tuple-element.34.sums_a_ref, f32[8,128]{1,0:T(8,128)S(1)} %collective-permute-done.5.sums_b_ref, f32[8,128]{1,0:T(8,128)S(1)} %copy-done.4, bf16[128,1024]{1,0:T(8,128)(2,1)S(1)} %copy-done, ...), custom_call_target="tpu_custom_call" | custom-call | flops 536870912 | bytes 1048576 | tf_op jit(solution)/shard_map/pallas_call | solution.py:588
  34.5 0.0 collective-permute-start.13
  34.5 2.7 %shard_map.115 = (f32[520,128]{1,0:T(8,128)S(1)}, f32[520,128]{1,0:T(8,128)S(1)}) custom-call(s32[1]{0:T(128)} %bitcast.span_ref, f32[8,128]{1,0:T(8,128)S(1)} %get-tuple-element.34.sums_a_ref, f32[8,128]{1,0:T(8,128)S(1)} %collective-permute-done.5.sums_b_ref, f32[8,128]{1,0:T(8,128)S(1)} %copy-done.4, bf16[128,1024]{1,0:T(8,128)(2,1)S(1)} %copy-done, ...), custom_call_target="tpu_custom_call" | custom-call | flops 536870912 | bytes 1048576 | tf_op jit(solution)/shard_map/pallas_call | solution.py:588
  37.3 0.5 collective-permute-start.6
  37.8 0.0 collective-permute-done.13
  37.8 3.7 %collective-permute-start.14 = (f32[264,128]{1,0:T(8,128)S(1)}, f32[264,128]{1,0:T(8,128)S(1)}, u32[]{:S(2)}, u32[]{:S(2)}) collective-permute-start(f32[264,128]{1,0:T(8,128)S(1)} %slice.90), channel_id=1, source_target_pairs={{0,8},{2,10},{4,12},{6,14},{8,0},{10,2},{12,4},{14,6},{16,24},{18,... | collective-permute-start | bytes 405512 | tf_op jit(solution)/shard_map/ppermute | solution.py:495
  41.5 0.0 collective-permute-done.6
  41.6 2.5 %collective-permute-start.7 = (f32[264,128]{1,0:T(8,128)S(1)}, f32[264,128]{1,0:T(8,128)S(1)}, u32[]{:S(2)}, u32[]{:S(2)}) collective-permute-start(f32[264,128]{1,0:T(8,128)S(1)} %slice.81), channel_id=1, source_target_pairs={{0,4},{2,6},{4,0},{6,2},{8,12},{10,14},{12,8},{14,10},{16,20},{18,... | collective-permute-start | bytes 405512 | tf_op jit(solution)/shard_map/ppermute | solution.py:495
  44.1 1.3 %collective-permute-done.14 = f32[264,128]{1,0:T(8,128)S(1)} collective-permute-done((f32[264,128]{1,0:T(8,128)S(1)}, f32[264,128]{1,0:T(8,128)S(1)}, u32[]{:S(2)}, u32[]{:S(2)}) %collective-permute-start.14) | collective-permute-done | bytes 135200 | tf_op jit(solution)/shard_map/ppermute | solution.py:495
  45.4 2.5 %collective-permute-start.15 = (f32[136,128]{1,0:T(8,128)S(1)}, f32[136,128]{1,0:T(8,128)S(1)}, u32[]{:S(2)}, u32[]{:S(2)}) collective-permute-start(f32[136,128]{1,0:T(8,128)S(1)} %pad_maximum_fusion.6), channel_id=1, source_target_pairs={{0,4},{2,6},{4,0},{6,2},{8,12},{10,14},{12,8},{14,10},{16,20},{18,... | collective-permute-start | bytes 208904 | tf_op jit(solution)/shard_map/ppermute | solution.py:495
  47.9 0.0 collective-permute-done.7
  47.9 1.8 %collective-permute-start.8 = (f32[136,128]{1,0:T(8,128)S(1)}, f32[136,128]{1,0:T(8,128)S(1)}, u32[]{:S(2)}, u32[]{:S(2)}) collective-permute-start(f32[136,128]{1,0:T(8,128)S(1)} %pad_maximum_fusion.7), channel_id=1, source_target_pairs={{0,8},{2,10},{4,12},{6,14},{8,0},{10,2},{12,4},{14,6},{16,24},{18,... | collective-permute-start | bytes 208904 | tf_op jit(solution)/shard_map/ppermute | solution.py:495
  49.7 0.4 collective-permute-done.15
  50.2 6.5 %collective-permute-start.16 = (f32[136,128]{1,0:T(8,128)S(1)}, f32[136,128]{1,0:T(8,128)S(1)}, u32[]{:S(2)}, u32[]{:S(2)}) collective-permute-start(f32[136,128]{1,0:T(8,128)S(1)} %pad_maximum_fusion.9), channel_id=1, source_target_pairs={{0,16},{2,18},{4,20},{6,22},{8,24},{10,26},{12,28},{14,30},{16,0},... | collective-permute-start | bytes 208904 | tf_op jit(solution)/shard_map/ppermute | solution.py:495
  56.7 0.0 collective-permute-done.8
  56.7 2.5 %collective-permute-start.9 = (f32[136,128]{1,0:T(8,128)S(1)}, f32[136,128]{1,0:T(8,128)S(1)}, u32[]{:S(2)}, u32[]{:S(2)}) collective-permute-start(f32[136,128]{1,0:T(8,128)S(1)} %pad_maximum_fusion.8), channel_id=1, source_target_pairs={{0,16},{2,18},{4,20},{6,22},{8,24},{10,26},{12,28},{14,30},{16,0},... | collective-permute-start | bytes 208904 | tf_op jit(solution)/shard_map/ppermute | solution.py:495
  59.2 0.1 collective-permute-done.16
  59.3 3.9 %collective-permute-start.17 = (f32[128,128]{1,0:T(8,128)S(1)}, f32[128,128]{1,0:T(8,128)S(1)}, u32[]{:S(2)}, u32[]{:S(2)}) collective-permute-start(f32[128,128]{1,0:T(8,128)S(1)} %slice.97), channel_id=1, source_target_pairs={{0,4},{2,6},{4,0},{6,2},{8,12},{10,14},{12,8},{14,10},{16,20},{18,... | collective-permute-start | bytes 196616 | tf_op jit(solution)/shard_map/ppermute | solution.py:495
  63.2 0.0 collective-permute-done.9
  63.2 0.6 collective-permute-start.10
  63.8 1.6 %collective-permute-done.17 = f32[128,128]{1,0:T(8,128)S(1)} collective-permute-done((f32[128,128]{1,0:T(8,128)S(1)}, f32[128,128]{1,0:T(8,128)S(1)}, u32[]{:S(2)}, u32[]{:S(2)}) %collective-permute-start.17) | collective-permute-done | bytes 65568 | tf_op jit(solution)/shard_map/ppermute | solution.py:495
  65.5 0.6 collective-permute-start.18
  66.1 1.5 %collective-permute-done.10 = f32[128,128]{1,0:T(8,128)S(1)} collective-permute-done((f32[128,128]{1,0:T(8,128)S(1)}, f32[128,128]{1,0:T(8,128)S(1)}, u32[]{:S(2)}, u32[]{:S(2)}) %collective-permute-start.10) | collective-permute-done | bytes 65568 | tf_op jit(solution)/shard_map/ppermute | solution.py:495
  67.6 1.2 %collective-permute-start.11 = (f32[256,128]{1,0:T(8,128)S(1)}, f32[256,128]{1,0:T(8,128)S(1)}, u32[]{:S(2)}, u32[]{:S(2)}) collective-permute-start(f32[256,128]{1,0:T(8,128)S(1)} %pad_maximum_fusion.4), channel_id=1, source_target_pairs={{0,4},{2,6},{4,0},{6,2},{8,12},{10,14},{12,8},{14,10},{16,20},{18,... | collective-permute-start | bytes 393224 | tf_op jit(solution)/shard_map/ppermute | solution.py:495
  68.8 1.7 %collective-permute-done.18 = f32[256,128]{1,0:T(8,128)S(1)} collective-permute-done((f32[256,128]{1,0:T(8,128)S(1)}, f32[256,128]{1,0:T(8,128)S(1)}, u32[]{:S(2)}, u32[]{:S(2)}) %collective-permute-start.18) | collective-permute-done | bytes 131104 | tf_op jit(solution)/shard_map/ppermute | solution.py:495
  70.5 0.1 collective-permute-start.19
  70.6 2.0 %collective-permute-done.11 = f32[256,128]{1,0:T(8,128)S(1)} collective-permute-done((f32[256,128]{1,0:T(8,128)S(1)}, f32[256,128]{1,0:T(8,128)S(1)}, u32[]{:S(2)}, u32[]{:S(2)}) %collective-permute-start.11) | collective-permute-done | bytes 131104 | tf_op jit(solution)/shard_map/ppermute | solution.py:495
  72.6 0.1 collective-permute-start.12
  72.7 0.0 collective-permute-done.19.refs_4_
  72.7 1.5 %collective-permute-done.12.refs_1_ = f32[512,128]{1,0:T(8,128)S(1)} collective-permute-done((f32[512,128]{1,0:T(8,128)S(1)}, f32[512,128]{1,0:T(8,128)S(1)}, u32[]{:S(2)}, u32[]{:S(2)}) %collective-permute-start.12) | collective-permute-done | bytes 262176 | tf_op jit(solution)/shard_map/ppermute | solution.py:495
  74.2 1.0 %shard_map.117 = (f32[8,128,128]{2,1,0:T(8,128)}, f32[8,128,128]{2,1,0:T(8,128)}, f32[8,12]{1,0:T(8,128)}, f32[8,128]{1,0:T(8,128)}) custom-call(s32[1]{0:T(128)} %bitcast.span_ref, f32[512,128]{1,0:T(8,128)S(1)} %pad_maximum_fusion.1.refs_0_, f32[512,128]{1,0:T(8,128)S(1)} %collective-permute-done.12.refs_1_, f32[136,128]{1,0:T(8,128)S(1)} %fusion.1.refs_2_, ...), custom_call_target="tpu_custom_call" | custom-call | flops 1048576 | bytes 1048576 | tf_op jit(solution)/shard_map/pallas_call | solution.py:622
  (26 shorter events, 0.3 us)
Async XLA Ops:
  0.6 24.4 %copy-start = (bf16[128,1024]{1,0:T(8,128)(2,1)S(1)}, bf16[128,1024]{1,0:T(8,128)(2,1)}, u32[]{:S(2)}) copy-start(bf16[128,1024]{1,0:T(8,128)(2,1)} %q_ref.7) | copy-start | bytes 786436
  1.6 8.0 %collective-permute-start = (bf16[1,288,128]{2,1,0:T(8,128)(2,1)S(1)}, bf16[1,288,128]{2,1,0:T(8,128)(2,1)S(1)}, u32[]{:S(2)}, u32[]{:S(2)}) collective-permute-start(bf16[1,288,128]{2,1,0:T(8,128)(2,1)S(1)} %bitcast.4), channel_id=1, source_target_pairs={{0,16},{2,18},{4,20},{6,22},{8,24},{10,26},{12,28},{14,30},{16,0},... | collective-permute-start | bytes 221192 | tf_op jit(solution)/shard_map/ppermute | solution.py:495
  9.7 5.2 %collective-permute-start.1 = (bf16[2,288,128]{2,1,0:T(8,128)(2,1)S(1)}, bf16[2,288,128]{2,1,0:T(8,128)(2,1)S(1)}, u32[]{:S(2)}, u32[]{:S(2)}) collective-permute-start(bf16[2,288,128]{2,1,0:T(8,128)(2,1)S(1)} %pad_maximum_fusion.3), channel_id=1, source_target_pairs={{0,8},{2,10},{4,12},{6,14},{8,0},{10,2},{12,4},{14,6},{16,24},{18,... | collective-permute-start | bytes 442376 | tf_op jit(solution)/shard_map/ppermute | solution.py:495
  14.9 6.8 %collective-permute-start.3 = (bf16[4,288,128]{2,1,0:T(8,128)(2,1)S(1)}, bf16[4,288,128]{2,1,0:T(8,128)(2,1)S(1)}, u32[]{:S(2)}, u32[]{:S(2)}) collective-permute-start(bf16[4,288,128]{2,1,0:T(8,128)(2,1)S(1)} %pad_maximum_fusion.even_ref.even_a_ref), channel_id=1, source_target_pairs={{0,4},{2,6},{4,0},{6,2},{8,12},{10,14},{12,8},{14,10},{16,20},{18,... | collective-permute-start | bytes 884744 | tf_op jit(solution)/shard_map/ppermute | solution.py:495
  16.7 8.3 %collective-permute-start.2 = (bf16[4,288,128]{2,1,0:T(8,128)(2,1)S(1)}, bf16[4,288,128]{2,1,0:T(8,128)(2,1)S(1)}, u32[]{:S(2)}, u32[]{:S(2)}) collective-permute-start(bf16[4,288,128]{2,1,0:T(8,128)(2,1)S(1)} %pad_maximum_fusion.even_ref.even_a_ref), channel_id=1, source_target_pairs={{0,2},{2,0},{4,6},{6,4},{8,10},{10,8},{12,14},{14,12},{16,18},{18,... | collective-permute-start | bytes 884744 | tf_op jit(solution)/shard_map/ppermute | solution.py:495
  21.7 3.7 %collective-permute-start.4 = (bf16[4,288,128]{2,1,0:T(8,128)(2,1)S(1)}, bf16[4,288,128]{2,1,0:T(8,128)(2,1)S(1)}, u32[]{:S(2)}, u32[]{:S(2)}) collective-permute-start(bf16[4,288,128]{2,1,0:T(8,128)(2,1)S(1)} %collective-permute-done.3.even_b_ref), channel_id=1, source_target_pairs={{0,2},{2,0},{4,6},{6,4},{8,10},{10,8},{12,14},{14,12},{16,18},{18,... | collective-permute-start | bytes 884744 | tf_op jit(solution)/shard_map/ppermute | solution.py:495
  25.0 0.7 copy-start.4
  25.0 0.7 copy-start.5
  25.0 0.7 copy-start.6
  25.7 6.1 %copy-start.1 = (f32[8,128,128]{2,1,0:T(8,128)S(1)}, f32[8,128,128]{2,1,0:T(8,128)}, u32[]{:S(2)}) copy-start(f32[8,128,128]{2,1,0:T(8,128)} %kmap_ref.3) | copy-start | bytes 1572868
  25.7 6.1 %copy-start.2 = (bf16[128,128]{1,0:T(8,128)(2,1)S(1)}, bf16[128,128]{1,0:T(8,128)(2,1)}, u32[]{:S(2)}) copy-start(bf16[128,128]{1,0:T(8,128)(2,1)} %k_ref.3) | copy-start | bytes 98308
  25.7 6.1 %copy-start.3 = (bf16[128,128]{1,0:T(8,128)(2,1)S(1)}, bf16[128,128]{1,0:T(8,128)(2,1)}, u32[]{:S(2)}) copy-start(bf16[128,128]{1,0:T(8,128)(2,1)} %v_ref.3) | copy-start | bytes 98308
  28.2 3.6 %collective-permute-start.5 = (f32[8,128]{1,0:T(8,128)S(1)}, f32[8,128]{1,0:T(8,128)S(1)}, u32[]{:S(2)}, u32[]{:S(2)}) collective-permute-start(f32[8,128]{1,0:T(8,128)S(1)} %get-tuple-element.34.sums_a_ref), channel_id=1, source_target_pairs={{0,1},{1,0},{2,3},{3,2},{4,5},{5,4},{6,7},{7,6},{8,9},{9,8},{10,11... | collective-permute-start | bytes 12296 | tf_op jit(solution)/shard_map/ppermute | solution.py:495
  34.5 3.3 %collective-permute-start.13 = (f32[520,128]{1,0:T(8,128)S(1)}, f32[520,128]{1,0:T(8,128)S(1)}, u32[]{:S(2)}, u32[]{:S(2)}) collective-permute-start(f32[520,128]{1,0:T(8,128)S(1)} %get-tuple-element.45), channel_id=1, source_target_pairs={{0,2},{2,0},{4,6},{6,4},{8,10},{10,8},{12,14},{14,12},{16,18},{18,... | collective-permute-start | bytes 798728 | tf_op jit(solution)/shard_map/ppermute | solution.py:495
  37.3 4.3 %collective-permute-start.6 = (f32[520,128]{1,0:T(8,128)S(1)}, f32[520,128]{1,0:T(8,128)S(1)}, u32[]{:S(2)}, u32[]{:S(2)}) collective-permute-start(f32[520,128]{1,0:T(8,128)S(1)} %get-tuple-element.43), channel_id=1, source_target_pairs={{0,2},{2,0},{4,6},{6,4},{8,10},{10,8},{12,14},{14,12},{16,18},{18,... | collective-permute-start | bytes 798728 | tf_op jit(solution)/shard_map/ppermute | solution.py:495
  37.8 7.5 %collective-permute-start.14 = (f32[264,128]{1,0:T(8,128)S(1)}, f32[264,128]{1,0:T(8,128)S(1)}, u32[]{:S(2)}, u32[]{:S(2)}) collective-permute-start(f32[264,128]{1,0:T(8,128)S(1)} %slice.90), channel_id=1, source_target_pairs={{0,8},{2,10},{4,12},{6,14},{8,0},{10,2},{12,4},{14,6},{16,24},{18,... | collective-permute-start | bytes 405512 | tf_op jit(solution)/shard_map/ppermute | solution.py:495
  41.6 6.3 %collective-permute-start.7 = (f32[264,128]{1,0:T(8,128)S(1)}, f32[264,128]{1,0:T(8,128)S(1)}, u32[]{:S(2)}, u32[]{:S(2)}) collective-permute-start(f32[264,128]{1,0:T(8,128)S(1)} %slice.81), channel_id=1, source_target_pairs={{0,4},{2,6},{4,0},{6,2},{8,12},{10,14},{12,8},{14,10},{16,20},{18,... | collective-permute-start | bytes 405512 | tf_op jit(solution)/shard_map/ppermute | solution.py:495
  45.4 4.8 %collective-permute-start.15 = (f32[136,128]{1,0:T(8,128)S(1)}, f32[136,128]{1,0:T(8,128)S(1)}, u32[]{:S(2)}, u32[]{:S(2)}) collective-permute-start(f32[136,128]{1,0:T(8,128)S(1)} %pad_maximum_fusion.6), channel_id=1, source_target_pairs={{0,4},{2,6},{4,0},{6,2},{8,12},{10,14},{12,8},{14,10},{16,20},{18,... | collective-permute-start | bytes 208904 | tf_op jit(solution)/shard_map/ppermute | solution.py:495
  47.9 8.7 %collective-permute-start.8 = (f32[136,128]{1,0:T(8,128)S(1)}, f32[136,128]{1,0:T(8,128)S(1)}, u32[]{:S(2)}, u32[]{:S(2)}) collective-permute-start(f32[136,128]{1,0:T(8,128)S(1)} %pad_maximum_fusion.7), channel_id=1, source_target_pairs={{0,8},{2,10},{4,12},{6,14},{8,0},{10,2},{12,4},{14,6},{16,24},{18,... | collective-permute-start | bytes 208904 | tf_op jit(solution)/shard_map/ppermute | solution.py:495
  50.2 9.1 %collective-permute-start.16 = (f32[136,128]{1,0:T(8,128)S(1)}, f32[136,128]{1,0:T(8,128)S(1)}, u32[]{:S(2)}, u32[]{:S(2)}) collective-permute-start(f32[136,128]{1,0:T(8,128)S(1)} %pad_maximum_fusion.9), channel_id=1, source_target_pairs={{0,16},{2,18},{4,20},{6,22},{8,24},{10,26},{12,28},{14,30},{16,0},... | collective-permute-start | bytes 208904 | tf_op jit(solution)/shard_map/ppermute | solution.py:495
  56.7 6.5 %collective-permute-start.9 = (f32[136,128]{1,0:T(8,128)S(1)}, f32[136,128]{1,0:T(8,128)S(1)}, u32[]{:S(2)}, u32[]{:S(2)}) collective-permute-start(f32[136,128]{1,0:T(8,128)S(1)} %pad_maximum_fusion.8), channel_id=1, source_target_pairs={{0,16},{2,18},{4,20},{6,22},{8,24},{10,26},{12,28},{14,30},{16,0},... | collective-permute-start | bytes 208904 | tf_op jit(solution)/shard_map/ppermute | solution.py:495
  59.3 6.1 %collective-permute-start.17 = (f32[128,128]{1,0:T(8,128)S(1)}, f32[128,128]{1,0:T(8,128)S(1)}, u32[]{:S(2)}, u32[]{:S(2)}) collective-permute-start(f32[128,128]{1,0:T(8,128)S(1)} %slice.97), channel_id=1, source_target_pairs={{0,4},{2,6},{4,0},{6,2},{8,12},{10,14},{12,8},{14,10},{16,20},{18,... | collective-permute-start | bytes 196616 | tf_op jit(solution)/shard_map/ppermute | solution.py:495
  63.2 4.3 %collective-permute-start.10 = (f32[128,128]{1,0:T(8,128)S(1)}, f32[128,128]{1,0:T(8,128)S(1)}, u32[]{:S(2)}, u32[]{:S(2)}) collective-permute-start(f32[128,128]{1,0:T(8,128)S(1)} %slice.88), channel_id=1, source_target_pairs={{0,8},{2,10},{4,12},{6,14},{8,0},{10,2},{12,4},{14,6},{16,24},{18,... | collective-permute-start | bytes 196616 | tf_op jit(solution)/shard_map/ppermute | solution.py:495
  65.5 5.0 %collective-permute-start.18 = (f32[256,128]{1,0:T(8,128)S(1)}, f32[256,128]{1,0:T(8,128)S(1)}, u32[]{:S(2)}, u32[]{:S(2)}) collective-permute-start(f32[256,128]{1,0:T(8,128)S(1)} %pad_maximum_fusion.5), channel_id=1, source_target_pairs={{0,8},{2,10},{4,12},{6,14},{8,0},{10,2},{12,4},{14,6},{16,24},{18,... | collective-permute-start | bytes 393224 | tf_op jit(solution)/shard_map/ppermute | solution.py:495
  67.6 5.0 %collective-permute-start.11 = (f32[256,128]{1,0:T(8,128)S(1)}, f32[256,128]{1,0:T(8,128)S(1)}, u32[]{:S(2)}, u32[]{:S(2)}) collective-permute-start(f32[256,128]{1,0:T(8,128)S(1)} %pad_maximum_fusion.4), channel_id=1, source_target_pairs={{0,4},{2,6},{4,0},{6,2},{8,12},{10,14},{12,8},{14,10},{16,20},{18,... | collective-permute-start | bytes 393224 | tf_op jit(solution)/shard_map/ppermute | solution.py:495
  70.5 2.2 %collective-permute-start.19 = (f32[512,128]{1,0:T(8,128)S(1)}, f32[512,128]{1,0:T(8,128)S(1)}, u32[]{:S(2)}, u32[]{:S(2)}) collective-permute-start(f32[512,128]{1,0:T(8,128)S(1)} %pad_maximum_fusion.2.refs_3_), channel_id=1, source_target_pairs={{0,2},{2,0},{4,6},{6,4},{8,10},{10,8},{12,14},{14,12},{16,18},{18,... | collective-permute-start | bytes 786440 | tf_op jit(solution)/shard_map/ppermute | solution.py:495
  72.6 1.6 %collective-permute-start.12 = (f32[512,128]{1,0:T(8,128)S(1)}, f32[512,128]{1,0:T(8,128)S(1)}, u32[]{:S(2)}, u32[]{:S(2)}) collective-permute-start(f32[512,128]{1,0:T(8,128)S(1)} %pad_maximum_fusion.1.refs_0_), channel_id=1, source_target_pairs={{0,2},{2,0},{4,6},{6,4},{8,10},{10,8},{12,14},{14,12},{16,18},{18,... | collective-permute-start | bytes 786440 | tf_op jit(solution)/shard_map/ppermute | solution.py:495

commit v2 on v1

--- a/solution.py
+++ b/solution.py
@@ -16,7 +16,6 @@
 NN = (((1,), (0,)), ((), ()))
 NT = (((1,), (1,)), ((), ()))
 TN = (((0,), (0,)), ((), ()))
-GATE_ROWS = 32
 PARTS = 2
 
 
@@ -69,32 +68,39 @@
 
 def pack_kernel(k_hbm, v_hbm, gate_hbm, out_ref, k_ref, v_ref, gate_ref, sems):
     fetch(sems, (k_hbm, k_ref), (v_hbm, v_ref), (gate_hbm, gate_ref))
-    rows = k_ref.shape[0]
-    heads = gate_ref.shape[0]
-    out_ref[0:rows, :] = k_ref[...].astype(F32).T.astype(BF16)
-    out_ref[rows : 2 * rows, :] = v_ref[...]
+    half = k_ref.shape[0] // 2
     gate = gate_ref[...]
     high = gate.astype(BF16).astype(F32)
     middle = (gate - high).astype(BF16).astype(F32)
-    low = gate - high - middle
-    blank = jnp.zeros((GATE_ROWS - 3 * heads, gate.shape[1]), F32)
-    out_ref[2 * rows :, :] = jnp.concatenate([high, middle, low, blank], axis=0).astype(BF16)
+    gates = jnp.concatenate([high, middle, gate - high - middle], axis=0).astype(BF16)
+    for part in range(2):
+        tokens = slice(part * half, (part + 1) * half)
+        out_ref[part, 0, 0:half, :] = k_ref[tokens, :]
+        out_ref[part, 0, half : 2 * half, :] = v_ref[tokens, :]
+        out_ref[part, 0, 2 * half :, :] = gates
+
+
+def gates_of(piece):
+    heads = piece.shape[0] // 3
+    piece = piece.astype(F32)
+    return piece[0:heads] + piece[heads : 2 * heads] + piece[2 * heads : 3 * heads]
 
 
 def local_kernel(
-    packed_ref, level_hbm, q_hbm, qmap_hbm, kmap_hbm, qp_ref, qt_ref, sd_ref, mix_ref, loc_ref,
+    packed_ref, level_hbm, q_hbm, qmap_hbm, kmap_hbm, qp_ref, qt_ref, sd_ref, mix_ref, loc_ref, entry_ref, rows_ref,
     q_ref, qmap_ref, kmap_ref, level_ref, sems,
 ):
     fetch(sems, (q_hbm, q_ref), (qmap_hbm, qmap_ref), (kmap_hbm, kmap_ref), (level_hbm, level_ref))
     heads, dim, _ = qmap_ref.shape
-    width, rows = packed_ref.shape
+    rows = q_ref.shape[0]
+    half = rows // 2
     low_bits = rows.bit_length() - 1
-    piece = packed_ref[width - GATE_ROWS :, :].astype(F32)
-    gate = piece[0:heads] + piece[heads : 2 * heads] + piece[2 * heads : 3 * heads]
-    cum = exact_dot(gate, upper_ones(rows))
+    cum = exact_dot(gates_of(packed_ref[0, 0, rows:, :]), upper_ones(rows))
     cum_t = cum.T
-    kt = packed_ref[0:rows, :]
-    v = packed_ref[rows : 2 * rows, :]
+    entry_ref[...] = jnp.exp(cum_t)
+    rows_ref[...] = stacked_queries(q_ref, dim)
+    k = jnp.concatenate([packed_ref[0, 0, 0:half, :], packed_ref[1, 0, 0:half, :]], axis=0)
+    v = jnp.concatenate([packed_ref[0, 0, half:rows, :], packed_ref[1, 0, half:rows, :]], axis=0)
     row, col = iota2((rows, rows), 0), iota2((rows, rows), 1)
     causal = col <= row
     differ = row ^ col
@@ -107,7 +113,7 @@
         high, low = halves(qt)
         highs.append(high)
         lows.append(low)
-    score = dot_left((jnp.concatenate(highs, axis=0), jnp.concatenate(lows, axis=0)), kt)
+    score = dot_left((jnp.concatenate(highs, axis=0), jnp.concatenate(lows, axis=0)), k, NT)
     highs, lows = [], []
     for h in range(heads):
         decay = jnp.exp(jnp.where(causal, cum_t[:, h : h + 1] - cum[h : h + 1, :], NEGATIVE))
@@ -129,133 +135,162 @@
     return jnp.concatenate([q_ref[:, at : at + dim] for at in range(0, q_ref.shape[1], dim)], axis=0)
 
 
-def pair_decay(span, even_ref, odd_ref, heads):
-    pairs, width, rows = even_ref.shape
+def unit_decay(span, evens, odds):
     gates = []
-    for ref in (even_ref, odd_ref):
-        for p in range(pairs):
-            piece = ref[p, width - GATE_ROWS :, :].astype(F32)
-            gates.append(piece[0:heads] + piece[heads : 2 * heads] + piece[2 * heads : 3 * heads])
+    for ref in (*evens, *odds):
+        for p in range(ref.shape[0]):
+            gates.append(gates_of(ref[p, ref.shape[2] :, :]))
+    rows = gates[0].shape[1]
     cum = exact_dot(jnp.concatenate(gates, axis=0), upper_ones(rows))
-    cum_e, cum_o = cum[: pairs * heads], cum[pairs * heads :]
-    end_e = jnp.broadcast_to(cum_e[:, rows - 1 : rows], cum_e.shape)
-    end_o = jnp.broadcast_to(cum_o[:, rows - 1 : rows], cum_o.shape)
+    end = jnp.broadcast_to(cum[:, rows - 1 : rows], cum.shape)
+    size = cum.shape[0] // 4
     odd_span = (span & 1) == 1
-    decay_e = jnp.exp(end_e - cum_e + jnp.where(odd_span, 0.0, end_o))
-    decay_o = jnp.exp(end_o - cum_o + jnp.where(odd_span, end_e, 0.0))
-    return cum_e, cum_o, end_e, end_o, decay_e, decay_o
-
-
-def pair_blocks(even_ref, odd_ref, p, rows):
-    kt = jnp.concatenate([even_ref[p, 0:rows, :], odd_ref[p, 0:rows, :]], axis=1)
-    v = jnp.concatenate([even_ref[p, rows : 2 * rows, :], odd_ref[p, rows : 2 * rows, :]], axis=0)
-    return kt, v
-
-
-def pair_state(kt, v, weight, state_ref, p):
+    units, nexts = [], []
+    left = iota2((size, rows), 1) < rows // 2
+    for part in range(2):
+        e, o = slice(part * size, (part + 1) * size), slice((part + 2) * size, (part + 3) * size)
+        decay_e = jnp.exp(end[e] - cum[e] + jnp.where(odd_span, 0.0, end[o]))
+        decay_o = jnp.exp(end[o] - cum[o] + jnp.where(odd_span, end[e], 0.0))
+        alone = jnp.exp(end[o] - cum[o])
+        if part == 0:
+            decay_o, alone = pltpu.roll(decay_o, rows // 2, 1), pltpu.roll(alone, rows // 2, 1)
+        else:
+            decay_e = pltpu.roll(decay_e, rows // 2, 1)
+        units.append(jnp.where(left, decay_e, decay_o))
+        nexts.append(jnp.where(left, 0.0, alone))
+    return units, nexts, end[0:size] + end[2 * size : 3 * size], end[2 * size : 3 * size]
+
+
+def unit_block(even_ref, odd_ref, p):
+    half = even_ref.shape[2] // 2
+    k = jnp.concatenate([even_ref[p, 0:half, :], odd_ref[p, 0:half, :]], axis=0)
+    v = jnp.concatenate([even_ref[p, half : 2 * half, :], odd_ref[p, half : 2 * half, :]], axis=0)
+    return k.astype(F32).T, v
+
+
+def unit_values(even_ref, odd_ref, p):
+    half = even_ref.shape[2] // 2
+    return [even_ref[p, half : 2 * half, :], odd_ref[p, half : 2 * half, :]]
+
+
+def pair_state(kt, v, weight, state_ref, i):
     heads = weight.shape[0]
     dim = kt.shape[0]
-    kt32 = kt.astype(F32)
     highs, lows = [], []
     for h in range(heads):
-        high, low = halves(kt32 * weight[h : h + 1, :])
+        high, low = halves(kt * weight[h : h + 1, :])
         highs.append(high)
         lows.append(low)
     state = dot_left((jnp.concatenate(highs, axis=0), jnp.concatenate(lows, axis=0)), v)
     for h in range(heads):
-        state_ref[p, h] = state[h * dim : (h + 1) * dim]
-
-
-def by_level(offsets):
+        state_ref[i, h] = state[h * dim : (h + 1) * dim]
+
+
+def pairs_of(offsets):
+    table = {}
+    for part, row in enumerate(offsets):
+        for p, offset in enumerate(row):
+            table.setdefault(offset, []).append((part, p))
+    return sorted(table.items())
+
+
+def by_level(table):
     levels = {}
-    for p, offset in enumerate(offsets):
-        if p > 0:
-            levels.setdefault(offset.bit_length() - 1, []).append(p)
+    for i, (offset, units) in enumerate(table):
+        if offset:
+            levels.setdefault(offset.bit_length() - 1, []).append((i, units))
     return sorted(levels.items())
 
 
+def take_level(group, q_all, evens, odds, weights, score_ref, peak_ref, state_ref):
+    heads = q_all.shape[0] // evens[0].shape[2]
+    count = evens[0].shape[0]
+    scale = q_all.shape[1] ** (-0.5)
+    blocks = {unit: unit_block(evens[unit[0]], odds[unit[0]], unit[1]) for _, units in group for unit in units}
+    top = peak_ref[...]
+    names = list(blocks)
+    for at in range(0, len(names), 2):
+        both = names[at : at + 2]
+        keys = jnp.concatenate([blocks[unit][0].astype(BF16) for unit in both], axis=1)
+        score = dot(q_all, keys) * scale
+        for i, (part, p) in enumerate(both):
+            one = score[:, i * (score.shape[1] // len(both)) : (i + 1) * (score.shape[1] // len(both))]
+            score_ref[part * count + p] = one
+            top = jnp.maximum(top, one)
+    peak_ref[...] = top
+    for i, units in group:
+        kt = jnp.concatenate([blocks[unit][0] for unit in units], axis=1)
+        v = jnp.concatenate([blocks[unit][1] for unit in units], axis=0)
+        weight = jnp.concatenate([weights[part][p * heads : (p + 1) * heads] for part, p in units], axis=1)
+        pair_state(kt, v, weight, state_ref, i)
+
+
 def early_kernel(
-    span_ref, q_ref, even_ref, odd_ref, score_ref, peak_ref, state_ref, ends_ref, before_ref, decay_scr, *, offsets,
+    span_ref, q_ref, even_a_ref, odd_a_ref, even_b_ref, odd_b_ref,
+    score_ref, peak_ref, state_ref, ends_ref, before_ref, *, offsets,
 ):
-    pairs, heads, dim, _ = state_ref.shape
-    rows = even_ref.shape[2]
+    _, heads, dim, _ = state_ref.shape
+    rows = even_a_ref.shape[2]
     span = span_ref[0]
-    _, cum_o, end_e, end_o, decay_e, decay_o = pair_decay(span, even_ref, odd_ref, heads)
-    ends_ref[...] = end_e + end_o
-    before_ref[...] = end_o[0:heads]
-    for p in range(pairs):
-        at = slice(p * heads, (p + 1) * heads)
-        if p == 0:
-            first = jnp.concatenate([jnp.zeros_like(decay_e[at]), jnp.exp(end_o[at] - cum_o[at])], axis=1)
-            decay_scr[p] = first
-        else:
-            decay_scr[p] = jnp.concatenate([decay_e[at], decay_o[at]], axis=1)
-    q_all = stacked_queries(q_ref, dim)
-    scale = dim ** (-0.5)
+    evens, odds = (even_a_ref, even_b_ref), (odd_a_ref, odd_b_ref)
+    weights, nexts, ends, later = unit_decay(span, evens, odds)
+    ends_ref[...] = ends
+    before_ref[...] = later[0:heads]
+    q_all = q_ref[...]
+    count = even_a_ref.shape[0]
+    table = pairs_of(offsets)
+    odd_span = (span & 1) == 1
     row, col = iota2((rows, 2 * rows), 0), iota2((rows, 2 * rows), 1)
-    odd_span = (span & 1) == 1
-    seen = (col <= row) | ((col >= rows) & odd_span)
-    kt, v = pair_blocks(even_ref, odd_ref, 0, rows)
-    score = dot(q_all, kt) * scale
+    place = col % rows
+    token = place + (col // rows) * (rows // 2)
+    seen = ((place < rows // 2) & (token <= row)) | ((place >= rows // 2) & odd_span)
+    blocks = [unit_block(evens[part], odds[part], 0) for part in range(2)]
+    kt = jnp.concatenate([kt for kt, _ in blocks], axis=1)
+    score = dot(q_all, kt.astype(BF16)) * dim ** (-0.5)
     score = jnp.where(jnp.concatenate([seen] * heads, axis=0), score, NEGATIVE)
-    score_ref[0] = score
+    score_ref[0] = score[:, :rows]
+    score_ref[count] = score[:, rows:]
     peak_ref[...] = jnp.maximum(score[:, :rows], score[:, rows:])
 
     @pl.when(odd_span)
     def _():
-        pair_state(kt, v, decay_scr[0], state_ref, 0)
-
-    for bit, members in by_level(offsets[:pairs]):
+        v = jnp.concatenate([v for _, v in blocks], axis=0)
+        pair_state(kt, v, jnp.concatenate([nexts[0][0:heads], nexts[1][0:heads]], axis=1), state_ref, 0)
+
+    for bit, group in by_level(table):
 
         @pl.when(((span >> bit) & 1) == 1)
-        def _(members=members):
-            top = peak_ref[...]
-            blocks = [pair_blocks(even_ref, odd_ref, p, rows) for p in members]
-            for p, (kt, _) in zip(members, blocks):
-                score = dot(q_all, kt) * scale
-                score_ref[p] = score
-                top = jnp.maximum(top, jnp.maximum(score[:, :rows], score[:, rows:]))
-            peak_ref[...] = top
-            for p, (kt, v) in zip(members, blocks):
-                pair_state(kt, v, decay_scr[p], state_ref, p)
+        def _(group=group):
+            take_level(group, q_all, evens, odds, weights, score_ref, peak_ref, state_ref)
 
 
 def forward_kernel(
-    span_ref, level_ref, q_ref, even_a_ref, odd_a_ref, even_b_ref, odd_b_ref, score_a_ref, peak_a_ref, state_a_ref,
-    ends_a_ref, before_ref, qt_ref, loc_ref, gain_ref, gate_ref,
+    span_ref, level_ref, q_ref, ea_ref, oa_ref, eb_ref, ob_ref, late_ea_ref, late_oa_ref, late_eb_ref, late_ob_ref,
+    score_a_ref, peak_a_ref, state_a_ref, ends_a_ref, before_ref, qt_ref, loc_ref, gain_ref, entry_ref,
     raw_ref, target_ref, level_state_ref, comb_ref, sums_ref,
-    score_scr, peak_scr, state_scr, total_scr, acc_scr, *, offsets,
+    score_scr, peak_scr, state_scr, total_scr, acc_scr, *, early, late,
 ):
     heads, rows, dim = qt_ref.shape
-    early, late = even_a_ref.shape[0], even_b_ref.shape[0]
-    pairs = early + late
+    count = ea_ref.shape[0]
+    offsets = early[0] + late[0]
+    pairs = len(offsets)
     span_bits = level_state_ref.shape[0]
     low_bits = rows.bit_length() - 1
     span = span_ref[0]
     odd_span = (span & 1) == 1
-    scale = dim ** (-0.5)
-    q_all = stacked_queries(q_ref, dim)
-    _, _, end_e, end_o, decay_e, decay_o = pair_decay(span, even_b_ref, odd_b_ref, heads)
+    q_all = q_ref[...]
+    early_refs = ((ea_ref, eb_ref), (oa_ref, ob_ref))
+    late_refs = ((late_ea_ref, late_eb_ref), (late_oa_ref, late_ob_ref))
+    early_table, late_table = pairs_of(early), pairs_of(late)
+    weights, _, ends_b, _ = unit_decay(span, *late_refs)
     peak_scr[...] = peak_a_ref[...]
-    for bit, members in by_level(offsets):
-        members = [p - early for p in members if p >= early]
-        if not members:
-            continue
+    for bit, group in by_level(late_table):
 
         @pl.when(((span >> bit) & 1) == 1)
-        def _(members=members):
-            top = peak_scr[...]
-            blocks = [pair_blocks(even_b_ref, odd_b_ref, p, rows) for p in members]
-            for p, (kt, _) in zip(members, blocks):
-                score = dot(q_all, kt) * scale
-                score_scr[p] = score
-                top = jnp.maximum(top, jnp.maximum(score[:, :rows], score[:, rows:]))
-            peak_scr[...] = top
-            for p, (kt, v) in zip(members, blocks):
-                at = slice(p * heads, (p + 1) * heads)
-                pair_state(kt, v, jnp.concatenate([decay_e[at], decay_o[at]], axis=1), state_scr, p)
-
-    ends = jnp.concatenate([ends_a_ref[...], end_e + end_o], axis=0)
+        def _(group=group):
+            take_level(group, q_all, *late_refs, weights, score_scr, peak_scr, state_scr)
+
+    ends = jnp.concatenate([ends_a_ref[...], ends_b], axis=0)
     size = pairs * heads
 
     def pair_of(index):
@@ -275,42 +310,48 @@
     peak = jnp.max(peak_scr[...], axis=1, keepdims=True)
     peak_scr[...] = jnp.broadcast_to(peak, peak_scr.shape)
 
-    def weigh(members):
+    def weigh(early_units, late_units):
         top = peak_scr[...]
-        total, weights, values = None, [], []
-        for p in members:
-            if p < early:
-                score, v = score_a_ref[p], pair_blocks(even_a_ref, odd_a_ref, p, rows)[1]
-            else:
-                score, v = score_scr[p - early], pair_blocks(even_b_ref, odd_b_ref, p - early, rows)[1]
-            left = jnp.exp(score[:, :rows] - top)
-            right = jnp.exp(score[:, rows:] - top)
-            total = left + right if total is None else total + (left + right)
-            weights += [left.astype(BF16), right.astype(BF16)]
-            values.append(v)
-        return total, dot(jnp.concatenate(weights, axis=1), jnp.concatenate(values, axis=0))
-
-    total_scr[...], acc_scr[...] = weigh([0])
-    for bit, members in by_level(offsets):
+        total, parts, values = None, [], []
+        for units, refs, score_ref in ((early_units, early_refs, score_a_ref), (late_units, late_refs, score_scr)):
+            for part, p in units:
+                weight = jnp.exp(score_ref[part * count + p] - top)
+                total = weight if total is None else total + weight
+                parts.append(weight.astype(BF16))
+                values += unit_values(refs[0][part], refs[1][part], p)
+        return total, dot(jnp.concatenate(parts, axis=1), jnp.concatenate(values, axis=0))
+
+    total_scr[...], acc_scr[...] = weigh([(0, 0), (1, 0)], [])
+    early_levels, late_levels = dict(by_level(early_table)), dict(by_level(late_table))
+    for bit in sorted({*early_levels, *late_levels}):
 
         @pl.when(((span >> bit) & 1) == 1)
-        def _(members=members):
-            total, acc = weigh(members)
+        def _(bit=bit):
+            total, acc = weigh(
+                [unit for _, units in early_levels.get(bit, []) for unit in units],
+                [unit for _, units in late_levels.get(bit, []) for unit in units],
+            )
             total_scr[...] += total
             acc_scr[...] += acc
 
     for level in range(span_bits):
-        members = [p for p in range(pairs) if max(offsets[p], 1).bit_length() - 1 == level]
         used = ((span >> level) & 1) == 1
+        members = [
+            (ref, i, offset)
+            for ref, table in ((state_a_ref, early_table), (state_scr, late_table))
+            for i, (offset, _) in enumerate(table)
+            if max(offset, 1).bit_length() - 1 == level
+        ]
 
         @pl.when(used)
         def _(members=members, level=level):
             for h in range(heads):
                 value = None
-                for p in members:
-                    state = state_a_ref[p, h] if p < early else state_scr[p - early, h]
-                    if p > 0:
-                        state = state * factor[p * heads + h : p * heads + h + 1, :]
+                for ref, i, offset in members:
+                    state = ref[i, h]
+                    if offset:
+                        at = offsets.index(offset) * heads + h
+                        state = state * factor[at : at + 1, :]
                     value = state if value is None else value + state
                 level_state_ref[level, h] = value
 
@@ -320,7 +361,7 @@
 
     total = jnp.sum(total_scr[...], axis=1, keepdims=True)
     target_all = acc_scr[...] / total
-    entry = jnp.exp(exact_dot(gate_ref[...], upper_ones(rows)).T)
+    entry = entry_ref[...]
     squares = jnp.zeros((rows, dim), F32)
     gained = jnp.zeros((rows, dim), F32)
     crossed = jnp.zeros((rows, dim), F32)
@@ -363,7 +404,7 @@
 
 
 def backward_kernel(
-    span_ref, sums_a_ref, sums_b_ref, gate_ref, q_ref, k_ref, v_ref, kmap_ref, gain_ref,
+    span_ref, sums_a_ref, sums_b_ref, entry_ref, q_ref, k_ref, v_ref, kmap_ref, gain_ref,
     qp_ref, qt_ref, sd_ref, mix_ref, raw_ref, target_ref, state_ref, comb_ref,
     keep_ref, send_ref, *, norm_width, total_tokens, splits, heads,
 ):
@@ -378,7 +419,7 @@
     inverse = lax.rsqrt(squares / norm_width + EPSILON)
     inner = (inverse * gained - crossed) / total_tokens
     shrink = inverse * inverse * inverse * inner / norm_width
-    entry = jnp.exp(exact_dot(gate_ref[...], upper_ones(rows)).T)
+    entry = entry_ref[...]
     k = k_ref[...]
     v = v_ref[...]
     row, col = iota2((rows, rows), 0), iota2((rows, rows), 1)
@@ -417,7 +458,7 @@
         d_qt = halves(d_local[i * rows : (i + 1) * rows] + dot_f32(lead, halves(comb_ref[h]), NT))
         grad_k = dot_f32(d_qt, halves(qp_ref[h]), TN)
         d_qp = dot_f32(d_qt, halves(kmap_ref[h]))
-        grad_q = dot_right(q_ref[:, h * dim : (h + 1) * dim], halves(d_qp), TN)
+        grad_q = dot_right(q_ref[h * rows : (h + 1) * rows, :], halves(d_qp), TN)
         d_comb = dot_f32(halves(qt_ref[h]), lead, TN)
         for level in range(span_bits):
             level_rows[i].append(jnp.sum(state_ref[level, h] * d_comb, axis=0, keepdims=True))
@@ -508,21 +549,24 @@
     strides = [1 << bit for bit in reversed(range(1, span_bits))]
     orders = [(2, 4), (4, 2)]
     cube = (heads, dim, dim)
-    packed_rows = 2 * rows + GATE_ROWS
-
+    packed_rows = rows + 3 * heads
+
+    shared, (far, near) = strides[:-2], strides[-2:]
     offsets = [0]
-    for stride in strides:
+    for stride in shared:
         offsets += [offset + stride for offset in offsets]
-    early = len(offsets) // 2
-
-    packed = call(pack_kernel, hbm(3), shape(packed_rows, rows, dtype=BF16), 8, 1 << 20, scratch=[
+    early = [offsets + [offset + turn for offset in offsets] for turn in (far, near)]
+    late = [[offset + turn for offset in row] for row, turn in zip(early, (near, far))]
+    count_early = len(early[0])
+
+    packed = call(pack_kernel, hbm(3), shape(2, 1, packed_rows, dim, dtype=BF16), 8, 1 << 20, scratch=[
         pltpu.VMEM((rows, dim), BF16),
         pltpu.VMEM((rows, dim), BF16),
         pltpu.VMEM((heads, rows), F32),
         pltpu.SemaphoreType.DMA((3,)),
     ])(*in_hbm(key_vectors, value_vectors, log_gate))
-    qp, qt, score_decay, mix, local = call(
-        local_kernel, vmem(1) + hbm(4), [shape(*cube)] * 5, 24, 1 << 29,
+    qp, qt, score_decay, mix, local, entry, stacked = call(
+        local_kernel, vmem(1) + hbm(4), [shape(*cube)] * 5 + [shape(rows, heads), shape(heads * rows, dim, dtype=BF16)], 24, 1 << 29,
         scratch=[
             pltpu.VMEM(queries.shape, BF16),
             pltpu.VMEM(cube, F32),
@@ -532,46 +576,51 @@
         ],
     )(packed, *in_hbm(level_weight, queries, query_map, key_map))
 
-    even_a = packed[None]
-    for stride in strides[:-1]:
-        received = swap(even_a, "seq", stride)
-        even_a = jnp.concatenate([even_a, received], axis=0)
-    even_b = swap(even_a, "seq", strides[-1])
-    odd_a = swap(even_a, "seq", 1)
-    odd_b = swap(even_b, "seq", 1)
+    held = packed
+    for stride in shared:
+        received = swap(held, "seq", stride)
+        held = jnp.concatenate([held, received], axis=1)
+    evens, odds = [], []
+    for part, turn in enumerate((far, near)):
+        evens.append(jnp.concatenate([held[part], swap(held[part], "seq", turn)], axis=0))
+    for part, turn in enumerate((near, far)):
+        evens.append(swap(evens[part], "seq", turn))
+        odds.append(swap(evens[part], "seq", 1))
+    for part in range(2):
+        odds.append(swap(evens[2 + part], "seq", 1))
+    blocks = [value for pair in zip(evens, odds) for value in pair]
 
     scores, peaks, states, ends, before = call(
         early_kernel,
-        smem(1) + vmem(3),
+        smem(1) + vmem(5),
         [
-            shape(early, heads * rows, 2 * rows),
+            shape(2 * count_early, heads * rows, rows),
             shape(heads * rows, rows),
-            shape(early, *cube),
-            shape(early * heads, rows),
+            shape(len(pairs_of(early)), *cube),
+            shape(count_early * heads, rows),
             shape(heads, rows),
         ],
         24,
         1 << 30,
-        scratch=[pltpu.VMEM((early, heads, 2 * rows), F32)],
-        offsets=tuple(offsets),
-    )(span, queries, even_a, odd_a)
+        offsets=early,
+    )(span, stacked, *blocks[:4])
     raw, target, level_states, combined, sums = call(
         forward_kernel,
-        smem(2) + vmem(14),
+        smem(2) + vmem(18),
         [shape(*cube), shape(*cube), shape(span_bits, *cube), shape(*cube), shape(8, rows)],
         32,
         1 << 31,
         scratch=[
-            pltpu.VMEM((early, heads * rows, 2 * rows), F32),
+            pltpu.VMEM((2 * count_early, heads * rows, rows), F32),
             pltpu.VMEM((heads * rows, rows), F32),
-            pltpu.VMEM((early, *cube), F32),
+            pltpu.VMEM((len(pairs_of(late)), *cube), F32),
             pltpu.VMEM((heads * rows, rows), F32),
             pltpu.VMEM((heads * rows, dim), F32),
         ],
-        offsets=tuple(offsets),
+        early=early,
+        late=late,
     )(
-        span, level_weight, queries, even_a, odd_a, even_b, odd_b, scores, peaks, states, ends, before,
-        qt, local, gain, log_gate,
+        span, level_weight, stacked, *blocks, scores, peaks, states, ends, before, qt, local, gain, entry,
     )
 
     stride = 1
@@ -596,7 +645,7 @@
             splits=orders[part],
             heads=range(part * share, (part + 1) * share),
         )(
-            span, sums, received, log_gate, queries, key_vectors, value_vectors, key_map, gain,
+            span, sums, received, entry, stacked, key_vectors, value_vectors, key_map, gain,
             qp, qt, score_decay, mix, raw, target, level_states, combined,
         )
         held.append(keep + swap(send, "seq", 1))

time: 75.5 us -> 73 us (0.967)
  waiting for transfers between devices: 25.5 us -> 24.1 us
    ppermute x20 -> x24, waiting for transfers between devices: 25.5 us -> 24.1 us  [swap(): return lax.ppermute(value, axis, [(i, i ^ stride) for i in range(count)])]
    ppermute x20 -> x24, starting transfers between devices: 34.7 us -> 34.1 us  [swap(): return lax.ppermute(value, axis, [(i, i ^ stride) for i in range(count)])]
  transfers between devices with their start and end apart: 20 -> 24, of which waited for: 12 -> 13; matrix products, arithmetic and copies ran while one was open for 0% -> 0% of each run, Pallas kernels for 8% -> 9%
where the time goes in v2:
time: 73 us; the launch traced here: 72.7 us
  starting transfers between devices  34.1 us (47%)
  waiting for transfers between devices  24.1 us (33%)
  Pallas kernels  13.2 us (18%)
  between operations  0.92 us (1%)
    ppermute x24, starting transfers between devices, swap(): return lax.ppermute(value, axis, [(i, i ^ stride) for i in range(count)])  34.1 us
    ppermute x24, waiting for transfers between devices, swap(): return lax.ppermute(value, axis, [(i, i ^ stride) for i in range(count)])  24.1 us
    pallas_call x2, Pallas kernels, on_device(): call(backward_kernel, smem(1) + vmem(16), [shape(share * (dim + 2), dim)]...  5.21 us
    pallas_call x1, Pallas kernels, on_device(): call(local_kernel, vmem(1) + hbm(4), [shape(*cube)] * 5 + [shape(rows, he...  3.3 us
    pallas_call x1, Pallas kernels, on_device(): call(forward_kernel, smem(2) + vmem(18), [shape(*cube), shape(*cube), sha...  2.44 us
  transfers between devices with their start and end apart: 24, of which 13 were waited for; matrix products, arithmetic and copies ran while one was open for 0% of the time, Pallas kernels for 9%

profile of v2, /device:TPU:0, one launch (start us, length us, event | category | flops | bytes accessed | tf_op | source)
XLA Modules:
  0.0 72.7 jit_solution(3101405617271668837)
XLA Ops:
  0.6 0.8 %shard_map.111.packed_ref = bf16[2,1,152,128]{3,2,1,0:T(8,128)(2,1)S(1)} custom-call(bf16[128,128]{1,0:T(8,128)(2,1)} %k_ref.3, bf16[128,128]{1,0:T(8,128)(2,1)} %v_ref.3, f32[8,128]{1,0:T(8,128)} %gate_hbm.1), custom_call_target="tpu_custom_call" | custom-call | flops 1048576 | bytes 1048576 | tf_op jit(solution)/shard_map/pallas_call | solution.py:562
  1.5 4.1 %collective-permute-start = (bf16[2,1,152,128]{3,2,1,0:T(8,128)(2,1)S(1)}, bf16[2,1,152,128]{3,2,1,0:T(8,128)(2,1)S(1)}, u32[]{:S(2)}, u32[]{:S(2)}) collective-permute-start(bf16[2,1,152,128]{3,2,1,0:T(8,128)(2,1)S(1)} %shard_map.111.packed_ref), channel_id=1, source_target_pairs={{0,16},{2,18},{4,20},{6,22},{8,24},{10,26},{12,28},{14,30},{16,0},... | collective-permute-start | bytes 233480 | tf_op jit(solution)/shard_map/ppermute | solution.py:536
  5.6 4.0 %collective-permute-done = bf16[2,1,152,128]{3,2,1,0:T(8,128)(2,1)S(1)} collective-permute-done((bf16[2,1,152,128]{3,2,1,0:T(8,128)(2,1)S(1)}, bf16[2,1,152,128]{3,2,1,0:T(8,128)(2,1)S(1)}, u32[]{:S(2)}, u32[]{:S(2)}) %collective-permute-start) | collective-permute-done | bytes 77856 | tf_op jit(solution)/shard_map/ppermute | solution.py:536
  9.6 0.8 %collective-permute-start.1 = (bf16[2,152,128]{2,1,0:T(8,128)(2,1)S(1)}, bf16[2,152,128]{2,1,0:T(8,128)(2,1)S(1)}, u32[]{:S(2)}, u32[]{:S(2)}) collective-permute-start(bf16[2,152,128]{2,1,0:T(8,128)(2,1)S(1)} %get-tuple-element.55), channel_id=1, source_target_pairs={{0,8},{2,10},{4,12},{6,14},{8,0},{10,2},{12,4},{14,6},{16,24},{18,... | collective-permute-start | bytes 233480 | tf_op jit(solution)/shard_map/ppermute | solution.py:536
  10.4 1.5 %collective-permute-start.3 = (bf16[2,152,128]{2,1,0:T(8,128)(2,1)S(1)}, bf16[2,152,128]{2,1,0:T(8,128)(2,1)S(1)}, u32[]{:S(2)}, u32[]{:S(2)}) collective-permute-start(bf16[2,152,128]{2,1,0:T(8,128)(2,1)S(1)} %get-tuple-element.54), channel_id=1, source_target_pairs={{0,4},{2,6},{4,0},{6,2},{8,12},{10,14},{12,8},{14,10},{16,20},{18,... | collective-permute-start | bytes 233480 | tf_op jit(solution)/shard_map/ppermute | solution.py:536
  11.9 2.2 %collective-permute-done.1 = bf16[2,152,128]{2,1,0:T(8,128)(2,1)S(1)} collective-permute-done((bf16[2,152,128]{2,1,0:T(8,128)(2,1)S(1)}, bf16[2,152,128]{2,1,0:T(8,128)(2,1)S(1)}, u32[]{:S(2)}, u32[]{:S(2)}) %collective-permute-start.1) | collective-permute-done | bytes 77856 | tf_op jit(solution)/shard_map/ppermute | solution.py:536
  14.1 0.0 copy-start.3
  14.1 0.0 copy-start.4
  14.2 1.8 %collective-permute-start.5 = (bf16[4,152,128]{2,1,0:T(8,128)(2,1)S(1)}, bf16[4,152,128]{2,1,0:T(8,128)(2,1)S(1)}, u32[]{:S(2)}, u32[]{:S(2)}) collective-permute-start(bf16[4,152,128]{2,1,0:T(8,128)(2,1)S(1)} %pad_maximum_fusion.2.even_a_ref.ea_ref), channel_id=1, source_target_pairs={{0,4},{2,6},{4,0},{6,2},{8,12},{10,14},{12,8},{14,10},{16,20},{18,... | collective-permute-start | bytes 466952 | tf_op jit(solution)/shard_map/ppermute | solution.py:536
  15.9 0.0 collective-permute-done.3
  16.0 0.6 collective-permute-start.7
  16.5 0.0 collective-permute-start.2
  16.5 0.5 collective-permute-start.4
  17.0 2.4 %collective-permute-done.5.late_ea_ref = bf16[4,152,128]{2,1,0:T(8,128)(2,1)S(1)} collective-permute-done((bf16[4,152,128]{2,1,0:T(8,128)(2,1)S(1)}, bf16[4,152,128]{2,1,0:T(8,128)(2,1)S(1)}, u32[]{:S(2)}, u32[]{:S(2)}) %collective-permute-start.5) | collective-permute-done | bytes 155680 | tf_op jit(solution)/shard_map/ppermute | solution.py:536
  19.5 0.0 collective-permute-start.6
  19.5 1.8 %collective-permute-done.7.late_eb_ref = bf16[4,152,128]{2,1,0:T(8,128)(2,1)S(1)} collective-permute-done((bf16[4,152,128]{2,1,0:T(8,128)(2,1)S(1)}, bf16[4,152,128]{2,1,0:T(8,128)(2,1)S(1)}, u32[]{:S(2)}, u32[]{:S(2)}) %collective-permute-start.7) | collective-permute-done | bytes 155680 | tf_op jit(solution)/shard_map/ppermute | solution.py:536
  21.3 0.0 collective-permute-start.8
  21.3 3.3 %shard_map.112 = (f32[8,128,128]{2,1,0:T(8,128)S(1)}, f32[8,128,128]{2,1,0:T(8,128)S(1)}, f32[8,128,128]{2,1,0:T(8,128)S(1)}, f32[8,128,128]{2,1,0:T(8,128)S(1)}...) custom-call(bf16[2,1,152,128]{3,2,1,0:T(8,128)(2,1)S(1)} %shard_map.111.packed_ref, ...), custom_call_target="tpu_custom_call" | custom-call | flops 536870912 | bytes 1048576 | tf_op jit(solution)/shard_map/pallas_call | solution.py:568
  24.6 0.0 collective-permute-done.2.odd_a_ref.oa_ref
  24.6 0.0 collective-permute-done.4.odd_b_ref.ob_ref
  24.6 0.4 shard_map.113
  25.0 0.0 collective-permute-done.6.late_oa_ref
  25.1 0.0 collective-permute-done.8.late_ob_ref
  25.1 0.0 copy-done.3
  25.1 0.0 copy-done.4
  25.1 0.0 copy-start
  25.1 0.0 copy-start.1
  25.1 0.0 copy-start.2
  25.1 2.4 %shard_map.114 = (f32[8,128,128]{2,1,0:T(8,128)S(1)}, f32[8,128,128]{2,1,0:T(8,128)S(1)}, f32[4,8,128,128]{3,2,1,0:T(8,128)S(1)}, f32[8,128,128]{2,1,0:T(8,128)S(1)}, f32[8,128]{1,0:T(8,128)S(1)}) custom-call(s32[1]{0:T(128)} %bitcast.span_ref, f32[8,12]{1,0:T(8,128)S(1)} %copy-done.4, bf16[1024,128]{1,0:T(8,128)(2,1)S(1)} %get-tuple-element.29.q_ref, ...), custom_call_target="tpu_custom_call" | custom-call | flops 2147483648 | bytes 1048576 | tf_op jit(solution)/shard_map/pallas_call | solution.py:607
  27.6 1.5 %collective-permute-start.9 = (f32[8,128]{1,0:T(8,128)S(1)}, f32[8,128]{1,0:T(8,128)S(1)}, u32[]{:S(2)}, u32[]{:S(2)}) collective-permute-start(f32[8,128]{1,0:T(8,128)S(1)} %get-tuple-element.38.sums_a_ref), channel_id=1, source_target_pairs={{0,1},{1,0},{2,3},{3,2},{4,5},{5,4},{6,7},{7,6},{8,9},{9,8},{10,11... | collective-permute-start | bytes 12296 | tf_op jit(solution)/shard_map/ppermute | solution.py:536
  29.1 2.1 %collective-permute-done.9.sums_b_ref = f32[8,128]{1,0:T(8,128)S(1)} collective-permute-done((f32[8,128]{1,0:T(8,128)S(1)}, f32[8,128]{1,0:T(8,128)S(1)}, u32[]{:S(2)}, u32[]{:S(2)}) %collective-permute-start.9) | collective-permute-done | bytes 4128 | tf_op jit(solution)/shard_map/ppermute | solution.py:536
  31.2 0.0 copy-done
  31.2 0.0 copy-done.1
  31.2 2.6 %shard_map.116 = (f32[520,128]{1,0:T(8,128)S(1)}, f32[520,128]{1,0:T(8,128)S(1)}) custom-call(s32[1]{0:T(128)} %bitcast.span_ref, f32[8,128]{1,0:T(8,128)S(1)} %get-tuple-element.38.sums_a_ref, f32[8,128]{1,0:T(8,128)S(1)} %collective-permute-done.9.sums_b_ref, f32[128,8]{1,0:T(8,128)S(1)} %get-tuple-element.37.entry_ref, ...), custom_call_target="tpu_custom_call" | custom-call | flops 536870912 | bytes 1048576 | tf_op jit(solution)/shard_map/pallas_call | solution.py:637
  33.8 0.0 collective-permute-start.17
  33.8 2.6 %shard_map.115 = (f32[520,128]{1,0:T(8,128)S(1)}, f32[520,128]{1,0:T(8,128)S(1)}) custom-call(s32[1]{0:T(128)} %bitcast.span_ref, f32[8,128]{1,0:T(8,128)S(1)} %get-tuple-element.38.sums_a_ref, f32[8,128]{1,0:T(8,128)S(1)} %collective-permute-done.9.sums_b_ref, f32[128,8]{1,0:T(8,128)S(1)} %get-tuple-element.37.entry_ref, ...), custom_call_target="tpu_custom_call" | custom-call | flops 536870912 | bytes 1048576 | tf_op jit(solution)/shard_map/pallas_call | solution.py:637
  36.4 0.5 collective-permute-start.10
  37.0 0.0 collective-permute-done.17
  37.0 2.4 %collective-permute-start.18 = (f32[264,128]{1,0:T(8,128)S(1)}, f32[264,128]{1,0:T(8,128)S(1)}, u32[]{:S(2)}, u32[]{:S(2)}) collective-permute-start(f32[264,128]{1,0:T(8,128)S(1)} %slice.102), channel_id=1, source_target_pairs={{0,8},{2,10},{4,12},{6,14},{8,0},{10,2},{12,4},{14,6},{16,24},{18,... | collective-permute-start | bytes 405512 | tf_op jit(solution)/shard_map/ppermute | solution.py:536
  39.5 0.0 collective-permute-done.10
  39.5 2.9 %collective-permute-start.11 = (f32[264,128]{1,0:T(8,128)S(1)}, f32[264,128]{1,0:T(8,128)S(1)}, u32[]{:S(2)}, u32[]{:S(2)}) collective-permute-start(f32[264,128]{1,0:T(8,128)S(1)} %slice.93), channel_id=1, source_target_pairs={{0,4},{2,6},{4,0},{6,2},{8,12},{10,14},{12,8},{14,10},{16,20},{18,... | collective-permute-start | bytes 405512 | tf_op jit(solution)/shard_map/ppermute | solution.py:536
  42.4 0.8 %collective-permute-done.18 = f32[264,128]{1,0:T(8,128)S(1)} collective-permute-done((f32[264,128]{1,0:T(8,128)S(1)}, f32[264,128]{1,0:T(8,128)S(1)}, u32[]{:S(2)}, u32[]{:S(2)}) %collective-permute-start.18) | collective-permute-done | bytes 135200 | tf_op jit(solution)/shard_map/ppermute | solution.py:536
  43.3 2.9 %collective-permute-start.19 = (f32[136,128]{1,0:T(8,128)S(1)}, f32[136,128]{1,0:T(8,128)S(1)}, u32[]{:S(2)}, u32[]{:S(2)}) collective-permute-start(f32[136,128]{1,0:T(8,128)S(1)} %pad_maximum_fusion.7), channel_id=1, source_target_pairs={{0,4},{2,6},{4,0},{6,2},{8,12},{10,14},{12,8},{14,10},{16,20},{18,... | collective-permute-start | bytes 208904 | tf_op jit(solution)/shard_map/ppermute | solution.py:536
  46.2 0.0 collective-permute-done.11
  46.2 1.8 %collective-permute-start.12 = (f32[136,128]{1,0:T(8,128)S(1)}, f32[136,128]{1,0:T(8,128)S(1)}, u32[]{:S(2)}, u32[]{:S(2)}) collective-permute-start(f32[136,128]{1,0:T(8,128)S(1)} %pad_maximum_fusion.8), channel_id=1, source_target_pairs={{0,8},{2,10},{4,12},{6,14},{8,0},{10,2},{12,4},{14,6},{16,24},{18,... | collective-permute-start | bytes 208904 | tf_op jit(solution)/shard_map/ppermute | solution.py:536
  48.0 0.4 collective-permute-done.19
  48.5 5.9 %collective-permute-start.20 = (f32[136,128]{1,0:T(8,128)S(1)}, f32[136,128]{1,0:T(8,128)S(1)}, u32[]{:S(2)}, u32[]{:S(2)}) collective-permute-start(f32[136,128]{1,0:T(8,128)S(1)} %pad_maximum_fusion.10), channel_id=1, source_target_pairs={{0,16},{2,18},{4,20},{6,22},{8,24},{10,26},{12,28},{14,30},{16,0},... | collective-permute-start | bytes 208904 | tf_op jit(solution)/shard_map/ppermute | solution.py:536
  54.4 0.0 collective-permute-done.12
  54.4 2.3 %collective-permute-start.13 = (f32[136,128]{1,0:T(8,128)S(1)}, f32[136,128]{1,0:T(8,128)S(1)}, u32[]{:S(2)}, u32[]{:S(2)}) collective-permute-start(f32[136,128]{1,0:T(8,128)S(1)} %pad_maximum_fusion.9), channel_id=1, source_target_pairs={{0,16},{2,18},{4,20},{6,22},{8,24},{10,26},{12,28},{14,30},{16,0},... | collective-permute-start | bytes 208904 | tf_op jit(solution)/shard_map/ppermute | solution.py:536
  56.7 2.1 %collective-permute-done.20 = f32[136,128]{1,0:T(8,128)S(1)} collective-permute-done((f32[136,128]{1,0:T(8,128)S(1)}, f32[136,128]{1,0:T(8,128)S(1)}, u32[]{:S(2)}, u32[]{:S(2)}) %collective-permute-start.20) | collective-permute-done | bytes 69664 | tf_op jit(solution)/shard_map/ppermute | solution.py:536
  58.8 1.9 %collective-permute-start.21 = (f32[128,128]{1,0:T(8,128)S(1)}, f32[128,128]{1,0:T(8,128)S(1)}, u32[]{:S(2)}, u32[]{:S(2)}) collective-permute-start(f32[128,128]{1,0:T(8,128)S(1)} %slice.109), channel_id=1, source_target_pairs={{0,4},{2,6},{4,0},{6,2},{8,12},{10,14},{12,8},{14,10},{16,20},{18,... | collective-permute-start | bytes 196616 | tf_op jit(solution)/shard_map/ppermute | solution.py:536
  60.7 0.0 collective-permute-done.13
  60.7 0.9 %collective-permute-start.14 = (f32[128,128]{1,0:T(8,128)S(1)}, f32[128,128]{1,0:T(8,128)S(1)}, u32[]{:S(2)}, u32[]{:S(2)}) collective-permute-start(f32[128,128]{1,0:T(8,128)S(1)} %slice.100), channel_id=1, source_target_pairs={{0,8},{2,10},{4,12},{6,14},{8,0},{10,2},{12,4},{14,6},{16,24},{18,... | collective-permute-start | bytes 196616 | tf_op jit(solution)/shard_map/ppermute | solution.py:536
  61.6 1.6 %collective-permute-done.21 = f32[128,128]{1,0:T(8,128)S(1)} collective-permute-done((f32[128,128]{1,0:T(8,128)S(1)}, f32[128,128]{1,0:T(8,128)S(1)}, u32[]{:S(2)}, u32[]{:S(2)}) %collective-permute-start.21) | collective-permute-done | bytes 65568 | tf_op jit(solution)/shard_map/ppermute | solution.py:536
  63.1 0.5 collective-permute-start.22
  63.6 1.4 %collective-permute-done.14 = f32[128,128]{1,0:T(8,128)S(1)} collective-permute-done((f32[128,128]{1,0:T(8,128)S(1)}, f32[128,128]{1,0:T(8,128)S(1)}, u32[]{:S(2)}, u32[]{:S(2)}) %collective-permute-start.14) | collective-permute-done | bytes 65568 | tf_op jit(solution)/shard_map/ppermute | solution.py:536
  65.0 1.2 %collective-permute-start.15 = (f32[256,128]{1,0:T(8,128)S(1)}, f32[256,128]{1,0:T(8,128)S(1)}, u32[]{:S(2)}, u32[]{:S(2)}) collective-permute-start(f32[256,128]{1,0:T(8,128)S(1)} %pad_maximum_fusion.4), channel_id=1, source_target_pairs={{0,4},{2,6},{4,0},{6,2},{8,12},{10,14},{12,8},{14,10},{16,20},{18,... | collective-permute-start | bytes 393224 | tf_op jit(solution)/shard_map/ppermute | solution.py:536
  66.3 1.9 %collective-permute-done.22 = f32[256,128]{1,0:T(8,128)S(1)} collective-permute-done((f32[256,128]{1,0:T(8,128)S(1)}, f32[256,128]{1,0:T(8,128)S(1)}, u32[]{:S(2)}, u32[]{:S(2)}) %collective-permute-start.22) | collective-permute-done | bytes 131104 | tf_op jit(solution)/shard_map/ppermute | solution.py:536
  68.2 0.1 collective-permute-start.23
  68.3 1.8 %collective-permute-done.15 = f32[256,128]{1,0:T(8,128)S(1)} collective-permute-done((f32[256,128]{1,0:T(8,128)S(1)}, f32[256,128]{1,0:T(8,128)S(1)}, u32[]{:S(2)}, u32[]{:S(2)}) %collective-permute-start.15) | collective-permute-done | bytes 131104 | tf_op jit(solution)/shard_map/ppermute | solution.py:536
  70.1 0.1 collective-permute-start.16
  70.2 0.0 collective-permute-done.23.refs_4_
  70.2 1.5 %collective-permute-done.16.refs_1_ = f32[512,128]{1,0:T(8,128)S(1)} collective-permute-done((f32[512,128]{1,0:T(8,128)S(1)}, f32[512,128]{1,0:T(8,128)S(1)}, u32[]{:S(2)}, u32[]{:S(2)}) %collective-permute-start.16) | collective-permute-done | bytes 262176 | tf_op jit(solution)/shard_map/ppermute | solution.py:536
  71.7 1.0 %shard_map.117 = (f32[8,128,128]{2,1,0:T(8,128)}, f32[8,128,128]{2,1,0:T(8,128)}, f32[8,12]{1,0:T(8,128)}, f32[8,128]{1,0:T(8,128)}) custom-call(s32[1]{0:T(128)} %bitcast.span_ref, f32[512,128]{1,0:T(8,128)S(1)} %pad_maximum_fusion.refs_0_, f32[512,128]{1,0:T(8,128)S(1)} %collective-permute-done.16.refs_1_, f32[136,128]{1,0:T(8,128)S(1)} %fusion.4.refs_2_, ...), custom_call_target="tpu_custom_call" | custom-call | flops 1048576 | bytes 1048576 | tf_op jit(solution)/shard_map/pallas_call | solution.py:671
  (28 shorter events, 0.3 us)
Async XLA Ops:
  1.5 8.2 %collective-permute-start = (bf16[2,1,152,128]{3,2,1,0:T(8,128)(2,1)S(1)}, bf16[2,1,152,128]{3,2,1,0:T(8,128)(2,1)S(1)}, u32[]{:S(2)}, u32[]{:S(2)}) collective-permute-start(bf16[2,1,152,128]{3,2,1,0:T(8,128)(2,1)S(1)} %shard_map.111.packed_ref), channel_id=1, source_target_pairs={{0,16},{2,18},{4,20},{6,22},{8,24},{10,26},{12,28},{14,30},{16,0},... | collective-permute-start | bytes 233480 | tf_op jit(solution)/shard_map/ppermute | solution.py:536
  9.6 4.5 %collective-permute-start.1 = (bf16[2,152,128]{2,1,0:T(8,128)(2,1)S(1)}, bf16[2,152,128]{2,1,0:T(8,128)(2,1)S(1)}, u32[]{:S(2)}, u32[]{:S(2)}) collective-permute-start(bf16[2,152,128]{2,1,0:T(8,128)(2,1)S(1)} %get-tuple-element.55), channel_id=1, source_target_pairs={{0,8},{2,10},{4,12},{6,14},{8,0},{10,2},{12,4},{14,6},{16,24},{18,... | collective-permute-start | bytes 233480 | tf_op jit(solution)/shard_map/ppermute | solution.py:536
  10.4 5.5 %collective-permute-start.3 = (bf16[2,152,128]{2,1,0:T(8,128)(2,1)S(1)}, bf16[2,152,128]{2,1,0:T(8,128)(2,1)S(1)}, u32[]{:S(2)}, u32[]{:S(2)}) collective-permute-start(bf16[2,152,128]{2,1,0:T(8,128)(2,1)S(1)} %get-tuple-element.54), channel_id=1, source_target_pairs={{0,4},{2,6},{4,0},{6,2},{8,12},{10,14},{12,8},{14,10},{16,20},{18,... | collective-permute-start | bytes 233480 | tf_op jit(solution)/shard_map/ppermute | solution.py:536
  14.1 10.9 %copy-start.3 = (f32[1024]{0:T(1024)S(1)}, f32[1024]{0:T(1024)}, u32[]{:S(2)}) copy-start(f32[1024]{0:T(1024)} %param.15) | copy-start | bytes 12292
  14.1 10.9 %copy-start.4 = (f32[8,12]{1,0:T(8,128)S(1)}, f32[8,12]{1,0:T(8,128)}, u32[]{:S(2)}) copy-start(f32[8,12]{1,0:T(8,128)} %level_ref.1) | copy-start | bytes 1156
  14.2 5.3 %collective-permute-start.5 = (bf16[4,152,128]{2,1,0:T(8,128)(2,1)S(1)}, bf16[4,152,128]{2,1,0:T(8,128)(2,1)S(1)}, u32[]{:S(2)}, u32[]{:S(2)}) collective-permute-start(bf16[4,152,128]{2,1,0:T(8,128)(2,1)S(1)} %pad_maximum_fusion.2.even_a_ref.ea_ref), channel_id=1, source_target_pairs={{0,4},{2,6},{4,0},{6,2},{8,12},{10,14},{12,8},{14,10},{16,20},{18,... | collective-permute-start | bytes 466952 | tf_op jit(solution)/shard_map/ppermute | solution.py:536
  16.0 5.3 %collective-permute-start.7 = (bf16[4,152,128]{2,1,0:T(8,128)(2,1)S(1)}, bf16[4,152,128]{2,1,0:T(8,128)(2,1)S(1)}, u32[]{:S(2)}, u32[]{:S(2)}) collective-permute-start(bf16[4,152,128]{2,1,0:T(8,128)(2,1)S(1)} %pad_maximum_fusion.3.even_b_ref.eb_ref), channel_id=1, source_target_pairs={{0,8},{2,10},{4,12},{6,14},{8,0},{10,2},{12,4},{14,6},{16,24},{18,... | collective-permute-start | bytes 466952 | tf_op jit(solution)/shard_map/ppermute | solution.py:536
  16.5 8.0 %collective-permute-start.2 = (bf16[4,152,128]{2,1,0:T(8,128)(2,1)S(1)}, bf16[4,152,128]{2,1,0:T(8,128)(2,1)S(1)}, u32[]{:S(2)}, u32[]{:S(2)}) collective-permute-start(bf16[4,152,128]{2,1,0:T(8,128)(2,1)S(1)} %pad_maximum_fusion.2.even_a_ref.ea_ref), channel_id=1, source_target_pairs={{0,2},{2,0},{4,6},{6,4},{8,10},{10,8},{12,14},{14,12},{16,18},{18,... | collective-permute-start | bytes 466952 | tf_op jit(solution)/shard_map/ppermute | solution.py:536
  16.5 8.1 %collective-permute-start.4 = (bf16[4,152,128]{2,1,0:T(8,128)(2,1)S(1)}, bf16[4,152,128]{2,1,0:T(8,128)(2,1)S(1)}, u32[]{:S(2)}, u32[]{:S(2)}) collective-permute-start(bf16[4,152,128]{2,1,0:T(8,128)(2,1)S(1)} %pad_maximum_fusion.3.even_b_ref.eb_ref), channel_id=1, source_target_pairs={{0,2},{2,0},{4,6},{6,4},{8,10},{10,8},{12,14},{14,12},{16,18},{18,... | collective-permute-start | bytes 466952 | tf_op jit(solution)/shard_map/ppermute | solution.py:536
  19.5 5.6 %collective-permute-start.6 = (bf16[4,152,128]{2,1,0:T(8,128)(2,1)S(1)}, bf16[4,152,128]{2,1,0:T(8,128)(2,1)S(1)}, u32[]{:S(2)}, u32[]{:S(2)}) collective-permute-start(bf16[4,152,128]{2,1,0:T(8,128)(2,1)S(1)} %collective-permute-done.5.late_ea_ref), channel_id=1, source_target_pairs={{0,2},{2,0},{4,6},{6,4},{8,10},{10,8},{12,14},{14,12},{16,18},{18,... | collective-permute-start | bytes 466952 | tf_op jit(solution)/shard_map/ppermute | solution.py:536
  21.3 3.8 %collective-permute-start.8 = (bf16[4,152,128]{2,1,0:T(8,128)(2,1)S(1)}, bf16[4,152,128]{2,1,0:T(8,128)(2,1)S(1)}, u32[]{:S(2)}, u32[]{:S(2)}) collective-permute-start(bf16[4,152,128]{2,1,0:T(8,128)(2,1)S(1)} %collective-permute-done.7.late_eb_ref), channel_id=1, source_target_pairs={{0,2},{2,0},{4,6},{6,4},{8,10},{10,8},{12,14},{14,12},{16,18},{18,... | collective-permute-start | bytes 466952 | tf_op jit(solution)/shard_map/ppermute | solution.py:536
  25.1 6.1 %copy-start = (f32[8,128,128]{2,1,0:T(8,128)S(1)}, f32[8,128,128]{2,1,0:T(8,128)}, u32[]{:S(2)}) copy-start(f32[8,128,128]{2,1,0:T(8,128)} %kmap_ref.3) | copy-start | bytes 1572868
  25.1 6.1 %copy-start.1 = (bf16[128,128]{1,0:T(8,128)(2,1)S(1)}, bf16[128,128]{1,0:T(8,128)(2,1)}, u32[]{:S(2)}) copy-start(bf16[128,128]{1,0:T(8,128)(2,1)} %k_ref.3) | copy-start | bytes 98308
  25.1 6.1 %copy-start.2 = (bf16[128,128]{1,0:T(8,128)(2,1)S(1)}, bf16[128,128]{1,0:T(8,128)(2,1)}, u32[]{:S(2)}) copy-start(bf16[128,128]{1,0:T(8,128)(2,1)} %v_ref.3) | copy-start | bytes 98308
  27.6 3.7 %collective-permute-start.9 = (f32[8,128]{1,0:T(8,128)S(1)}, f32[8,128]{1,0:T(8,128)S(1)}, u32[]{:S(2)}, u32[]{:S(2)}) collective-permute-start(f32[8,128]{1,0:T(8,128)S(1)} %get-tuple-element.38.sums_a_ref), channel_id=1, source_target_pairs={{0,1},{1,0},{2,3},{3,2},{4,5},{5,4},{6,7},{7,6},{8,9},{9,8},{10,11... | collective-permute-start | bytes 12296 | tf_op jit(solution)/shard_map/ppermute | solution.py:536
  33.8 3.1 %collective-permute-start.17 = (f32[520,128]{1,0:T(8,128)S(1)}, f32[520,128]{1,0:T(8,128)S(1)}, u32[]{:S(2)}, u32[]{:S(2)}) collective-permute-start(f32[520,128]{1,0:T(8,128)S(1)} %get-tuple-element.49), channel_id=1, source_target_pairs={{0,2},{2,0},{4,6},{6,4},{8,10},{10,8},{12,14},{14,12},{16,18},{18,... | collective-permute-start | bytes 798728 | tf_op jit(solution)/shard_map/ppermute | solution.py:536
  36.4 3.0 %collective-permute-start.10 = (f32[520,128]{1,0:T(8,128)S(1)}, f32[520,128]{1,0:T(8,128)S(1)}, u32[]{:S(2)}, u32[]{:S(2)}) collective-permute-start(f32[520,128]{1,0:T(8,128)S(1)} %get-tuple-element.47), channel_id=1, source_target_pairs={{0,2},{2,0},{4,6},{6,4},{8,10},{10,8},{12,14},{14,12},{16,18},{18,... | collective-permute-start | bytes 798728 | tf_op jit(solution)/shard_map/ppermute | solution.py:536
  37.0 6.2 %collective-permute-start.18 = (f32[264,128]{1,0:T(8,128)S(1)}, f32[264,128]{1,0:T(8,128)S(1)}, u32[]{:S(2)}, u32[]{:S(2)}) collective-permute-start(f32[264,128]{1,0:T(8,128)S(1)} %slice.102), channel_id=1, source_target_pairs={{0,8},{2,10},{4,12},{6,14},{8,0},{10,2},{12,4},{14,6},{16,24},{18,... | collective-permute-start | bytes 405512 | tf_op jit(solution)/shard_map/ppermute | solution.py:536
  39.5 6.6 %collective-permute-start.11 = (f32[264,128]{1,0:T(8,128)S(1)}, f32[264,128]{1,0:T(8,128)S(1)}, u32[]{:S(2)}, u32[]{:S(2)}) collective-permute-start(f32[264,128]{1,0:T(8,128)S(1)} %slice.93), channel_id=1, source_target_pairs={{0,4},{2,6},{4,0},{6,2},{8,12},{10,14},{12,8},{14,10},{16,20},{18,... | collective-permute-start | bytes 405512 | tf_op jit(solution)/shard_map/ppermute | solution.py:536
  43.3 5.2 %collective-permute-start.19 = (f32[136,128]{1,0:T(8,128)S(1)}, f32[136,128]{1,0:T(8,128)S(1)}, u32[]{:S(2)}, u32[]{:S(2)}) collective-permute-start(f32[136,128]{1,0:T(8,128)S(1)} %pad_maximum_fusion.7), channel_id=1, source_target_pairs={{0,4},{2,6},{4,0},{6,2},{8,12},{10,14},{12,8},{14,10},{16,20},{18,... | collective-permute-start | bytes 208904 | tf_op jit(solution)/shard_map/ppermute | solution.py:536
  46.2 8.2 %collective-permute-start.12 = (f32[136,128]{1,0:T(8,128)S(1)}, f32[136,128]{1,0:T(8,128)S(1)}, u32[]{:S(2)}, u32[]{:S(2)}) collective-permute-start(f32[136,128]{1,0:T(8,128)S(1)} %pad_maximum_fusion.8), channel_id=1, source_target_pairs={{0,8},{2,10},{4,12},{6,14},{8,0},{10,2},{12,4},{14,6},{16,24},{18,... | collective-permute-start | bytes 208904 | tf_op jit(solution)/shard_map/ppermute | solution.py:536
  48.5 10.3 %collective-permute-start.20 = (f32[136,128]{1,0:T(8,128)S(1)}, f32[136,128]{1,0:T(8,128)S(1)}, u32[]{:S(2)}, u32[]{:S(2)}) collective-permute-start(f32[136,128]{1,0:T(8,128)S(1)} %pad_maximum_fusion.10), channel_id=1, source_target_pairs={{0,16},{2,18},{4,20},{6,22},{8,24},{10,26},{12,28},{14,30},{16,0},... | collective-permute-start | bytes 208904 | tf_op jit(solution)/shard_map/ppermute | solution.py:536
  54.4 6.2 %collective-permute-start.13 = (f32[136,128]{1,0:T(8,128)S(1)}, f32[136,128]{1,0:T(8,128)S(1)}, u32[]{:S(2)}, u32[]{:S(2)}) collective-permute-start(f32[136,128]{1,0:T(8,128)S(1)} %pad_maximum_fusion.9), channel_id=1, source_target_pairs={{0,16},{2,18},{4,20},{6,22},{8,24},{10,26},{12,28},{14,30},{16,0},... | collective-permute-start | bytes 208904 | tf_op jit(solution)/shard_map/ppermute | solution.py:536
  58.8 4.3 %collective-permute-start.21 = (f32[128,128]{1,0:T(8,128)S(1)}, f32[128,128]{1,0:T(8,128)S(1)}, u32[]{:S(2)}, u32[]{:S(2)}) collective-permute-start(f32[128,128]{1,0:T(8,128)S(1)} %slice.109), channel_id=1, source_target_pairs={{0,4},{2,6},{4,0},{6,2},{8,12},{10,14},{12,8},{14,10},{16,20},{18,... | collective-permute-start | bytes 196616 | tf_op jit(solution)/shard_map/ppermute | solution.py:536
  60.7 4.3 %collective-permute-start.14 = (f32[128,128]{1,0:T(8,128)S(1)}, f32[128,128]{1,0:T(8,128)S(1)}, u32[]{:S(2)}, u32[]{:S(2)}) collective-permute-start(f32[128,128]{1,0:T(8,128)S(1)} %slice.100), channel_id=1, source_target_pairs={{0,8},{2,10},{4,12},{6,14},{8,0},{10,2},{12,4},{14,6},{16,24},{18,... | collective-permute-start | bytes 196616 | tf_op jit(solution)/shard_map/ppermute | solution.py:536
  63.1 5.0 %collective-permute-start.22 = (f32[256,128]{1,0:T(8,128)S(1)}, f32[256,128]{1,0:T(8,128)S(1)}, u32[]{:S(2)}, u32[]{:S(2)}) collective-permute-start(f32[256,128]{1,0:T(8,128)S(1)} %pad_maximum_fusion.5), channel_id=1, source_target_pairs={{0,8},{2,10},{4,12},{6,14},{8,0},{10,2},{12,4},{14,6},{16,24},{18,... | collective-permute-start | bytes 393224 | tf_op jit(solution)/shard_map/ppermute | solution.py:536
  65.0 5.0 %collective-permute-start.15 = (f32[256,128]{1,0:T(8,128)S(1)}, f32[256,128]{1,0:T(8,128)S(1)}, u32[]{:S(2)}, u32[]{:S(2)}) collective-permute-start(f32[256,128]{1,0:T(8,128)S(1)} %pad_maximum_fusion.4), channel_id=1, source_target_pairs={{0,4},{2,6},{4,0},{6,2},{8,12},{10,14},{12,8},{14,10},{16,20},{18,... | collective-permute-start | bytes 393224 | tf_op jit(solution)/shard_map/ppermute | solution.py:536
  68.2 2.0 %collective-permute-start.23 = (f32[512,128]{1,0:T(8,128)S(1)}, f32[512,128]{1,0:T(8,128)S(1)}, u32[]{:S(2)}, u32[]{:S(2)}) collective-permute-start(f32[512,128]{1,0:T(8,128)S(1)} %pad_maximum_fusion.1.refs_3_), channel_id=1, source_target_pairs={{0,2},{2,0},{4,6},{6,4},{8,10},{10,8},{12,14},{14,12},{16,18},{18,... | collective-permute-start | bytes 786440 | tf_op jit(solution)/shard_map/ppermute | solution.py:536
  70.1 1.6 %collective-permute-start.16 = (f32[512,128]{1,0:T(8,128)S(1)}, f32[512,128]{1,0:T(8,128)S(1)}, u32[]{:S(2)}, u32[]{:S(2)}) collective-permute-start(f32[512,128]{1,0:T(8,128)S(1)} %pad_maximum_fusion.refs_0_), channel_id=1, source_target_pairs={{0,2},{2,0},{4,6},{6,4},{8,10},{10,8},{12,14},{14,12},{16,18},{18,... | collective-permute-start | bytes 786440 | tf_op jit(solution)/shard_map/ppermute | solution.py:536

commit v3 on v2

--- a/solution.py
+++ b/solution.py
@@ -11,6 +11,7 @@
 HIGHEST = lax.Precision.HIGHEST
 NEGATIVE = -1e30
 EPSILON = 1e-05
+LOG2E = 1.4426950408889634
 F32 = jnp.float32
 BF16 = jnp.bfloat16
 NN = (((1,), (0,)), ((), ()))
@@ -87,7 +88,7 @@
 
 
 def local_kernel(
-    packed_ref, level_hbm, q_hbm, qmap_hbm, kmap_hbm, qp_ref, qt_ref, sd_ref, mix_ref, loc_ref, entry_ref, rows_ref,
+    packed_ref, level_hbm, q_hbm, qmap_hbm, kmap_hbm, qp_ref, qe_ref, km_ref, sd_ref, mix_ref, loc_ref, entry_ref, rows_ref,
     q_ref, qmap_ref, kmap_ref, level_ref, sems,
 ):
     fetch(sems, (q_hbm, q_ref), (qmap_hbm, qmap_ref), (kmap_hbm, kmap_ref), (level_hbm, level_ref))
@@ -97,7 +98,6 @@
     low_bits = rows.bit_length() - 1
     cum = exact_dot(gates_of(packed_ref[0, 0, rows:, :]), upper_ones(rows))
     cum_t = cum.T
-    entry_ref[...] = jnp.exp(cum_t)
     rows_ref[...] = stacked_queries(q_ref, dim)
     k = jnp.concatenate([packed_ref[0, 0, 0:half, :], packed_ref[1, 0, 0:half, :]], axis=0)
     v = jnp.concatenate([packed_ref[0, 0, half:rows, :], packed_ref[1, 0, half:rows, :]], axis=0)
@@ -105,11 +105,15 @@
     causal = col <= row
     differ = row ^ col
     highs, lows = [], []
+    entry = jnp.exp(cum_t)
+    entry_ref[...] = entry
     for h in range(heads):
-        qp = dot_right(q_ref[:, h * dim : (h + 1) * dim], halves(qmap_ref[h]))
-        qp_ref[h] = qp
-        qt = dot_f32(halves(qp), halves(kmap_ref[h]), NT)
-        qt_ref[h] = qt
+        qp = halves(dot_right(q_ref[:, h * dim : (h + 1) * dim], halves(qmap_ref[h])))
+        km = halves(kmap_ref[h])
+        qp_ref[h, 0], qp_ref[h, 1] = qp
+        km_ref[h, 0], km_ref[h, 1] = km
+        qt = dot_f32(qp, km, NT)
+        qe_ref[h, 0], qe_ref[h, 1] = halves(entry[:, h : h + 1] * qt)
         high, low = halves(qt)
         highs.append(high)
         lows.append(low)
@@ -173,7 +177,7 @@
     return [even_ref[p, half : 2 * half, :], odd_ref[p, half : 2 * half, :]]
 
 
-def pair_state(kt, v, weight, state_ref, i):
+def pair_state(kt, v, weight, state_ref, i, base_ref=None, base=0):
     heads = weight.shape[0]
     dim = kt.shape[0]
     highs, lows = [], []
@@ -183,7 +187,8 @@
         lows.append(low)
     state = dot_left((jnp.concatenate(highs, axis=0), jnp.concatenate(lows, axis=0)), v)
     for h in range(heads):
-        state_ref[i, h] = state[h * dim : (h + 1) * dim]
+        value = state[h * dim : (h + 1) * dim]
+        state_ref[i, h] = value if base_ref is None else value + base_ref[base, h]
 
 
 def pairs_of(offsets):
@@ -202,10 +207,10 @@
     return sorted(levels.items())
 
 
-def take_level(group, q_all, evens, odds, weights, score_ref, peak_ref, state_ref):
+def take_level(group, q_all, evens, odds, weights, score_ref, peak_ref, state_ref, base_ref=None, bases={}):
     heads = q_all.shape[0] // evens[0].shape[2]
     count = evens[0].shape[0]
-    scale = q_all.shape[1] ** (-0.5)
+    scale = LOG2E * q_all.shape[1] ** (-0.5)
     blocks = {unit: unit_block(evens[unit[0]], odds[unit[0]], unit[1]) for _, units in group for unit in units}
     top = peak_ref[...]
     names = list(blocks)
@@ -222,7 +227,7 @@
         kt = jnp.concatenate([blocks[unit][0] for unit in units], axis=1)
         v = jnp.concatenate([blocks[unit][1] for unit in units], axis=0)
         weight = jnp.concatenate([weights[part][p * heads : (p + 1) * heads] for part, p in units], axis=1)
-        pair_state(kt, v, weight, state_ref, i)
+        pair_state(kt, v, weight, state_ref, i, base_ref if i in bases else None, bases.get(i, 0))
 
 
 def early_kernel(
@@ -246,7 +251,7 @@
     seen = ((place < rows // 2) & (token <= row)) | ((place >= rows // 2) & odd_span)
     blocks = [unit_block(evens[part], odds[part], 0) for part in range(2)]
     kt = jnp.concatenate([kt for kt, _ in blocks], axis=1)
-    score = dot(q_all, kt.astype(BF16)) * dim ** (-0.5)
+    score = dot(q_all, kt.astype(BF16)) * (LOG2E * dim ** (-0.5))
     score = jnp.where(jnp.concatenate([seen] * heads, axis=0), score, NEGATIVE)
     score_ref[0] = score[:, :rows]
     score_ref[count] = score[:, rows:]
@@ -266,11 +271,11 @@
 
 def forward_kernel(
     span_ref, level_ref, q_ref, ea_ref, oa_ref, eb_ref, ob_ref, late_ea_ref, late_oa_ref, late_eb_ref, late_ob_ref,
-    score_a_ref, peak_a_ref, state_a_ref, ends_a_ref, before_ref, qt_ref, loc_ref, gain_ref, entry_ref,
+    score_a_ref, peak_a_ref, state_a_ref, ends_a_ref, before_ref, qe_ref, loc_ref, gain_ref,
     raw_ref, target_ref, level_state_ref, comb_ref, sums_ref,
     score_scr, peak_scr, state_scr, total_scr, acc_scr, *, early, late,
 ):
-    heads, rows, dim = qt_ref.shape
+    heads, rows, dim = loc_ref.shape
     count = ea_ref.shape[0]
     offsets = early[0] + late[0]
     pairs = len(offsets)
@@ -283,13 +288,6 @@
     late_refs = ((late_ea_ref, late_eb_ref), (late_oa_ref, late_ob_ref))
     early_table, late_table = pairs_of(early), pairs_of(late)
     weights, _, ends_b, _ = unit_decay(span, *late_refs)
-    peak_scr[...] = peak_a_ref[...]
-    for bit, group in by_level(late_table):
-
-        @pl.when(((span >> bit) & 1) == 1)
-        def _(group=group):
-            take_level(group, q_all, *late_refs, weights, score_scr, peak_scr, state_scr)
-
     ends = jnp.concatenate([ends_a_ref[...], ends_b], axis=0)
     size = pairs * heads
 
@@ -306,6 +304,38 @@
     carried = exact_dot(between.astype(F32), ends)
     before = jnp.where(odd_span, before_ref[...], 0.0)
     factor = jnp.exp(carried + jnp.concatenate([before] * pairs, axis=0))
+    early_at = {offset: i for i, (offset, _) in enumerate(early_table)}
+    late_at = {offset: i for i, (offset, _) in enumerate(late_table)}
+    bases = {i: early_at[offset] for i, (offset, _) in enumerate(late_table) if offset in early_at}
+
+    def sum_level(level):
+        chosen = [k for k in sorted({*early_at, *late_at}) if max(k, 1).bit_length() - 1 == level]
+        for h in range(heads):
+            value = None
+            for k in chosen:
+                state = state_scr[late_at[k], h] if k in late_at else state_a_ref[early_at[k], h]
+                if k:
+                    at = offsets.index(k) * heads + h
+                    state = state * factor[at : at + 1, :]
+                value = state if value is None else value + state
+            level_state_ref[level, h] = value
+
+    peak_scr[...] = peak_a_ref[...]
+    late_levels = dict(by_level(late_table))
+    for level in range(span_bits):
+        used = ((span >> level) & 1) == 1
+
+        @pl.when(used)
+        def _(level=level):
+            if level in late_levels:
+                take_level(
+                    late_levels[level], q_all, *late_refs, weights, score_scr, peak_scr, state_scr, state_a_ref, bases
+                )
+            sum_level(level)
+
+        @pl.when(jnp.logical_not(used))
+        def _(level=level):
+            level_state_ref[level] = jnp.zeros_like(level_state_ref[level])
 
     peak = jnp.max(peak_scr[...], axis=1, keepdims=True)
     peak_scr[...] = jnp.broadcast_to(peak, peak_scr.shape)
@@ -315,14 +345,14 @@
         total, parts, values = None, [], []
         for units, refs, score_ref in ((early_units, early_refs, score_a_ref), (late_units, late_refs, score_scr)):
             for part, p in units:
-                weight = jnp.exp(score_ref[part * count + p] - top)
+                weight = jnp.exp2(score_ref[part * count + p] - top)
                 total = weight if total is None else total + weight
                 parts.append(weight.astype(BF16))
                 values += unit_values(refs[0][part], refs[1][part], p)
         return total, dot(jnp.concatenate(parts, axis=1), jnp.concatenate(values, axis=0))
 
     total_scr[...], acc_scr[...] = weigh([(0, 0), (1, 0)], [])
-    early_levels, late_levels = dict(by_level(early_table)), dict(by_level(late_table))
+    early_levels = dict(by_level(early_table))
     for bit in sorted({*early_levels, *late_levels}):
 
         @pl.when(((span >> bit) & 1) == 1)
@@ -334,44 +364,22 @@
             total_scr[...] += total
             acc_scr[...] += acc
 
-    for level in range(span_bits):
-        used = ((span >> level) & 1) == 1
-        members = [
-            (ref, i, offset)
-            for ref, table in ((state_a_ref, early_table), (state_scr, late_table))
-            for i, (offset, _) in enumerate(table)
-            if max(offset, 1).bit_length() - 1 == level
-        ]
-
-        @pl.when(used)
-        def _(members=members, level=level):
-            for h in range(heads):
-                value = None
-                for ref, i, offset in members:
-                    state = ref[i, h]
-                    if offset:
-                        at = offsets.index(offset) * heads + h
-                        state = state * factor[at : at + 1, :]
-                    value = state if value is None else value + state
-                level_state_ref[level, h] = value
-
-        @pl.when(jnp.logical_not(used))
-        def _(level=level):
-            level_state_ref[level] = jnp.zeros_like(level_state_ref[level])
-
     total = jnp.sum(total_scr[...], axis=1, keepdims=True)
     target_all = acc_scr[...] / total
-    entry = entry_ref[...]
+    combined = []
+    for h in range(heads):
+        value = level_ref[h, low_bits + 1] * level_state_ref[0, h]
+        for level in range(1, span_bits):
+            value = value + level_ref[h, low_bits + 1 + level] * level_state_ref[level, h]
+        value = halves(value)
+        comb_ref[h, 0], comb_ref[h, 1] = value
+        combined.append(value)
+    fars = [dot_f32((qe_ref[h, 0], qe_ref[h, 1]), combined[h]) for h in range(heads)]
     squares = jnp.zeros((rows, dim), F32)
     gained = jnp.zeros((rows, dim), F32)
     crossed = jnp.zeros((rows, dim), F32)
     for h in range(heads):
-        combined = jnp.zeros((dim, dim), F32)
-        for level in range(span_bits):
-            combined = combined + level_ref[h, low_bits + 1 + level] * level_state_ref[level, h]
-        comb_ref[h] = combined
-        far = entry[:, h : h + 1] * dot_f32(halves(qt_ref[h]), halves(combined))
-        raw = loc_ref[h] + far
+        raw = loc_ref[h] + fars[h]
         target = target_all[h * rows : (h + 1) * rows]
         raw_ref[h] = raw
         target_ref[h] = target
@@ -404,11 +412,11 @@
 
 
 def backward_kernel(
-    span_ref, sums_a_ref, sums_b_ref, entry_ref, q_ref, k_ref, v_ref, kmap_ref, gain_ref,
-    qp_ref, qt_ref, sd_ref, mix_ref, raw_ref, target_ref, state_ref, comb_ref,
+    span_ref, sums_a_ref, sums_b_ref, entry_ref, q_ref, k_ref, v_ref, gain_ref,
+    qp_ref, qe_ref, km_ref, sd_ref, mix_ref, raw_ref, target_ref, state_ref, comb_ref,
     keep_ref, send_ref, *, norm_width, total_tokens, splits, heads,
 ):
-    _, rows, dim = qt_ref.shape
+    _, rows, dim = raw_ref.shape
     share = len(heads)
     span_bits = state_ref.shape[0]
     low_bits = rows.bit_length() - 1
@@ -419,11 +427,6 @@
     inverse = lax.rsqrt(squares / norm_width + EPSILON)
     inner = (inverse * gained - crossed) / total_tokens
     shrink = inverse * inverse * inverse * inner / norm_width
-    entry = entry_ref[...]
-    k = k_ref[...]
-    v = v_ref[...]
-    row, col = iota2((rows, rows), 0), iota2((rows, rows), 1)
-    differ = row ^ col
     levels = low_bits + 1 + span_bits
     pad = 16
     gain_rows, residuals, highs, lows = [], [], [], []
@@ -431,42 +434,58 @@
         gain = gain_ref[h : h + 1, :]
         raw = raw_ref[h]
         normed = raw * inverse
-        mismatch = (normed * gain - target_ref[h]) / total_tokens
+        mismatch = (normed * gain - target_ref[h]) * (1.0 / total_tokens)
         gain_rows.append(jnp.sum(mismatch * normed, axis=0, keepdims=True))
         residual = inverse * (mismatch * gain) - raw * shrink
         residuals.append(residual)
         high, low = halves(residual)
         highs.append(high)
         lows.append(low)
-    d_mix = dot_left((jnp.concatenate(highs, axis=0), jnp.concatenate(lows, axis=0)), v, NT)
-    level_rows, highs, lows = [], [], []
+    d_mix = dot_left((jnp.concatenate(highs, axis=0), jnp.concatenate(lows, axis=0)), v_ref[...], NT)
+    leads = [halves(entry_ref[:, h : h + 1] * residual) for h, residual in zip(heads, residuals)]
+    d_fars = [dot_f32(lead, (comb_ref[h, 0], comb_ref[h, 1]), NT) for h, lead in zip(heads, leads)]
+    d_combs = [
+        dot_f32((qe_ref[h, 0], qe_ref[h, 1]), (high, low), TN) for h, high, low in zip(heads, highs, lows)
+    ]
+    throughs, highs, lows = [], [], []
     for i, h in enumerate(heads):
         d_mix_h = d_mix[i * rows : (i + 1) * rows]
         high, low = halves(d_mix_h * mix_ref[h])
         highs.append(high)
         lows.append(low)
-        through = d_mix_h * sd_ref[h]
-        mine = []
-        for level in range(low_bits + 1):
-            least = 0 if level == 0 else 1 << (level - 1)
-            here = (differ >= least) & (differ < (1 << level))
-            mine.append(jnp.sum(jnp.where(here, through, 0.0), axis=0, keepdims=True))
-        level_rows.append(mine)
-    d_local = dot_left((jnp.concatenate(highs, axis=0), jnp.concatenate(lows, axis=0)), k)
+        throughs.append(d_mix_h * sd_ref[h])
+    d_local = dot_left((jnp.concatenate(highs, axis=0), jnp.concatenate(lows, axis=0)), k_ref[...])
+    d_qts = [halves(d_local[i * rows : (i + 1) * rows] + d_fars[i]) for i in range(share)]
+    d_qps = [halves(dot_f32(d_qts[i], (km_ref[h, 0], km_ref[h, 1]))) for i, h in enumerate(heads)]
+    grads_k = [dot_f32(d_qts[i], (qp_ref[h, 0], qp_ref[h, 1]), TN) for i, h in enumerate(heads)]
+    grads_q = [dot_right(q_ref[h * rows : (h + 1) * rows, :], d_qps[i], TN) for i, h in enumerate(heads)]
+
+    block = 8
+    inside = block.bit_length() - 1
+    lane = iota2((block, rows), 1)
+    near = iota2((block, rows), 0) ^ (lane % block)
+    apart = [(lane // block) ^ i for i in range(rows // block)]
+    level_rows = []
     for i, h in enumerate(heads):
-        lead = halves(entry[:, h : h + 1] * residuals[i])
-        d_qt = halves(d_local[i * rows : (i + 1) * rows] + dot_f32(lead, halves(comb_ref[h]), NT))
-        grad_k = dot_f32(d_qt, halves(qp_ref[h]), TN)
-        d_qp = dot_f32(d_qt, halves(kmap_ref[h]))
-        grad_q = dot_right(q_ref[h * rows : (h + 1) * rows, :], halves(d_qp), TN)
-        d_comb = dot_f32(halves(qt_ref[h]), lead, TN)
+        pieces = [throughs[i][at : at + block] for at in range(0, rows, block)]
+        sums_by = [jnp.zeros((block, rows), F32) for _ in range(low_bits + 1 - inside)]
+        for piece, distance in zip(pieces, apart):
+            for level in range(len(sums_by)):
+                here = distance == 0 if level == 0 else (distance >> (level - 1)) == 1
+                sums_by[level] = sums_by[level] + jnp.where(here, piece, 0.0)
+        for level in range(inside + 1):
+            here = near == 0 if level == 0 else (near >> (level - 1)) == 1
+            level_rows.append(jnp.sum(jnp.where(here, sums_by[0], 0.0), axis=0, keepdims=True))
+        for level in range(1, len(sums_by)):
+            level_rows.append(jnp.sum(sums_by[level], axis=0, keepdims=True))
         for level in range(span_bits):
-            level_rows[i].append(jnp.sum(state_ref[level, h] * d_comb, axis=0, keepdims=True))
-        level_rows[i].append(jnp.zeros((pad - levels, rows), F32))
+            level_rows.append(jnp.sum(state_ref[level, h] * d_combs[i], axis=0, keepdims=True))
+        level_rows.append(jnp.zeros((pad - levels, rows), F32))
+    for i in range(share):
         at = pl.ds(pl.multiple_of(chunk_of(i, share, span, splits) * dim, dim), dim)
-        keep_ref[at, :] = jnp.where(first, grad_q, grad_k)
-        send_ref[at, :] = jnp.where(first, grad_k, grad_q)
-    table = jnp.sum(jnp.concatenate([r for mine in level_rows for r in mine], axis=0), axis=1, keepdims=True)
+        keep_ref[at, :] = jnp.where(first, grads_q[i], grads_k[i])
+        send_ref[at, :] = jnp.where(first, grads_k[i], grads_q[i])
+    table = jnp.sum(jnp.concatenate(level_rows, axis=0), axis=1, keepdims=True)
     spread = iota2((share * pad, rows), 0) % pad == iota2((share * pad, rows), 1)
     pick = iota2((share, share * pad), 1) // pad == iota2((share, share * pad), 0)
     level_sums = exact_dot(pick.astype(F32), jnp.where(spread, table, 0.0))
@@ -549,6 +568,7 @@
     strides = [1 << bit for bit in reversed(range(1, span_bits))]
     orders = [(2, 4), (4, 2)]
     cube = (heads, dim, dim)
+    pieces = shape(heads, 2, rows, dim, dtype=BF16)
     packed_rows = rows + 3 * heads
 
     shared, (far, near) = strides[:-2], strides[-2:]
@@ -565,8 +585,8 @@
         pltpu.VMEM((heads, rows), F32),
         pltpu.SemaphoreType.DMA((3,)),
     ])(*in_hbm(key_vectors, value_vectors, log_gate))
-    qp, qt, score_decay, mix, local, entry, stacked = call(
-        local_kernel, vmem(1) + hbm(4), [shape(*cube)] * 5 + [shape(rows, heads), shape(heads * rows, dim, dtype=BF16)], 24, 1 << 29,
+    qp, qe, km, score_decay, mix, local, entry, stacked = call(
+        local_kernel, vmem(1) + hbm(4), [pieces] * 3 + [shape(*cube)] * 3 + [shape(rows, heads), shape(heads * rows, dim, dtype=BF16)], 24, 1 << 29,
         scratch=[
             pltpu.VMEM(queries.shape, BF16),
             pltpu.VMEM(cube, F32),
@@ -606,8 +626,8 @@
     )(span, stacked, *blocks[:4])
     raw, target, level_states, combined, sums = call(
         forward_kernel,
-        smem(2) + vmem(18),
-        [shape(*cube), shape(*cube), shape(span_bits, *cube), shape(*cube), shape(8, rows)],
+        smem(2) + vmem(17),
+        [shape(*cube), shape(*cube), shape(span_bits, *cube), pieces, shape(8, rows)],
         32,
         1 << 31,
         scratch=[
@@ -620,7 +640,7 @@
         early=early,
         late=late,
     )(
-        span, level_weight, stacked, *blocks, scores, peaks, states, ends, before, qt, local, gain, entry,
+        span, level_weight, stacked, *blocks, scores, peaks, states, ends, before, qe, local, gain,
     )
 
     stride = 1
@@ -645,8 +665,8 @@
             splits=orders[part],
             heads=range(part * share, (part + 1) * share),
         )(
-            span, sums, received, entry, stacked, key_vectors, value_vectors, key_map, gain,
-            qp, qt, score_decay, mix, raw, target, level_states, combined,
+            span, sums, received, entry, stacked, key_vectors, value_vectors, gain,
+            qp, qe, km, score_decay, mix, raw, target, level_states, combined,
         )
         held.append(keep + swap(send, "seq", 1))
     for step in range(len(orders[0])):
@@ -665,9 +685,9 @@
         for part in range(PARTS):
             split = orders[part][step]
             mine[part] = jnp.concatenate([mine[part], swap(mine[part], "seq", split)])
-    pieces = []
+    found = []
     for part in range(PARTS):
-        pieces += [mine[part], swap(mine[part], "seq", 1), held[part]]
+        found += [mine[part], swap(mine[part], "seq", 1), held[part]]
     grad_query, grad_key, grad_levels, grad_gain = call(
         place_kernel,
         smem(1) + vmem(3 * PARTS),
@@ -675,7 +695,7 @@
         16,
         1 << 20,
         orders=orders,
-    )(span, *pieces)
+    )(span, *found)
     grad_gain = grad_gain.reshape(-1)
     return grad_query, grad_key, grad_levels, grad_gain
 

time: 73 us -> 69.8 us (0.956)
  Pallas kernels: 13.2 us -> 10.6 us
  starting transfers between devices: 34.1 us -> 33.2 us
    pallas_call x2, Pallas kernels: 5.21 us -> 2.6 us  [on_device(): call(backward_kernel, smem(1) + vmem(16), [shape(share * (dim + 2), dim)]...]
    ppermute x24, starting transfers between devices: 34.1 us -> 33.2 us  [swap(): return lax.ppermute(value, axis, [(i, i ^ stride) for i in range(count)])]
  transfers between devices with their start and end apart: 24 -> 24, of which waited for: 13 -> 13; matrix products, arithmetic and copies ran while one was open for 0% -> 0% of each run, Pallas kernels for 9% -> 7%
where the time goes in v3:
time: 69.8 us; the launch traced here: 69.6 us
  starting transfers between devices  33.2 us (48%)
  waiting for transfers between devices  24.5 us (35%)
  Pallas kernels  10.6 us (15%)
  between operations  0.92 us (1%)
    ppermute x24, starting transfers between devices, swap(): return lax.ppermute(value, axis, [(i, i ^ stride) for i in range(count)])  33.2 us
    ppermute x24, waiting for transfers between devices, swap(): return lax.ppermute(value, axis, [(i, i ^ stride) for i in range(count)])  24.5 us
    pallas_call x1, Pallas kernels, on_device(): call(local_kernel, vmem(1) + hbm(4), [pieces] * 3 + [shape(*cube)] * 3 +...  3.3 us
    pallas_call x2, Pallas kernels, on_device(): call(backward_kernel, smem(1) + vmem(16), [shape(share * (dim + 2), dim)]...  2.6 us
    pallas_call x1, Pallas kernels, on_device(): call(forward_kernel, smem(2) + vmem(17), [shape(*cube), shape(*cube), sha...  2.45 us
  transfers between devices with their start and end apart: 24, of which 13 were waited for; matrix products, arithmetic and copies ran while one was open for 0% of the time, Pallas kernels for 7%

profile of v3, /device:TPU:0, one launch (start us, length us, event | category | flops | bytes accessed | tf_op | source)
XLA Modules:
  0.0 69.6 jit_solution(2696186320180414166)
XLA Ops:
  0.6 0.8 %shard_map.111.packed_ref = bf16[2,1,152,128]{3,2,1,0:T(8,128)(2,1)S(1)} custom-call(bf16[128,128]{1,0:T(8,128)(2,1)} %k_ref.3, bf16[128,128]{1,0:T(8,128)(2,1)} %v_ref.3, f32[8,128]{1,0:T(8,128)} %gate_hbm.1), custom_call_target="tpu_custom_call" | custom-call | flops 1048576 | bytes 1048576 | tf_op jit(solution)/shard_map/pallas_call | solution.py:582
  1.5 4.1 %collective-permute-start = (bf16[2,1,152,128]{3,2,1,0:T(8,128)(2,1)S(1)}, bf16[2,1,152,128]{3,2,1,0:T(8,128)(2,1)S(1)}, u32[]{:S(2)}, u32[]{:S(2)}) collective-permute-start(bf16[2,1,152,128]{3,2,1,0:T(8,128)(2,1)S(1)} %shard_map.111.packed_ref), channel_id=1, source_target_pairs={{0,16},{2,18},{4,20},{6,22},{8,24},{10,26},{12,28},{14,30},{16,0},... | collective-permute-start | bytes 233480 | tf_op jit(solution)/shard_map/ppermute | solution.py:555
  5.6 4.0 %collective-permute-done = bf16[2,1,152,128]{3,2,1,0:T(8,128)(2,1)S(1)} collective-permute-done((bf16[2,1,152,128]{3,2,1,0:T(8,128)(2,1)S(1)}, bf16[2,1,152,128]{3,2,1,0:T(8,128)(2,1)S(1)}, u32[]{:S(2)}, u32[]{:S(2)}) %collective-permute-start) | collective-permute-done | bytes 77856 | tf_op jit(solution)/shard_map/ppermute | solution.py:555
  9.6 0.8 %collective-permute-start.1 = (bf16[2,152,128]{2,1,0:T(8,128)(2,1)S(1)}, bf16[2,152,128]{2,1,0:T(8,128)(2,1)S(1)}, u32[]{:S(2)}, u32[]{:S(2)}) collective-permute-start(bf16[2,152,128]{2,1,0:T(8,128)(2,1)S(1)} %get-tuple-element.57), channel_id=1, source_target_pairs={{0,8},{2,10},{4,12},{6,14},{8,0},{10,2},{12,4},{14,6},{16,24},{18,... | collective-permute-start | bytes 233480 | tf_op jit(solution)/shard_map/ppermute | solution.py:555
  10.4 1.5 %collective-permute-start.3 = (bf16[2,152,128]{2,1,0:T(8,128)(2,1)S(1)}, bf16[2,152,128]{2,1,0:T(8,128)(2,1)S(1)}, u32[]{:S(2)}, u32[]{:S(2)}) collective-permute-start(bf16[2,152,128]{2,1,0:T(8,128)(2,1)S(1)} %get-tuple-element.56), channel_id=1, source_target_pairs={{0,4},{2,6},{4,0},{6,2},{8,12},{10,14},{12,8},{14,10},{16,20},{18,... | collective-permute-start | bytes 233480 | tf_op jit(solution)/shard_map/ppermute | solution.py:555
  11.9 2.2 %collective-permute-done.1 = bf16[2,152,128]{2,1,0:T(8,128)(2,1)S(1)} collective-permute-done((bf16[2,152,128]{2,1,0:T(8,128)(2,1)S(1)}, bf16[2,152,128]{2,1,0:T(8,128)(2,1)S(1)}, u32[]{:S(2)}, u32[]{:S(2)}) %collective-permute-start.1) | collective-permute-done | bytes 77856 | tf_op jit(solution)/shard_map/ppermute | solution.py:555
  14.1 0.0 copy-start.2
  14.1 0.0 copy-start.3
  14.2 1.8 %collective-permute-start.5 = (bf16[4,152,128]{2,1,0:T(8,128)(2,1)S(1)}, bf16[4,152,128]{2,1,0:T(8,128)(2,1)S(1)}, u32[]{:S(2)}, u32[]{:S(2)}) collective-permute-start(bf16[4,152,128]{2,1,0:T(8,128)(2,1)S(1)} %pad_maximum_fusion.2.even_a_ref.ea_ref), channel_id=1, source_target_pairs={{0,4},{2,6},{4,0},{6,2},{8,12},{10,14},{12,8},{14,10},{16,20},{18,... | collective-permute-start | bytes 466952 | tf_op jit(solution)/shard_map/ppermute | solution.py:555
  15.9 0.0 collective-permute-done.3
  16.0 0.6 collective-permute-start.7
  16.5 0.0 collective-permute-start.2
  16.5 0.5 collective-permute-start.4
  17.0 2.4 %collective-permute-done.5.late_ea_ref = bf16[4,152,128]{2,1,0:T(8,128)(2,1)S(1)} collective-permute-done((bf16[4,152,128]{2,1,0:T(8,128)(2,1)S(1)}, bf16[4,152,128]{2,1,0:T(8,128)(2,1)S(1)}, u32[]{:S(2)}, u32[]{:S(2)}) %collective-permute-start.5) | collective-permute-done | bytes 155680 | tf_op jit(solution)/shard_map/ppermute | solution.py:555
  19.5 0.0 collective-permute-start.6
  19.5 1.8 %collective-permute-done.7.late_eb_ref = bf16[4,152,128]{2,1,0:T(8,128)(2,1)S(1)} collective-permute-done((bf16[4,152,128]{2,1,0:T(8,128)(2,1)S(1)}, bf16[4,152,128]{2,1,0:T(8,128)(2,1)S(1)}, u32[]{:S(2)}, u32[]{:S(2)}) %collective-permute-start.7) | collective-permute-done | bytes 155680 | tf_op jit(solution)/shard_map/ppermute | solution.py:555
  21.3 0.0 collective-permute-start.8
  21.3 3.3 %shard_map.112 = (bf16[8,2,128,128]{3,2,1,0:T(8,128)(2,1)S(1)}, bf16[8,2,128,128]{3,2,1,0:T(8,128)(2,1)S(1)}, bf16[8,2,128,128]{3,2,1,0:T(8,128)(2,1)S(1)}, f32[...) custom-call(bf16[2,1,152,128]{3,2,1,0:T(8,128)(2,1)S(1)} %shard_map., ...), custom_call_target="tpu_custom_call" | custom-call | flops 536870912 | bytes 1048576 | tf_op jit(solution)/shard_map/pallas_call | solution.py:588
  24.6 0.0 collective-permute-done.2.odd_a_ref.oa_ref
  24.6 0.0 collective-permute-done.4.odd_b_ref.ob_ref
  24.6 0.4 shard_map.113
  25.0 0.0 collective-permute-done.6.late_oa_ref
  25.1 0.0 collective-permute-done.8.late_ob_ref
  25.1 0.0 copy-done.2
  25.1 0.0 copy-done.3
  25.1 0.0 copy-start
  25.1 0.0 copy-start.1
  25.1 2.4 %shard_map.114 = (f32[8,128,128]{2,1,0:T(8,128)S(1)}, f32[8,128,128]{2,1,0:T(8,128)S(1)}, f32[4,8,128,128]{3,2,1,0:T(8,128)S(1)}, bf16[8,2,128,128]{3,2,1,0:T(8,128)(2,1)S(1)}, f32[8,128]{1,0:T(8,128)S(1)}) custom-call(s32[1]{0:T(128)} %bitcast.span_ref, f32[8,12]{1,0:T(8,128)S(1)} %copy-done.3, bf16[1024,128]{1,0:T(8,128)(2,1)S(1)} %get-tuple-element.30.q_ref, ...), custom_call_target="tpu_custom_call" | custom-call | flops 2147483648 | bytes 1048576 | tf_op jit(solution)/shard_map/pallas_call | solution.py:627
  27.6 1.5 %collective-permute-start.9 = (f32[8,128]{1,0:T(8,128)S(1)}, f32[8,128]{1,0:T(8,128)S(1)}, u32[]{:S(2)}, u32[]{:S(2)}) collective-permute-start(f32[8,128]{1,0:T(8,128)S(1)} %get-tuple-element.38.sums_a_ref), channel_id=1, source_target_pairs={{0,1},{1,0},{2,3},{3,2},{4,5},{5,4},{6,7},{7,6},{8,9},{9,8},{10,11... | collective-permute-start | bytes 12296 | tf_op jit(solution)/shard_map/ppermute | solution.py:555
  29.1 2.1 %collective-permute-done.9.sums_b_ref = f32[8,128]{1,0:T(8,128)S(1)} collective-permute-done((f32[8,128]{1,0:T(8,128)S(1)}, f32[8,128]{1,0:T(8,128)S(1)}, u32[]{:S(2)}, u32[]{:S(2)}) %collective-permute-start.9) | collective-permute-done | bytes 4128 | tf_op jit(solution)/shard_map/ppermute | solution.py:555
  31.2 0.0 copy-done
  31.2 0.0 copy-done.1
  31.2 1.3 %shard_map.116 = (f32[520,128]{1,0:T(8,128)S(1)}, f32[520,128]{1,0:T(8,128)S(1)}) custom-call(s32[1]{0:T(128)} %bitcast.span_ref, f32[8,128]{1,0:T(8,128)S(1)} %get-tuple-element.38.sums_a_ref, f32[8,128]{1,0:T(8,128)S(1)} %collective-permute-done.9.sums_b_ref, f32[128,8]{1,0:T(8,128)S(1)} %get-tuple-element.39.entry_ref, ...), custom_call_target="tpu_custom_call" | custom-call | flops 536870912 | bytes 1048576 | tf_op jit(solution)/shard_map/pallas_call | solution.py:657
  32.5 0.0 collective-permute-start.17
  32.6 1.3 %shard_map.115 = (f32[520,128]{1,0:T(8,128)S(1)}, f32[520,128]{1,0:T(8,128)S(1)}) custom-call(s32[1]{0:T(128)} %bitcast.span_ref, f32[8,128]{1,0:T(8,128)S(1)} %get-tuple-element.38.sums_a_ref, f32[8,128]{1,0:T(8,128)S(1)} %collective-permute-done.9.sums_b_ref, f32[128,8]{1,0:T(8,128)S(1)} %get-tuple-element.39.entry_ref, ...), custom_call_target="tpu_custom_call" | custom-call | flops 536870912 | bytes 1048576 | tf_op jit(solution)/shard_map/pallas_call | solution.py:657
  33.9 0.5 collective-permute-start.10
  34.4 0.0 collective-permute-done.17
  34.4 2.3 %collective-permute-start.18 = (f32[264,128]{1,0:T(8,128)S(1)}, f32[264,128]{1,0:T(8,128)S(1)}, u32[]{:S(2)}, u32[]{:S(2)}) collective-permute-start(f32[264,128]{1,0:T(8,128)S(1)} %slice.102), channel_id=1, source_target_pairs={{0,8},{2,10},{4,12},{6,14},{8,0},{10,2},{12,4},{14,6},{16,24},{18,... | collective-permute-start | bytes 405512 | tf_op jit(solution)/shard_map/ppermute | solution.py:555
  36.7 0.0 collective-permute-done.10
  36.8 2.8 %collective-permute-start.11 = (f32[264,128]{1,0:T(8,128)S(1)}, f32[264,128]{1,0:T(8,128)S(1)}, u32[]{:S(2)}, u32[]{:S(2)}) collective-permute-start(f32[264,128]{1,0:T(8,128)S(1)} %slice.93), channel_id=1, source_target_pairs={{0,4},{2,6},{4,0},{6,2},{8,12},{10,14},{12,8},{14,10},{16,20},{18,... | collective-permute-start | bytes 405512 | tf_op jit(solution)/shard_map/ppermute | solution.py:555
  39.6 0.9 %collective-permute-done.18 = f32[264,128]{1,0:T(8,128)S(1)} collective-permute-done((f32[264,128]{1,0:T(8,128)S(1)}, f32[264,128]{1,0:T(8,128)S(1)}, u32[]{:S(2)}, u32[]{:S(2)}) %collective-permute-start.18) | collective-permute-done | bytes 135200 | tf_op jit(solution)/shard_map/ppermute | solution.py:555
  40.5 2.8 %collective-permute-start.19 = (f32[136,128]{1,0:T(8,128)S(1)}, f32[136,128]{1,0:T(8,128)S(1)}, u32[]{:S(2)}, u32[]{:S(2)}) collective-permute-start(f32[136,128]{1,0:T(8,128)S(1)} %pad_maximum_fusion.7), channel_id=1, source_target_pairs={{0,4},{2,6},{4,0},{6,2},{8,12},{10,14},{12,8},{14,10},{16,20},{18,... | collective-permute-start | bytes 208904 | tf_op jit(solution)/shard_map/ppermute | solution.py:555
  43.3 0.0 collective-permute-done.11
  43.4 1.8 %collective-permute-start.12 = (f32[136,128]{1,0:T(8,128)S(1)}, f32[136,128]{1,0:T(8,128)S(1)}, u32[]{:S(2)}, u32[]{:S(2)}) collective-permute-start(f32[136,128]{1,0:T(8,128)S(1)} %pad_maximum_fusion.8), channel_id=1, source_target_pairs={{0,8},{2,10},{4,12},{6,14},{8,0},{10,2},{12,4},{14,6},{16,24},{18,... | collective-permute-start | bytes 208904 | tf_op jit(solution)/shard_map/ppermute | solution.py:555
  45.2 0.4 collective-permute-done.19
  45.7 5.7 %collective-permute-start.20 = (f32[136,128]{1,0:T(8,128)S(1)}, f32[136,128]{1,0:T(8,128)S(1)}, u32[]{:S(2)}, u32[]{:S(2)}) collective-permute-start(f32[136,128]{1,0:T(8,128)S(1)} %pad_maximum_fusion.10), channel_id=1, source_target_pairs={{0,16},{2,18},{4,20},{6,22},{8,24},{10,26},{12,28},{14,30},{16,0},... | collective-permute-start | bytes 208904 | tf_op jit(solution)/shard_map/ppermute | solution.py:555
  51.3 0.0 collective-permute-done.12
  51.4 2.2 %collective-permute-start.13 = (f32[136,128]{1,0:T(8,128)S(1)}, f32[136,128]{1,0:T(8,128)S(1)}, u32[]{:S(2)}, u32[]{:S(2)}) collective-permute-start(f32[136,128]{1,0:T(8,128)S(1)} %pad_maximum_fusion.9), channel_id=1, source_target_pairs={{0,16},{2,18},{4,20},{6,22},{8,24},{10,26},{12,28},{14,30},{16,0},... | collective-permute-start | bytes 208904 | tf_op jit(solution)/shard_map/ppermute | solution.py:555
  53.5 2.2 %collective-permute-done.20 = f32[136,128]{1,0:T(8,128)S(1)} collective-permute-done((f32[136,128]{1,0:T(8,128)S(1)}, f32[136,128]{1,0:T(8,128)S(1)}, u32[]{:S(2)}, u32[]{:S(2)}) %collective-permute-start.20) | collective-permute-done | bytes 69664 | tf_op jit(solution)/shard_map/ppermute | solution.py:555
  55.8 1.7 %collective-permute-start.21 = (f32[128,128]{1,0:T(8,128)S(1)}, f32[128,128]{1,0:T(8,128)S(1)}, u32[]{:S(2)}, u32[]{:S(2)}) collective-permute-start(f32[128,128]{1,0:T(8,128)S(1)} %slice.109), channel_id=1, source_target_pairs={{0,4},{2,6},{4,0},{6,2},{8,12},{10,14},{12,8},{14,10},{16,20},{18,... | collective-permute-start | bytes 196616 | tf_op jit(solution)/shard_map/ppermute | solution.py:555
  57.5 0.0 collective-permute-done.13
  57.6 0.9 %collective-permute-start.14 = (f32[128,128]{1,0:T(8,128)S(1)}, f32[128,128]{1,0:T(8,128)S(1)}, u32[]{:S(2)}, u32[]{:S(2)}) collective-permute-start(f32[128,128]{1,0:T(8,128)S(1)} %slice.100), channel_id=1, source_target_pairs={{0,8},{2,10},{4,12},{6,14},{8,0},{10,2},{12,4},{14,6},{16,24},{18,... | collective-permute-start | bytes 196616 | tf_op jit(solution)/shard_map/ppermute | solution.py:555
  58.5 1.7 %collective-permute-done.21 = f32[128,128]{1,0:T(8,128)S(1)} collective-permute-done((f32[128,128]{1,0:T(8,128)S(1)}, f32[128,128]{1,0:T(8,128)S(1)}, u32[]{:S(2)}, u32[]{:S(2)}) %collective-permute-start.21) | collective-permute-done | bytes 65568 | tf_op jit(solution)/shard_map/ppermute | solution.py:555
  60.2 0.3 collective-permute-start.22
  60.4 1.4 %collective-permute-done.14 = f32[128,128]{1,0:T(8,128)S(1)} collective-permute-done((f32[128,128]{1,0:T(8,128)S(1)}, f32[128,128]{1,0:T(8,128)S(1)}, u32[]{:S(2)}, u32[]{:S(2)}) %collective-permute-start.14) | collective-permute-done | bytes 65568 | tf_op jit(solution)/shard_map/ppermute | solution.py:555
  61.9 1.2 %collective-permute-start.15 = (f32[256,128]{1,0:T(8,128)S(1)}, f32[256,128]{1,0:T(8,128)S(1)}, u32[]{:S(2)}, u32[]{:S(2)}) collective-permute-start(f32[256,128]{1,0:T(8,128)S(1)} %pad_maximum_fusion.4), channel_id=1, source_target_pairs={{0,4},{2,6},{4,0},{6,2},{8,12},{10,14},{12,8},{14,10},{16,20},{18,... | collective-permute-start | bytes 393224 | tf_op jit(solution)/shard_map/ppermute | solution.py:555
  63.1 2.1 %collective-permute-done.22 = f32[256,128]{1,0:T(8,128)S(1)} collective-permute-done((f32[256,128]{1,0:T(8,128)S(1)}, f32[256,128]{1,0:T(8,128)S(1)}, u32[]{:S(2)}, u32[]{:S(2)}) %collective-permute-start.22) | collective-permute-done | bytes 131104 | tf_op jit(solution)/shard_map/ppermute | solution.py:555
  65.2 0.1 collective-permute-start.23
  65.3 1.7 %collective-permute-done.15 = f32[256,128]{1,0:T(8,128)S(1)} collective-permute-done((f32[256,128]{1,0:T(8,128)S(1)}, f32[256,128]{1,0:T(8,128)S(1)}, u32[]{:S(2)}, u32[]{:S(2)}) %collective-permute-start.15) | collective-permute-done | bytes 131104 | tf_op jit(solution)/shard_map/ppermute | solution.py:555
  67.0 0.1 collective-permute-start.16
  67.0 0.0 collective-permute-done.23.refs_4_
  67.0 1.5 %collective-permute-done.16.refs_1_ = f32[512,128]{1,0:T(8,128)S(1)} collective-permute-done((f32[512,128]{1,0:T(8,128)S(1)}, f32[512,128]{1,0:T(8,128)S(1)}, u32[]{:S(2)}, u32[]{:S(2)}) %collective-permute-start.16) | collective-permute-done | bytes 262176 | tf_op jit(solution)/shard_map/ppermute | solution.py:555
  68.6 1.0 %shard_map.117 = (f32[8,128,128]{2,1,0:T(8,128)}, f32[8,128,128]{2,1,0:T(8,128)}, f32[8,12]{1,0:T(8,128)}, f32[8,128]{1,0:T(8,128)}) custom-call(s32[1]{0:T(128)} %bitcast.span_ref, f32[512,128]{1,0:T(8,128)S(1)} %pad_maximum_fusion.refs_0_, f32[512,128]{1,0:T(8,128)S(1)} %collective-permute-done.16.refs_1_, f32[136,128]{1,0:T(8,128)S(1)} %fusion.4.refs_2_, ...), custom_call_target="tpu_custom_call" | custom-call | flops 1048576 | bytes 1048576 | tf_op jit(solution)/shard_map/pallas_call | solution.py:691
  (27 shorter events, 0.3 us)
Async XLA Ops:
  1.5 8.2 %collective-permute-start = (bf16[2,1,152,128]{3,2,1,0:T(8,128)(2,1)S(1)}, bf16[2,1,152,128]{3,2,1,0:T(8,128)(2,1)S(1)}, u32[]{:S(2)}, u32[]{:S(2)}) collective-permute-start(bf16[2,1,152,128]{3,2,1,0:T(8,128)(2,1)S(1)} %shard_map.111.packed_ref), channel_id=1, source_target_pairs={{0,16},{2,18},{4,20},{6,22},{8,24},{10,26},{12,28},{14,30},{16,0},... | collective-permute-start | bytes 233480 | tf_op jit(solution)/shard_map/ppermute | solution.py:555
  9.6 4.5 %collective-permute-start.1 = (bf16[2,152,128]{2,1,0:T(8,128)(2,1)S(1)}, bf16[2,152,128]{2,1,0:T(8,128)(2,1)S(1)}, u32[]{:S(2)}, u32[]{:S(2)}) collective-permute-start(bf16[2,152,128]{2,1,0:T(8,128)(2,1)S(1)} %get-tuple-element.57), channel_id=1, source_target_pairs={{0,8},{2,10},{4,12},{6,14},{8,0},{10,2},{12,4},{14,6},{16,24},{18,... | collective-permute-start | bytes 233480 | tf_op jit(solution)/shard_map/ppermute | solution.py:555
  10.4 5.5 %collective-permute-start.3 = (bf16[2,152,128]{2,1,0:T(8,128)(2,1)S(1)}, bf16[2,152,128]{2,1,0:T(8,128)(2,1)S(1)}, u32[]{:S(2)}, u32[]{:S(2)}) collective-permute-start(bf16[2,152,128]{2,1,0:T(8,128)(2,1)S(1)} %get-tuple-element.56), channel_id=1, source_target_pairs={{0,4},{2,6},{4,0},{6,2},{8,12},{10,14},{12,8},{14,10},{16,20},{18,... | collective-permute-start | bytes 233480 | tf_op jit(solution)/shard_map/ppermute | solution.py:555
  14.1 10.9 %copy-start.2 = (f32[1024]{0:T(1024)S(1)}, f32[1024]{0:T(1024)}, u32[]{:S(2)}) copy-start(f32[1024]{0:T(1024)} %param.15) | copy-start | bytes 12292
  14.1 10.9 %copy-start.3 = (f32[8,12]{1,0:T(8,128)S(1)}, f32[8,12]{1,0:T(8,128)}, u32[]{:S(2)}) copy-start(f32[8,12]{1,0:T(8,128)} %level_ref.1) | copy-start | bytes 1156
  14.2 5.3 %collective-permute-start.5 = (bf16[4,152,128]{2,1,0:T(8,128)(2,1)S(1)}, bf16[4,152,128]{2,1,0:T(8,128)(2,1)S(1)}, u32[]{:S(2)}, u32[]{:S(2)}) collective-permute-start(bf16[4,152,128]{2,1,0:T(8,128)(2,1)S(1)} %pad_maximum_fusion.2.even_a_ref.ea_ref), channel_id=1, source_target_pairs={{0,4},{2,6},{4,0},{6,2},{8,12},{10,14},{12,8},{14,10},{16,20},{18,... | collective-permute-start | bytes 466952 | tf_op jit(solution)/shard_map/ppermute | solution.py:555
  16.0 5.3 %collective-permute-start.7 = (bf16[4,152,128]{2,1,0:T(8,128)(2,1)S(1)}, bf16[4,152,128]{2,1,0:T(8,128)(2,1)S(1)}, u32[]{:S(2)}, u32[]{:S(2)}) collective-permute-start(bf16[4,152,128]{2,1,0:T(8,128)(2,1)S(1)} %pad_maximum_fusion.3.even_b_ref.eb_ref), channel_id=1, source_target_pairs={{0,8},{2,10},{4,12},{6,14},{8,0},{10,2},{12,4},{14,6},{16,24},{18,... | collective-permute-start | bytes 466952 | tf_op jit(solution)/shard_map/ppermute | solution.py:555
  16.5 8.0 %collective-permute-start.2 = (bf16[4,152,128]{2,1,0:T(8,128)(2,1)S(1)}, bf16[4,152,128]{2,1,0:T(8,128)(2,1)S(1)}, u32[]{:S(2)}, u32[]{:S(2)}) collective-permute-start(bf16[4,152,128]{2,1,0:T(8,128)(2,1)S(1)} %pad_maximum_fusion.2.even_a_ref.ea_ref), channel_id=1, source_target_pairs={{0,2},{2,0},{4,6},{6,4},{8,10},{10,8},{12,14},{14,12},{16,18},{18,... | collective-permute-start | bytes 466952 | tf_op jit(solution)/shard_map/ppermute | solution.py:555
  16.5 8.1 %collective-permute-start.4 = (bf16[4,152,128]{2,1,0:T(8,128)(2,1)S(1)}, bf16[4,152,128]{2,1,0:T(8,128)(2,1)S(1)}, u32[]{:S(2)}, u32[]{:S(2)}) collective-permute-start(bf16[4,152,128]{2,1,0:T(8,128)(2,1)S(1)} %pad_maximum_fusion.3.even_b_ref.eb_ref), channel_id=1, source_target_pairs={{0,2},{2,0},{4,6},{6,4},{8,10},{10,8},{12,14},{14,12},{16,18},{18,... | collective-permute-start | bytes 466952 | tf_op jit(solution)/shard_map/ppermute | solution.py:555
  19.5 5.6 %collective-permute-start.6 = (bf16[4,152,128]{2,1,0:T(8,128)(2,1)S(1)}, bf16[4,152,128]{2,1,0:T(8,128)(2,1)S(1)}, u32[]{:S(2)}, u32[]{:S(2)}) collective-permute-start(bf16[4,152,128]{2,1,0:T(8,128)(2,1)S(1)} %collective-permute-done.5.late_ea_ref), channel_id=1, source_target_pairs={{0,2},{2,0},{4,6},{6,4},{8,10},{10,8},{12,14},{14,12},{16,18},{18,... | collective-permute-start | bytes 466952 | tf_op jit(solution)/shard_map/ppermute | solution.py:555
  21.3 3.8 %collective-permute-start.8 = (bf16[4,152,128]{2,1,0:T(8,128)(2,1)S(1)}, bf16[4,152,128]{2,1,0:T(8,128)(2,1)S(1)}, u32[]{:S(2)}, u32[]{:S(2)}) collective-permute-start(bf16[4,152,128]{2,1,0:T(8,128)(2,1)S(1)} %collective-permute-done.7.late_eb_ref), channel_id=1, source_target_pairs={{0,2},{2,0},{4,6},{6,4},{8,10},{10,8},{12,14},{14,12},{16,18},{18,... | collective-permute-start | bytes 466952 | tf_op jit(solution)/shard_map/ppermute | solution.py:555
  25.1 6.1 %copy-start = (bf16[128,128]{1,0:T(8,128)(2,1)S(1)}, bf16[128,128]{1,0:T(8,128)(2,1)}, u32[]{:S(2)}) copy-start(bf16[128,128]{1,0:T(8,128)(2,1)} %k_ref.3) | copy-start | bytes 98308
  25.1 6.1 %copy-start.1 = (bf16[128,128]{1,0:T(8,128)(2,1)S(1)}, bf16[128,128]{1,0:T(8,128)(2,1)}, u32[]{:S(2)}) copy-start(bf16[128,128]{1,0:T(8,128)(2,1)} %v_ref.3) | copy-start | bytes 98308
  27.6 3.6 %collective-permute-start.9 = (f32[8,128]{1,0:T(8,128)S(1)}, f32[8,128]{1,0:T(8,128)S(1)}, u32[]{:S(2)}, u32[]{:S(2)}) collective-permute-start(f32[8,128]{1,0:T(8,128)S(1)} %get-tuple-element.38.sums_a_ref), channel_id=1, source_target_pairs={{0,1},{1,0},{2,3},{3,2},{4,5},{5,4},{6,7},{7,6},{8,9},{9,8},{10,11... | collective-permute-start | bytes 12296 | tf_op jit(solution)/shard_map/ppermute | solution.py:555
  32.5 1.9 %collective-permute-start.17 = (f32[520,128]{1,0:T(8,128)S(1)}, f32[520,128]{1,0:T(8,128)S(1)}, u32[]{:S(2)}, u32[]{:S(2)}) collective-permute-start(f32[520,128]{1,0:T(8,128)S(1)} %get-tuple-element.51), channel_id=1, source_target_pairs={{0,2},{2,0},{4,6},{6,4},{8,10},{10,8},{12,14},{14,12},{16,18},{18,... | collective-permute-start | bytes 798728 | tf_op jit(solution)/shard_map/ppermute | solution.py:555
  33.9 2.9 %collective-permute-start.10 = (f32[520,128]{1,0:T(8,128)S(1)}, f32[520,128]{1,0:T(8,128)S(1)}, u32[]{:S(2)}, u32[]{:S(2)}) collective-permute-start(f32[520,128]{1,0:T(8,128)S(1)} %get-tuple-element.49), channel_id=1, source_target_pairs={{0,2},{2,0},{4,6},{6,4},{8,10},{10,8},{12,14},{14,12},{16,18},{18,... | collective-permute-start | bytes 798728 | tf_op jit(solution)/shard_map/ppermute | solution.py:555
  34.4 6.1 %collective-permute-start.18 = (f32[264,128]{1,0:T(8,128)S(1)}, f32[264,128]{1,0:T(8,128)S(1)}, u32[]{:S(2)}, u32[]{:S(2)}) collective-permute-start(f32[264,128]{1,0:T(8,128)S(1)} %slice.102), channel_id=1, source_target_pairs={{0,8},{2,10},{4,12},{6,14},{8,0},{10,2},{12,4},{14,6},{16,24},{18,... | collective-permute-start | bytes 405512 | tf_op jit(solution)/shard_map/ppermute | solution.py:555
  36.8 6.6 %collective-permute-start.11 = (f32[264,128]{1,0:T(8,128)S(1)}, f32[264,128]{1,0:T(8,128)S(1)}, u32[]{:S(2)}, u32[]{:S(2)}) collective-permute-start(f32[264,128]{1,0:T(8,128)S(1)} %slice.93), channel_id=1, source_target_pairs={{0,4},{2,6},{4,0},{6,2},{8,12},{10,14},{12,8},{14,10},{16,20},{18,... | collective-permute-start | bytes 405512 | tf_op jit(solution)/shard_map/ppermute | solution.py:555
  40.5 5.1 %collective-permute-start.19 = (f32[136,128]{1,0:T(8,128)S(1)}, f32[136,128]{1,0:T(8,128)S(1)}, u32[]{:S(2)}, u32[]{:S(2)}) collective-permute-start(f32[136,128]{1,0:T(8,128)S(1)} %pad_maximum_fusion.7), channel_id=1, source_target_pairs={{0,4},{2,6},{4,0},{6,2},{8,12},{10,14},{12,8},{14,10},{16,20},{18,... | collective-permute-start | bytes 208904 | tf_op jit(solution)/shard_map/ppermute | solution.py:555
  43.4 7.9 %collective-permute-start.12 = (f32[136,128]{1,0:T(8,128)S(1)}, f32[136,128]{1,0:T(8,128)S(1)}, u32[]{:S(2)}, u32[]{:S(2)}) collective-permute-start(f32[136,128]{1,0:T(8,128)S(1)} %pad_maximum_fusion.8), channel_id=1, source_target_pairs={{0,8},{2,10},{4,12},{6,14},{8,0},{10,2},{12,4},{14,6},{16,24},{18,... | collective-permute-start | bytes 208904 | tf_op jit(solution)/shard_map/ppermute | solution.py:555
  45.7 10.1 %collective-permute-start.20 = (f32[136,128]{1,0:T(8,128)S(1)}, f32[136,128]{1,0:T(8,128)S(1)}, u32[]{:S(2)}, u32[]{:S(2)}) collective-permute-start(f32[136,128]{1,0:T(8,128)S(1)} %pad_maximum_fusion.10), channel_id=1, source_target_pairs={{0,16},{2,18},{4,20},{6,22},{8,24},{10,26},{12,28},{14,30},{16,0},... | collective-permute-start | bytes 208904 | tf_op jit(solution)/shard_map/ppermute | solution.py:555
  51.4 6.2 %collective-permute-start.13 = (f32[136,128]{1,0:T(8,128)S(1)}, f32[136,128]{1,0:T(8,128)S(1)}, u32[]{:S(2)}, u32[]{:S(2)}) collective-permute-start(f32[136,128]{1,0:T(8,128)S(1)} %pad_maximum_fusion.9), channel_id=1, source_target_pairs={{0,16},{2,18},{4,20},{6,22},{8,24},{10,26},{12,28},{14,30},{16,0},... | collective-permute-start | bytes 208904 | tf_op jit(solution)/shard_map/ppermute | solution.py:555
  55.8 4.3 %collective-permute-start.21 = (f32[128,128]{1,0:T(8,128)S(1)}, f32[128,128]{1,0:T(8,128)S(1)}, u32[]{:S(2)}, u32[]{:S(2)}) collective-permute-start(f32[128,128]{1,0:T(8,128)S(1)} %slice.109), channel_id=1, source_target_pairs={{0,4},{2,6},{4,0},{6,2},{8,12},{10,14},{12,8},{14,10},{16,20},{18,... | collective-permute-start | bytes 196616 | tf_op jit(solution)/shard_map/ppermute | solution.py:555
  57.6 4.3 %collective-permute-start.14 = (f32[128,128]{1,0:T(8,128)S(1)}, f32[128,128]{1,0:T(8,128)S(1)}, u32[]{:S(2)}, u32[]{:S(2)}) collective-permute-start(f32[128,128]{1,0:T(8,128)S(1)} %slice.100), channel_id=1, source_target_pairs={{0,8},{2,10},{4,12},{6,14},{8,0},{10,2},{12,4},{14,6},{16,24},{18,... | collective-permute-start | bytes 196616 | tf_op jit(solution)/shard_map/ppermute | solution.py:555
  60.2 5.0 %collective-permute-start.22 = (f32[256,128]{1,0:T(8,128)S(1)}, f32[256,128]{1,0:T(8,128)S(1)}, u32[]{:S(2)}, u32[]{:S(2)}) collective-permute-start(f32[256,128]{1,0:T(8,128)S(1)} %pad_maximum_fusion.5), channel_id=1, source_target_pairs={{0,8},{2,10},{4,12},{6,14},{8,0},{10,2},{12,4},{14,6},{16,24},{18,... | collective-permute-start | bytes 393224 | tf_op jit(solution)/shard_map/ppermute | solution.py:555
  61.9 5.0 %collective-permute-start.15 = (f32[256,128]{1,0:T(8,128)S(1)}, f32[256,128]{1,0:T(8,128)S(1)}, u32[]{:S(2)}, u32[]{:S(2)}) collective-permute-start(f32[256,128]{1,0:T(8,128)S(1)} %pad_maximum_fusion.4), channel_id=1, source_target_pairs={{0,4},{2,6},{4,0},{6,2},{8,12},{10,14},{12,8},{14,10},{16,20},{18,... | collective-permute-start | bytes 393224 | tf_op jit(solution)/shard_map/ppermute | solution.py:555
  65.2 1.8 %collective-permute-start.23 = (f32[512,128]{1,0:T(8,128)S(1)}, f32[512,128]{1,0:T(8,128)S(1)}, u32[]{:S(2)}, u32[]{:S(2)}) collective-permute-start(f32[512,128]{1,0:T(8,128)S(1)} %pad_maximum_fusion.1.refs_3_), channel_id=1, source_target_pairs={{0,2},{2,0},{4,6},{6,4},{8,10},{10,8},{12,14},{14,12},{16,18},{18,... | collective-permute-start | bytes 786440 | tf_op jit(solution)/shard_map/ppermute | solution.py:555
  67.0 1.6 %collective-permute-start.16 = (f32[512,128]{1,0:T(8,128)S(1)}, f32[512,128]{1,0:T(8,128)S(1)}, u32[]{:S(2)}, u32[]{:S(2)}) collective-permute-start(f32[512,128]{1,0:T(8,128)S(1)} %pad_maximum_fusion.refs_0_), channel_id=1, source_target_pairs={{0,2},{2,0},{4,6},{6,4},{8,10},{10,8},{12,14},{14,12},{16,18},{18,... | collective-permute-start | bytes 786440 | tf_op jit(solution)/shard_map/ppermute | solution.py:555
